TPU v7x, 32 devices: a whole 2x2x4 slice. The times are simulated.
32 devices in a mesh: group: 8 (over z, x), slot: 4 (over y, core).
Axes of the slice: x: 2, y: 2, z: 4, core: 2. Of those that a mesh axis runs over, the one named last changes fastest.
Arguments:
- rows_in: bfloat16 [16384, 768], P(('group', 'slot')), may hold values from -6 to 6
- cotangent: bfloat16 [16384, 2048], P(('group', 'slot')), may hold values from -6 to 6
- gate_prob: float32 [16384], P(('group', 'slot')), may hold values from 0.05 to 0.5
- row_counts: int32 [32], P(('group', 'slot')), may hold values from 1 to 512
- old_place: int32 [32, 1], replicated, may hold values from 0 to 7
- new_place: int32 [32, 1], replicated, may hold values from 0 to 7
- rows_next: bfloat16 [16384, 768], P(('group', 'slot')), may hold values from -6 to 6
- master: float32 [8, 768, 2048], P(None, 'slot', 'group'), may hold values from -0.21875 to 0.21875
- moment_one: bfloat16 [8, 768, 2048], P(None, 'slot', 'group'), may hold values from -18 to 18
- moment_two: bfloat16 [8, 768, 2048], P(None, 'slot', 'group'), may hold values from 0.049804688 to 2
Outputs:
- input_grad: bfloat16 [16384, 768], P(('group', 'slot'))
- gate_grad: float32 [16384], P(('group', 'slot'))
- new_master: float32 [8, 768, 2048], P(None, 'slot', 'group')
- new_first: bfloat16 [8, 768, 2048], P(None, 'slot', 'group')
- new_second: bfloat16 [8, 768, 2048], P(None, 'slot', 'group')
- next_out: bfloat16 [16384, 2048], P(('group', 'slot'))
Inputs may be any that keep to these rules, and one draw needn't show every extreme that they name: `old_place`: every one of the 8 experts is held by at least one of the 32 slots. `new_place`: every one of the 8 experts is listed for at least one of the 32 slots.
All inputs are finite; a program needn't handle non-finite values.
Results may differ from a plain program's by a relative error of at most 0.004.
The roundings to bfloat16 on the way count: a program that leaves them out, or rounds other values in their place, can miss the bound.
Values may be sent and summed in bfloat16 or wider, within the bound.
No kernel may reach another device: no remote copies, remote signals or barrier semaphores. Data moves between devices by JAX's collectives and lax.ppermute only.
A program may use at most 128 MiB of HBM per device.

v0:
```python
import jax
import jax.numpy as jnp
from jax import lax
from jax.sharding import PartitionSpec as P

beta_one = 0.9
beta_two = 0.999
adam_eps = 1e-08
learn_rate = 0.006
fix_one = 0.9999734386011124
fix_two = 0.0952078528862904


def to_slots(shard_in, expert_of, slot_count, group_count):
    part_rows = shard_in.shape[1]
    part_cols = shard_in.shape[2]
    picked = shard_in[expert_of].astype(jnp.bfloat16)
    picked = picked.reshape(group_count, slot_count, part_rows, part_cols)
    buffer = jnp.transpose(picked, (1, 2, 0, 3))
    arrived = lax.all_to_all(
        lax.all_to_all(buffer, "group", split_axis=2, concat_axis=2, tiled=True),
        "slot",
        split_axis=0,
        concat_axis=0,
        tiled=True,
    )
    return arrived.reshape(slot_count * part_rows, group_count * part_cols)


def shards(
    rows_in,
    cotangent,
    gate_prob,
    row_counts,
    old_place,
    new_place,
    rows_next,
    master,
    moment_one,
    moment_two,
):
    slot_count = lax.axis_size("slot")
    group_count = lax.axis_size("group")
    row_count = rows_in.shape[0]
    part_rows = master.shape[1]
    part_cols = master.shape[2]
    expert_of = old_place[:, 0]
    weight = to_slots(master, expert_of, slot_count, group_count)
    live_rows = (jnp.arange(row_count, dtype=jnp.int32) < row_counts[0])[:, None]
    masked_in = jnp.where(live_rows, rows_in, jnp.zeros_like(rows_in))
    masked_out = jnp.where(live_rows, cotangent, jnp.zeros_like(cotangent))
    back_prod = lax.dot_general(
        masked_out, weight, (((1,), (1,)), ((), ())), preferred_element_type=jnp.float32
    )
    input_grad = (gate_prob[:, None] * back_prod).astype(jnp.bfloat16)
    forward_out = jnp.dot(masked_in, weight, preferred_element_type=jnp.float32)
    gate_grad = jnp.sum(masked_out.astype(jnp.float32) * forward_out, axis=1)
    scaled_out = (gate_prob[:, None] * masked_out.astype(jnp.float32)).astype(jnp.bfloat16)
    expert_ids = jnp.arange(master.shape[0], dtype=jnp.int32)
    owner_map = (
        expert_of.reshape(group_count, slot_count)[None, :, :] == expert_ids[:, None, None]
    ).astype(jnp.bfloat16)
    slot_grad = lax.dot_general(
        masked_in, scaled_out, (((0,), (0,)), ((), ())), preferred_element_type=jnp.float32
    ).astype(jnp.bfloat16)
    buffer = slot_grad.reshape(slot_count, part_rows, group_count, part_cols)
    arrived = lax.all_to_all(
        lax.all_to_all(buffer, "group", split_axis=2, concat_axis=2, tiled=True),
        "slot",
        split_axis=0,
        concat_axis=0,
        tiled=True,
    )
    grad_sum = jnp.einsum("egs,sfgd->efd", owner_map, arrived, preferred_element_type=jnp.float32)
    first_full = beta_one * moment_one.astype(jnp.float32) + (1.0 - beta_one) * grad_sum
    second_full = beta_two * moment_two.astype(jnp.float32) + (1.0 - beta_two) * grad_sum * grad_sum
    new_master = master - learn_rate * (first_full / fix_one) / (
        jnp.sqrt(second_full / fix_two) + adam_eps
    )
    weight_next = to_slots(new_master, new_place[:, 0], slot_count, group_count)
    next_out = jnp.dot(rows_next, weight_next, preferred_element_type=jnp.float32).astype(
        jnp.bfloat16
    )
    return (
        input_grad,
        gate_grad,
        new_master,
        first_full.astype(jnp.bfloat16),
        second_full.astype(jnp.bfloat16),
        next_out,
    )


def solution(mesh):
    in_specs = (
        P(("group", "slot"), None),
        P(("group", "slot"), None),
        P(("group", "slot")),
        P(("group", "slot")),
        P(),
        P(),
        P(("group", "slot"), None),
        P(None, "slot", "group"),
        P(None, "slot", "group"),
        P(None, "slot", "group"),
    )
    out_specs = (
        P(("group", "slot"), None),
        P(("group", "slot")),
        P(None, "slot", "group"),
        P(None, "slot", "group"),
        P(None, "slot", "group"),
        P(("group", "slot"), None),
    )
    return jax.shard_map(shards, mesh=mesh, in_specs=in_specs, out_specs=out_specs, check_vma=False)
```

profile of v0, /device:TPU:0, one launch (start us, length us, event | category | flops | bytes accessed | tf_op | source)
XLA Modules:
  0.0 374.0 jit_solution(5071903789079228209)
XLA Ops:
  0.6 0.0 copy-start
  1.4 3.9 %convolution_convert_fusion = bf16[768,2048]{1,0:T(8,128)(2,1)S(1)} fusion(f32[512]{0:T(512)} %param.12, bf16[512,768]{1,0:T(8,128)(2,1)} %param.10, pred[512]{0:T(512)(128)(4,1)S(1)} %iota_compare_fusion.1, bf16[512,2048]{1,0:T(8,128)(2,1)} %param.11), kind=kOutput, calls=%fused_computation.6 | convolution fusion | flops 1616773120 | bytes 6031872 | tf_op jit(solution)/shard_map/dot_general | solution.py:63
  5.3 1.1 copy.69
  6.4 2.4 copy.55
  8.8 77.8 %all_to_all.30 = bf16[4,192,8,256]{3,0,1,2:T(4,128)(2,1)S(1)} all-to-all(bf16[4,192,8,256]{3,0,1,2:T(4,128)(2,1)S(1)} %copy.55), channel_id=1, replica_groups=mesh['group'=8,'slot'=4] {'group'}, dimensions={2} | all-to-all | bytes 6291456 | tf_op jit(solution)/shard_map/all_to_all | solution.py:68
  86.6 3.4 copy.56
  90.0 0.0 copy-start.4
  90.0 0.0 copy-start.2
  90.0 4.8 %all-to-all-start.3 = ((bf16[4,192,8,256]{3,2,1,0:T(8,128)(2,1)}), bf16[4,192,8,256]{3,2,1,0:T(8,128)(2,1)}, u32[]{:S(2)}, u32[]{:S(2)}) async-start(bf16[4,192,8,256]{3,2,1,0:T(8,128)(2,1)} %copy.56), calls=%async_computation.3 | async-start | bytes 6291456 | tf_op jit(solution)/shard_map/all_to_all | solution.py:67
  94.8 0.5 broadcast.35
  95.3 0.0 copy-done.4
  95.3 0.7 fusion.17
  96.0 0.0 copy-done.2
  96.0 2.5 gather_fusion
  98.5 33.2 %all-to-all-done.3 = bf16[4,192,8,256]{3,2,1,0:T(8,128)(2,1)} async-done(((bf16[4,192,8,256]{3,2,1,0:T(8,128)(2,1)}), bf16[4,192,8,256]{3,2,1,0:T(8,128)(2,1)}, u32[]{:S(2)}, u32[]{:S(2)}) %all-to-all-start.3) | async-done | bytes 3145760 | tf_op jit(solution)/shard_map/all_to_all | solution.py:67
  131.8 0.0 copy-start.8
  131.8 4.8 %all-to-all-start = ((bf16[4,192,8,256]{3,1,0,2:T(8,128)(2,1)}), bf16[4,192,8,256]{3,1,0,2:T(8,128)(2,1)}, u32[]{:S(2)}, u32[]{:S(2)}) async-start(bf16[4,192,8,256]{3,1,0,2:T(8,128)(2,1)} %bitcast.52), calls=%async_computation | async-start | bytes 6291456 | tf_op jit(solution)/shard_map/all_to_all | solution.py:21
  136.5 0.1 eq.15
  136.6 0.1 copy.54
  136.7 0.0 copy-done.8
  136.7 5.9 %fusion.8 = (bf16[8,192,256]{2,0,1:T(8,128)(2,1)}, f32[8,192,256]{2,0,1:T(8,128)S(1)}, bf16[8,192,256]{2,0,1:T(8,128)(2,1)S(1)}) fusion(bf16[8,192,256]{2,1,0:T(8,128)(2,1)} %param.19, bf16[8,192,256]{2,1,0:T(8,128)(2,1)} %param.18, f32[8,192,256]{2,1,0:T(8,128)S(1)} %copy-done.2, bf16[4,192,8,256]{3,2,1,0:T(8,128)(2,1)} %all-to-all-done.3, ...), kind=kOutput, calls=%fused_computation.18 | convolution fusion | flops 31457536 | bytes 9437312 | tf_op jit(solution)/shard_map/egs,sfgd->efd/dot_general | solution.py:74
  142.6 0.5 copy.63
  143.1 0.0 copy-start.1
  143.1 2.5 gather_fusion.1
  145.6 0.0 copy-done.1
  145.6 61.4 %all-to-all-done = bf16[4,192,8,256]{3,1,0,2:T(8,128)(2,1)} async-done(((bf16[4,192,8,256]{3,1,0,2:T(8,128)(2,1)}), bf16[4,192,8,256]{3,1,0,2:T(8,128)(2,1)}, u32[]{:S(2)}, u32[]{:S(2)}) %all-to-all-start) | async-done | bytes 3145760 | tf_op jit(solution)/shard_map/all_to_all | solution.py:21
  207.0 4.4 %all-to-all-start.4 = ((bf16[4,192,8,256]{3,1,0,2:T(8,128)(2,1)}), bf16[4,192,8,256]{3,1,0,2:T(8,128)(2,1)}, u32[]{:S(2)}, u32[]{:S(2)}) async-start(bf16[4,192,8,256]{3,1,0,2:T(8,128)(2,1)} %bitcast.53), calls=%async_computation.4 | async-start | bytes 6291456 | tf_op jit(solution)/shard_map/all_to_all | solution.py:21
  211.5 3.9 %copy.51 = bf16[4,192,8,256]{3,1,2,0:T(8,128)(2,1)} copy(bf16[4,192,8,256]{3,1,0,2:T(8,128)(2,1)} %all-to-all-done) | data formatting | bytes 6291456 | tf_op jit(solution)/shard_map/all_to_all | solution.py:21
  215.4 66.2 %all-to-all-done.4 = bf16[4,192,8,256]{3,1,0,2:T(8,128)(2,1)} async-done(((bf16[4,192,8,256]{3,1,0,2:T(8,128)(2,1)}), bf16[4,192,8,256]{3,1,0,2:T(8,128)(2,1)}, u32[]{:S(2)}, u32[]{:S(2)}) %all-to-all-start.4) | async-done | bytes 3145760 | tf_op jit(solution)/shard_map/all_to_all | solution.py:21
  281.7 4.7 %all-to-all-start.1 = ((bf16[4,192,8,256]{3,1,2,0:T(8,128)(2,1)}), bf16[4,192,8,256]{3,1,2,0:T(8,128)(2,1)}, u32[]{:S(2)}, u32[]{:S(2)}) async-start(bf16[4,192,8,256]{3,1,2,0:T(8,128)(2,1)} %copy.51), calls=%async_computation.1 | async-start | bytes 6291456 | tf_op jit(solution)/shard_map/all_to_all | solution.py:20
  286.3 3.9 %copy.61 = bf16[4,192,8,256]{3,1,2,0:T(8,128)(2,1)} copy(bf16[4,192,8,256]{3,1,0,2:T(8,128)(2,1)} %all-to-all-done.4) | data formatting | bytes 6291456 | tf_op jit(solution)/shard_map/all_to_all | solution.py:21
  290.2 33.1 %all-to-all-done.1 = bf16[4,192,8,256]{3,1,2,0:T(8,128)(2,1)} async-done(((bf16[4,192,8,256]{3,1,2,0:T(8,128)(2,1)}), bf16[4,192,8,256]{3,1,2,0:T(8,128)(2,1)}, u32[]{:S(2)}, u32[]{:S(2)}) %all-to-all-start.1) | async-done | bytes 3145760 | tf_op jit(solution)/shard_map/all_to_all | solution.py:20
  323.3 4.7 %all-to-all-start.5 = ((bf16[4,192,8,256]{3,1,2,0:T(8,128)(2,1)}), bf16[4,192,8,256]{3,1,2,0:T(8,128)(2,1)}, u32[]{:S(2)}, u32[]{:S(2)}) async-start(bf16[4,192,8,256]{3,1,2,0:T(8,128)(2,1)} %copy.61), calls=%async_computation.5 | async-start | bytes 6291456 | tf_op jit(solution)/shard_map/all_to_all | solution.py:20
  328.0 3.7 copy.52
  331.7 0.0 copy-start.3
  331.7 1.1 copy.68
  332.8 0.0 copy-start.5
  332.8 0.0 copy-start.7
  332.8 0.0 copy-done.3
  332.8 1.0 copy.65
  333.8 1.0 copy.64
  334.9 0.0 copy-done.5
  334.9 0.0 copy-done.7
  334.9 0.0 copy-start.6
  334.9 2.7 multiply_convert_fusion
  337.6 0.0 copy-done.6
  337.6 2.5 fusion
  340.1 24.8 %all-to-all-done.5 = bf16[4,192,8,256]{3,1,2,0:T(8,128)(2,1)} async-done(((bf16[4,192,8,256]{3,1,2,0:T(8,128)(2,1)}), bf16[4,192,8,256]{3,1,2,0:T(8,128)(2,1)}, u32[]{:S(2)}, u32[]{:S(2)}) %all-to-all-start.5) | async-done | bytes 3145760 | tf_op jit(solution)/shard_map/all_to_all | solution.py:20
  364.9 3.7 copy.62
  368.6 1.1 copy.70
  369.7 0.0 copy-done
  369.7 1.9 fusion.2
  371.6 2.4 copy.66
  (4 shorter events, 0.0 us)
Async XLA Ops:
  0.6 369.1 %copy-start = (bf16[512,768]{1,0:T(8,128)(2,1)S(1)}, bf16[512,768]{1,0:T(8,128)(2,1)}, u32[]{:S(2)}) copy-start(bf16[512,768]{1,0:T(8,128)(2,1)} %param.16) | copy-start | bytes 2359300
  90.0 5.3 %copy-start.4 = (s32[32,1]{0,1:T(1,128)S(1)}, s32[32,1]{0,1:T(1,128)}, u32[]{:S(2)}) copy-start(s32[32,1]{0,1:T(1,128)} %param.14) | copy-start | bytes 388
  90.0 6.0 %copy-start.2 = (f32[8,192,256]{2,1,0:T(8,128)S(1)}, f32[8,192,256]{2,1,0:T(8,128)}, u32[]{:S(2)}) copy-start(f32[8,192,256]{2,1,0:T(8,128)} %param.17) | copy-start | bytes 4718596
  90.0 41.8 %all-to-all-start.3 = ((bf16[4,192,8,256]{3,2,1,0:T(8,128)(2,1)}), bf16[4,192,8,256]{3,2,1,0:T(8,128)(2,1)}, u32[]{:S(2)}, u32[]{:S(2)}) async-start(bf16[4,192,8,256]{3,2,1,0:T(8,128)(2,1)} %copy.56), calls=%async_computation.3 | async-start | bytes 6291456 | tf_op jit(solution)/shard_map/all_to_all | solution.py:67
  131.8 4.9 %copy-start.8 = (s32[32,1]{0,1:T(1,128)S(1)}, s32[32,1]{0,1:T(1,128)}, u32[]{:S(2)}) copy-start(s32[32,1]{0,1:T(1,128)} %param.15) | copy-start | bytes 388
  131.8 75.3 %all-to-all-start = ((bf16[4,192,8,256]{3,1,0,2:T(8,128)(2,1)}), bf16[4,192,8,256]{3,1,0,2:T(8,128)(2,1)}, u32[]{:S(2)}, u32[]{:S(2)}) async-start(bf16[4,192,8,256]{3,1,0,2:T(8,128)(2,1)} %bitcast.52), calls=%async_computation | async-start | bytes 6291456 | tf_op jit(solution)/shard_map/all_to_all | solution.py:21
  143.1 2.5 copy-start.1
  207.0 74.6 %all-to-all-start.4 = ((bf16[4,192,8,256]{3,1,0,2:T(8,128)(2,1)}), bf16[4,192,8,256]{3,1,0,2:T(8,128)(2,1)}, u32[]{:S(2)}, u32[]{:S(2)}) async-start(bf16[4,192,8,256]{3,1,0,2:T(8,128)(2,1)} %bitcast.53), calls=%async_computation.4 | async-start | bytes 6291456 | tf_op jit(solution)/shard_map/all_to_all | solution.py:21
  281.7 41.6 %all-to-all-start.1 = ((bf16[4,192,8,256]{3,1,2,0:T(8,128)(2,1)}), bf16[4,192,8,256]{3,1,2,0:T(8,128)(2,1)}, u32[]{:S(2)}, u32[]{:S(2)}) async-start(bf16[4,192,8,256]{3,1,2,0:T(8,128)(2,1)} %copy.51), calls=%async_computation.1 | async-start | bytes 6291456 | tf_op jit(solution)/shard_map/all_to_all | solution.py:20
  323.3 41.6 %all-to-all-start.5 = ((bf16[4,192,8,256]{3,1,2,0:T(8,128)(2,1)}), bf16[4,192,8,256]{3,1,2,0:T(8,128)(2,1)}, u32[]{:S(2)}, u32[]{:S(2)}) async-start(bf16[4,192,8,256]{3,1,2,0:T(8,128)(2,1)} %copy.61), calls=%async_computation.5 | async-start | bytes 6291456 | tf_op jit(solution)/shard_map/all_to_all | solution.py:20
  331.7 1.1 copy-start.3
  332.8 2.1 copy-start.5
  332.8 2.1 copy-start.7
  334.9 2.7 copy-start.6
where the time goes:
time: 375 us; the launch traced here: 374 us
  waiting for transfers between devices  219 us (58%)
  blocking collectives  77.8 us (21%)
  local copies, waits for them, and re-layouts  35 us (9%)
  starting transfers between devices  23.3 us (6%)
  matrix products  16.9 us (5%)
    all_to_all x2, waiting for transfers between devices, to_slots(): lax.all_to_all(buffer, 'group', split_axis=2, concat_axis=2, tiled=True)  128 us
    all_to_all x1, blocking collectives, shards(): lax.all_to_all(buffer, 'group', split_axis=2, concat_axis=2, tiled=True)  77.8 us
    all_to_all x2, waiting for transfers between devices, to_slots(): lax.all_to_all(lax.all_to_all(buffer, 'group', split_axis=2, concat_axis=...  57.9 us
    all_to_all x1, waiting for transfers between devices, shards(): lax.all_to_all(lax.all_to_all(buffer, 'group', split_axis=2, concat_axis=...  33.2 us
    all_to_all x2, starting transfers between devices, to_slots(): lax.all_to_all(lax.all_to_all(buffer, 'group', split_axis=2, concat_axis=...  9.33 us
    all_to_all x2, starting transfers between devices, to_slots(): lax.all_to_all(buffer, 'group', split_axis=2, concat_axis=2, tiled=True)  9.2 us
    unnamed x26, local copies, waits for them, and re-layouts  8.78 us
    all_to_all x2, local copies, waits for them, and re-layouts, to_slots(): lax.all_to_all(buffer, 'group', split_axis=2, concat_axis=2, tiled=True)  7.8 us
  transfers between devices with their start and end apart: 5, of which 5 were waited for; matrix products, arithmetic and copies ran while one was open for 9% of the time, Pallas kernels for 0%

commit v1 on v0

v1 whole, which is shorter than its diff:
```python
import functools

import jax
import jax.numpy as jnp
from jax import lax
from jax.experimental import pallas as pl
from jax.experimental.pallas import tpu as pltpu
from jax.sharding import PartitionSpec as P

beta_one = 0.9
beta_two = 0.999
adam_eps = 1e-08
learn_rate = 0.006
fix_one = 0.9999734386011124
fix_two = 0.0952078528862904

BOTH = ("group", "slot")


def column_of(row):
    return jnp.transpose(jnp.broadcast_to(row, (8, row.shape[1])))[:, :1]


def slot_grad_kernel(count_ref, rows_ref, cot_ref, gate_ref, out_ref, turned):
    rows = rows_ref.shape[0]
    live = lax.broadcasted_iota(jnp.int32, (rows, 1), 0) < count_ref[0]

    @pl.when(pl.program_id(0) == 0)
    def _():
        kept = jnp.where(live, rows_ref[...].astype(jnp.float32), 0.0)
        turned[...] = jnp.transpose(kept).astype(jnp.bfloat16)

    scaled = column_of(gate_ref[...]) * cot_ref[...].astype(jnp.float32)
    scaled = jnp.where(live, scaled, 0.0).astype(jnp.bfloat16)
    out_ref[0] = jnp.dot(turned[...], scaled, preferred_element_type=jnp.float32).astype(
        jnp.bfloat16
    )


def slot_grads(row_counts, rows_in, cotangent, gate_row, group_count):
    rows, ff = rows_in.shape
    cols = cotangent.shape[1] // group_count
    return pl.pallas_call(
        slot_grad_kernel,
        name="slot_grads",
        out_shape=jax.ShapeDtypeStruct((group_count, ff, cols), jnp.bfloat16),
        grid_spec=pltpu.PrefetchScalarGridSpec(
            num_scalar_prefetch=1,
            grid=(group_count,),
            in_specs=[
                pl.BlockSpec((rows, ff), lambda g, c: (0, 0)),
                pl.BlockSpec((rows, cols), lambda g, c: (0, g)),
                pl.BlockSpec((1, rows), lambda g, c: (0, 0)),
            ],
            out_specs=pl.BlockSpec((1, ff, cols), lambda g, c: (g, 0, 0)),
            scratch_shapes=[pltpu.VMEM((ff, rows), jnp.bfloat16)],
        ),
        compiler_params=pltpu.CompilerParams(dimension_semantics=("arbitrary",)),
    )(row_counts, rows_in, cotangent, gate_row)


def update_kernel(
    old_ref, new_ref, grads_ref, master_ref, one_ref, two_ref,
    master_out, one_out, two_out, send_ref, total, fresh,
):
    slots = grads_ref.shape[0]
    total[...] = jnp.zeros_like(total)

    def add(s, _):
        e = old_ref[s]
        total[e] = total[e] + grads_ref[s].astype(jnp.float32)
        return 0

    lax.fori_loop(0, slots, add, 0)
    grad = total[...]
    first = beta_one * one_ref[...].astype(jnp.float32) + (1.0 - beta_one) * grad
    second = beta_two * two_ref[...].astype(jnp.float32) + (1.0 - beta_two) * grad * grad
    master = master_ref[...] - learn_rate * (first / fix_one) / (
        jnp.sqrt(second / fix_two) + adam_eps
    )
    master_out[...] = master
    one_out[...] = first.astype(jnp.bfloat16)
    two_out[...] = second.astype(jnp.bfloat16)
    fresh[...] = master.astype(jnp.bfloat16)

    def pick(s, _):
        send_ref[s] = fresh[new_ref[s]]
        return 0

    lax.fori_loop(0, slots, pick, 0)


def update(old, new, grads, master, one, two):
    slots, rows, cols = grads.shape
    experts = master.shape[0]
    step = 16
    state = pl.BlockSpec((experts, step, cols), lambda i, a, b: (0, i, 0))
    wide = pl.BlockSpec((slots, step, cols), lambda i, a, b: (0, i, 0))
    return pl.pallas_call(
        update_kernel,
        name="update",
        out_shape=(
            jax.ShapeDtypeStruct(master.shape, jnp.float32),
            jax.ShapeDtypeStruct(master.shape, jnp.bfloat16),
            jax.ShapeDtypeStruct(master.shape, jnp.bfloat16),
            jax.ShapeDtypeStruct(grads.shape, jnp.bfloat16),
        ),
        grid_spec=pltpu.PrefetchScalarGridSpec(
            num_scalar_prefetch=2,
            grid=(rows // step,),
            in_specs=[wide, state, state, state],
            out_specs=[state, state, state, wide],
            scratch_shapes=[
                pltpu.VMEM((experts, step, cols), jnp.float32),
                pltpu.VMEM((experts, step, cols), jnp.bfloat16),
            ],
        ),
        compiler_params=pltpu.CompilerParams(dimension_semantics=("arbitrary",)),
    )(old, new, grads, master, one, two)


def next_kernel(rows_ref, weight_ref, out_ref):
    out_ref[...] = jnp.dot(
        rows_ref[...], weight_ref[0], preferred_element_type=jnp.float32
    ).astype(jnp.bfloat16)


def next_rows(rows_next, weight):
    groups, ff, cols = weight.shape
    rows = rows_next.shape[0]
    return pl.pallas_call(
        next_kernel,
        name="next_rows",
        out_shape=jax.ShapeDtypeStruct((rows, groups * cols), jnp.bfloat16),
        grid=(groups,),
        in_specs=[
            pl.BlockSpec((rows, ff), lambda g: (0, 0)),
            pl.BlockSpec((1, ff, cols), lambda g: (g, 0, 0)),
        ],
        out_specs=pl.BlockSpec((rows, cols), lambda g: (0, g)),
        compiler_params=pltpu.CompilerParams(dimension_semantics=("arbitrary",)),
    )(rows_next, weight)


def back_kernel(count_ref, rows_ref, cot_ref, gate_ref, weight_ref, grad_ref, gate_out, total):
    g = pl.program_id(0)
    rows = rows_ref.shape[0]
    part = lax.dot_general(
        cot_ref[...],
        weight_ref[0],
        (((1,), (1,)), ((), ())),
        preferred_element_type=jnp.float32,
    )

    @pl.when(g == 0)
    def _():
        total[...] = part

    @pl.when(g > 0)
    def _():
        total[...] += part

    @pl.when(g == pl.num_programs(0) - 1)
    def _():
        live = lax.broadcasted_iota(jnp.int32, (rows, 1), 0) < count_ref[0]
        back = jnp.where(live, total[...], 0.0)
        grad_ref[...] = (column_of(gate_ref[...]) * back).astype(jnp.bfloat16)
        summed = jnp.sum(rows_ref[...].astype(jnp.float32) * back, axis=1, keepdims=True)
        gate_out[...] = jnp.transpose(jnp.broadcast_to(summed, (rows, 128)))[:1]


def back(row_counts, rows_in, cotangent, gate_row, weight):
    groups, ff, cols = weight.shape
    rows = rows_in.shape[0]
    return pl.pallas_call(
        back_kernel,
        name="back",
        out_shape=(
            jax.ShapeDtypeStruct((rows, ff), jnp.bfloat16),
            jax.ShapeDtypeStruct((1, rows), jnp.float32),
        ),
        grid_spec=pltpu.PrefetchScalarGridSpec(
            num_scalar_prefetch=1,
            grid=(groups,),
            in_specs=[
                pl.BlockSpec((rows, ff), lambda g, c: (0, 0)),
                pl.BlockSpec((rows, cols), lambda g, c: (0, g)),
                pl.BlockSpec((1, rows), lambda g, c: (0, 0)),
                pl.BlockSpec((1, ff, cols), lambda g, c: (g, 0, 0)),
            ],
            out_specs=[
                pl.BlockSpec((rows, ff), lambda g, c: (0, 0)),
                pl.BlockSpec((1, rows), lambda g, c: (0, 0)),
            ],
            scratch_shapes=[pltpu.VMEM((rows, ff), jnp.float32)],
        ),
        compiler_params=pltpu.CompilerParams(dimension_semantics=("arbitrary",)),
    )(row_counts, rows_in, cotangent, gate_row, weight)


def exchange(blocks):
    return lax.all_to_all(blocks, BOTH, split_axis=0, concat_axis=0, tiled=True)


def shards(
    rows_in, cotangent, gate_prob, row_counts, old_place, new_place, rows_next,
    master, moment_one, moment_two,
):
    slot_count = lax.axis_size("slot")
    group_count = lax.axis_size("group")
    part_rows, part_cols = master.shape[1:]
    ff = slot_count * part_rows
    old, new = old_place[:, 0], new_place[:, 0]
    gate_row = gate_prob.reshape(1, -1)
    grads = slot_grads(row_counts, rows_in, cotangent, gate_row, group_count)
    arrived = exchange(grads.reshape(-1, part_rows, part_cols))
    held = exchange(master[old].astype(jnp.bfloat16))
    new_master, new_first, new_second, send = update(
        old, new, arrived, master, moment_one, moment_two
    )
    weight = held.reshape(group_count, ff, part_cols)
    input_grad, gate_grad = back(row_counts, rows_in, cotangent, gate_row, weight)
    weight_next = exchange(send).reshape(group_count, ff, part_cols)
    next_out = next_rows(rows_next, weight_next)
    return input_grad, gate_grad.reshape(-1), new_master, new_first, new_second, next_out


def solution(mesh):
    rows = P(BOTH, None)
    row = P(BOTH)
    state = P(None, "slot", "group")
    return jax.shard_map(
        shards,
        mesh=mesh,
        in_specs=(rows, rows, row, row, P(), P(), rows, state, state, state),
        out_specs=(rows, row, state, state, state, rows),
        check_vma=False,
    )
```

time: 375 us -> 252 us (0.67)
  blocking collectives: 77.8 us -> 0 us
  Pallas kernels: 0 us -> 37.9 us
  local copies, waits for them, and re-layouts: 35 us -> 4.3 us
  waiting for transfers between devices: 219 us -> 191 us
  matrix products: 16.9 us -> 0 us
  starting transfers between devices: 23.3 us -> 16.7 us
    all_to_all x1 -> x0, blocking collectives: 77.8 us -> none  [shards(): lax.all_to_all(buffer, 'group', split_axis=2, concat_axis=2, tiled=True)]
    pallas_call x0 -> x4, Pallas kernels: none -> 37.9 us  [the longest x1 12.7 us: update(): pl.pallas_call(update_kernel, name='update', out_shape=(jax.ShapeDtypeStr...]
    all_to_all x5 -> x3, waiting for transfers between devices: 219 us -> 191 us  [exchange(): return lax.all_to_all(blocks, BOTH, split_axis=0, concat_axis=0, tiled=True)]
    all_to_all x5 -> x0, local copies, waits for them, and re-layouts: 18.6 us -> none  [the longest x2 7.8 us: to_slots(): lax.all_to_all(buffer, 'group', split_axis=2, concat_axis=2, tiled=True)]
    dot_general x5 -> x0, matrix products: 16.9 us -> none  [the longest x1 5.9 us: shards(): jnp.einsum('egs,sfgd->efd', owner_map, arrived, preferred_element_type=jn...]
    unnamed x26 -> x6, local copies, waits for them, and re-layouts: 8.78 us -> 1.72 us
    all_to_all x5 -> x3, starting transfers between devices: 23.3 us -> 16.7 us  [exchange(): return lax.all_to_all(blocks, BOTH, split_axis=0, concat_axis=0, tiled=True)]
  transfers between devices with their start and end apart: 5 -> 3, of which waited for: 5 -> 3; matrix products, arithmetic and copies ran while one was open for 9% -> 1% of each run, Pallas kernels for 0% -> 9%
where the time goes in v1:
time: 252 us; the launch traced here: 251 us
  waiting for transfers between devices  191 us (76%)
  Pallas kernels  37.9 us (15%)
  starting transfers between devices  16.7 us (7%)
  local copies, waits for them, and re-layouts  4.3 us (2%)
    all_to_all x3, waiting for transfers between devices, exchange(): return lax.all_to_all(blocks, BOTH, split_axis=0, concat_axis=0, tiled=True)  191 us
    all_to_all x3, starting transfers between devices, exchange(): return lax.all_to_all(blocks, BOTH, split_axis=0, concat_axis=0, tiled=True)  16.7 us
    pallas_call x1, Pallas kernels, update(): pl.pallas_call(update_kernel, name='update', out_shape=(jax.ShapeDtypeStr...  12.7 us
    pallas_call x1, Pallas kernels, back(): pl.pallas_call(back_kernel, name='back', out_shape=(jax.ShapeDtypeStruct(...  8.92 us
    pallas_call x1, Pallas kernels, slot_grads(): pl.pallas_call(slot_grad_kernel, name='slot_grads', out_shape=jax.ShapeDt...  8.84 us
    pallas_call x1, Pallas kernels, next_rows(): pl.pallas_call(next_kernel, name='next_rows', out_shape=jax.ShapeDtypeStr...  7.45 us
  transfers between devices with their start and end apart: 3, of which 3 were waited for; matrix products, arithmetic and copies ran while one was open for 1% of the time, Pallas kernels for 9%

profile of v1, /device:TPU:0, one launch (start us, length us, event | category | flops | bytes accessed | tf_op | source)
XLA Modules:
  0.0 250.8 jit_solution(14940466941197251858)
XLA Ops:
  1.3 8.8 %slot_grads.1 = bf16[8,768,256]{2,1,0:T(8,128)(2,1)} custom-call(s32[1]{0:T(128)S(6)} %copy.16.count_ref, bf16[512,768]{1,0:T(8,128)(2,1)} %rows_ref.4, bf16[512,2048]{1,0:T(8,128)(2,1)} %cot_ref.3, f32[1,512]{1,0:T(1,128)} %bitcast.11), custom_call_target="tpu_custom_call" | custom-call | tf_op jit(solution)/shard_map/slot_grads/pallas_call | solution.py:43
  10.1 0.0 copy-start.2
  10.1 0.0 copy-start
  10.1 7.5 %all-to-all-start.1 = ((bf16[32,192,256]{2,1,0:T(8,128)(2,1)}), bf16[32,192,256]{2,1,0:T(8,128)(2,1)}, u32[]{:S(2)}, u32[]{:S(2)}) async-start(bf16[32,192,256]{2,1,0:T(8,128)(2,1)} %bitcast.10), calls=%async_computation.1 | async-start | bytes 6291456 | tf_op jit(solution)/shard_map/all_to_all | solution.py:202
  17.6 0.0 copy-done.2
  17.6 0.0 copy-done
  17.6 2.6 %gather_fusion = bf16[32,192,256]{2,1,0:T(8,128)(2,1)} fusion(f32[8,192,256]{2,1,0:T(8,128)S(1)} %copy-done, s32[1024]{0:T(1024)S(1)} %pad_clamp_fusion), kind=kCustom, calls=%fused_computation | custom fusion | bytes 6291584 | tf_op jit(solution)/shard_map/gather | solution.py:217
  20.2 69.0 %all-to-all-done.1.grads_ref = bf16[32,192,256]{2,1,0:T(8,128)(2,1)} async-done(((bf16[32,192,256]{2,1,0:T(8,128)(2,1)}), bf16[32,192,256]{2,1,0:T(8,128)(2,1)}, u32[]{:S(2)}, u32[]{:S(2)}) %all-to-all-start.1) | async-done | bytes 3145760 | tf_op jit(solution)/shard_map/all_to_all | solution.py:202
  89.2 4.6 %all-to-all-start = ((bf16[32,192,256]{2,1,0:T(8,128)(2,1)}), bf16[32,192,256]{2,1,0:T(8,128)(2,1)S(1)}, u32[]{:S(2)}, u32[]{:S(2)}) async-start(bf16[32,192,256]{2,1,0:T(8,128)(2,1)} %gather_fusion), calls=%async_computation | async-start | bytes 6291456 | tf_op jit(solution)/shard_map/all_to_all | solution.py:202
  93.7 12.7 %update.1 = (f32[8,192,256]{2,1,0:T(8,128)}, bf16[8,192,256]{2,1,0:T(8,128)(2,1)}, bf16[8,192,256]{2,1,0:T(8,128)(2,1)}, bf16[32,192,256]{2,1,0:T(8,128)(2,1)}) custom-call(s32[32]{0:T(128)} %bitcast.13, s32[32]{0:T(128)} %bitcast.14, bf16[32,192,256]{2,1,0:T(8,128)(2,1)} %all-to-all-done.1.grads_ref, f32[8,192,256]{2,1,0:T(8,128)} %master_ref.1, ...), custom_call_target="tpu_custom_call" | custom-call | tf_op jit(solution)/shard_map/update/pallas_call | solution.py:99
  106.4 58.9 %all-to-all-done = bf16[32,192,256]{2,1,0:T(8,128)(2,1)S(1)} async-done(((bf16[32,192,256]{2,1,0:T(8,128)(2,1)}), bf16[32,192,256]{2,1,0:T(8,128)(2,1)S(1)}, u32[]{:S(2)}, u32[]{:S(2)}) %all-to-all-start) | async-done | bytes 3145760 | tf_op jit(solution)/shard_map/all_to_all | solution.py:202
  165.4 0.0 copy-start.1
  165.4 1.7 copy-done.1
  167.1 4.7 %all-to-all-start.2 = ((bf16[32,192,256]{2,1,0:T(8,128)(2,1)}), bf16[32,192,256]{2,1,0:T(8,128)(2,1)}, u32[]{:S(2)}, u32[]{:S(2)}) async-start(bf16[32,192,256]{2,1,0:T(8,128)(2,1)} %get-tuple-element.17), calls=%async_computation.2 | async-start | bytes 6291456 | tf_op jit(solution)/shard_map/all_to_all | solution.py:202
  171.8 8.9 %back.1 = (bf16[512,768]{1,0:T(8,128)(2,1)}, f32[1,512]{1,0:T(1,128)}) custom-call(s32[1]{0:T(128)S(6)} %copy.16.count_ref, bf16[512,768]{1,0:T(8,128)(2,1)} %rows_ref.4, bf16[512,2048]{1,0:T(8,128)(2,1)} %cot_ref.3, f32[1,512]{1,0:T(1,128)} %bitcast.12, bf16[8,768,256]{2,1,0:T(8,128)(2,1)} %bitcast.9), custom_call_target="tpu_custom_call" | custom-call | tf_op jit(solution)/shard_map/back/pallas_call | solution.py:175
  180.7 62.7 %all-to-all-done.2 = bf16[32,192,256]{2,1,0:T(8,128)(2,1)} async-done(((bf16[32,192,256]{2,1,0:T(8,128)(2,1)}), bf16[32,192,256]{2,1,0:T(8,128)(2,1)}, u32[]{:S(2)}, u32[]{:S(2)}) %all-to-all-start.2) | async-done | bytes 3145760 | tf_op jit(solution)/shard_map/all_to_all | solution.py:202
  243.4 7.5 %next_rows.1 = bf16[512,2048]{1,0:T(8,128)(2,1)} custom-call(bf16[512,768]{1,0:T(8,128)(2,1)} %rows_ref.5, bf16[8,768,256]{2,1,0:T(8,128)(2,1)} %bitcast.7.weight_ref), custom_call_target="tpu_custom_call" | custom-call | tf_op jit(solution)/shard_map/next_rows/pallas_call | solution.py:131
  (2 shorter events, 0.0 us)
Async XLA Ops:
  10.1 7.5 %copy-start.2 = (s32[32,1]{0,1:T(1,128)S(1)}, s32[32,1]{0,1:T(1,128)}, u32[]{:S(2)}) copy-start(s32[32,1]{0,1:T(1,128)} %param.14) | copy-start | bytes 388
  10.1 7.5 %copy-start = (f32[8,192,256]{2,1,0:T(8,128)S(1)}, f32[8,192,256]{2,1,0:T(8,128)}, u32[]{:S(2)}) copy-start(f32[8,192,256]{2,1,0:T(8,128)} %master_ref.1) | copy-start | bytes 4718596
  10.1 79.1 %all-to-all-start.1 = ((bf16[32,192,256]{2,1,0:T(8,128)(2,1)}), bf16[32,192,256]{2,1,0:T(8,128)(2,1)}, u32[]{:S(2)}, u32[]{:S(2)}) async-start(bf16[32,192,256]{2,1,0:T(8,128)(2,1)} %bitcast.10), calls=%async_computation.1 | async-start | bytes 6291456 | tf_op jit(solution)/shard_map/all_to_all | solution.py:202
  89.2 76.2 %all-to-all-start = ((bf16[32,192,256]{2,1,0:T(8,128)(2,1)}), bf16[32,192,256]{2,1,0:T(8,128)(2,1)S(1)}, u32[]{:S(2)}, u32[]{:S(2)}) async-start(bf16[32,192,256]{2,1,0:T(8,128)(2,1)} %gather_fusion), calls=%async_computation | async-start | bytes 6291456 | tf_op jit(solution)/shard_map/all_to_all | solution.py:202
  165.4 1.7 copy-start.1
  167.1 76.3 %all-to-all-start.2 = ((bf16[32,192,256]{2,1,0:T(8,128)(2,1)}), bf16[32,192,256]{2,1,0:T(8,128)(2,1)}, u32[]{:S(2)}, u32[]{:S(2)}) async-start(bf16[32,192,256]{2,1,0:T(8,128)(2,1)} %get-tuple-element.17), calls=%async_computation.2 | async-start | bytes 6291456 | tf_op jit(solution)/shard_map/all_to_all | solution.py:202

commit v2 on v1

v2 whole, which is shorter than its diff:
```python
import functools

import jax
import jax.numpy as jnp
from jax import lax
from jax.experimental import pallas as pl
from jax.experimental.pallas import tpu as pltpu
from jax.sharding import PartitionSpec as P

beta_one = 0.9
beta_two = 0.999
adam_eps = 1e-08
learn_rate = 0.006
fix_one = 0.9999734386011124
fix_two = 0.0952078528862904

BOTH = ("group", "slot")


def column_of(row):
    return jnp.transpose(jnp.broadcast_to(row, (8, row.shape[1])))[:, :1]


def slot_grad_kernel(count_ref, rows_ref, cot_ref, gate_ref, out_ref, turned):
    rows = rows_ref.shape[0]
    live = lax.broadcasted_iota(jnp.int32, (rows, 1), 0) < count_ref[0]

    @pl.when(pl.program_id(0) == 0)
    def _():
        kept = jnp.where(live, rows_ref[...].astype(jnp.float32), 0.0)
        turned[...] = jnp.transpose(kept).astype(jnp.bfloat16)

    scaled = column_of(gate_ref[...]) * cot_ref[...].astype(jnp.float32)
    scaled = jnp.where(live, scaled, 0.0).astype(jnp.bfloat16)
    cols = out_ref.shape[2]
    for i in range(out_ref.shape[0]):
        out_ref[i] = jnp.dot(
            turned[...],
            scaled[:, i * cols : (i + 1) * cols],
            preferred_element_type=jnp.float32,
        ).astype(jnp.bfloat16)


def slot_grads(row_counts, rows_in, cotangent, gate_row, group_count):
    rows, ff = rows_in.shape
    cols = cotangent.shape[1] // group_count
    return pl.pallas_call(
        slot_grad_kernel,
        name="slot_grads",
        out_shape=jax.ShapeDtypeStruct((group_count, ff, cols), jnp.bfloat16),
        grid_spec=pltpu.PrefetchScalarGridSpec(
            num_scalar_prefetch=1,
            grid=(group_count // 2,),
            in_specs=[
                pl.BlockSpec((rows, ff), lambda g, c: (0, 0)),
                pl.BlockSpec((rows, 2 * cols), lambda g, c: (0, g)),
                pl.BlockSpec((1, rows), lambda g, c: (0, 0)),
            ],
            out_specs=pl.BlockSpec((2, ff, cols), lambda g, c: (g, 0, 0)),
            scratch_shapes=[pltpu.VMEM((ff, rows), jnp.bfloat16)],
        ),
        compiler_params=pltpu.CompilerParams(dimension_semantics=("arbitrary",)),
    )(row_counts, rows_in, cotangent, gate_row)


def update_kernel(
    old_ref, new_ref, grads_ref, master_ref, one_ref, two_ref,
    master_out, one_out, two_out, send_ref, total, fresh,
):
    slots = grads_ref.shape[0]
    total[...] = jnp.zeros_like(total)

    def add(s, _):
        e = old_ref[s]
        total[e] = total[e] + grads_ref[s].astype(jnp.float32)
        return 0

    lax.fori_loop(0, slots, add, 0, unroll=8)
    grad = total[...]
    first = beta_one * one_ref[...].astype(jnp.float32) + (1.0 - beta_one) * grad
    second = beta_two * two_ref[...].astype(jnp.float32) + (1.0 - beta_two) * grad * grad
    master = master_ref[...] - (learn_rate / fix_one) * first / (
        jnp.sqrt(second * (1.0 / fix_two)) + adam_eps
    )
    master_out[...] = master
    one_out[...] = first.astype(jnp.bfloat16)
    two_out[...] = second.astype(jnp.bfloat16)
    fresh[...] = master.astype(jnp.bfloat16)

    def pick(s, _):
        send_ref[s] = fresh[new_ref[s]]
        return 0

    lax.fori_loop(0, slots, pick, 0, unroll=8)


def update(old, new, grads, master, one, two):
    slots, rows, cols = grads.shape
    experts = master.shape[0]
    step = max(d for d in (16, 32, 48) if rows % d == 0)
    state = pl.BlockSpec((experts, step, cols), lambda i, a, b: (0, i, 0))
    wide = pl.BlockSpec((slots, step, cols), lambda i, a, b: (0, i, 0))
    return pl.pallas_call(
        update_kernel,
        name="update",
        out_shape=(
            jax.ShapeDtypeStruct(master.shape, jnp.float32),
            jax.ShapeDtypeStruct(master.shape, jnp.bfloat16),
            jax.ShapeDtypeStruct(master.shape, jnp.bfloat16),
            jax.ShapeDtypeStruct(grads.shape, jnp.bfloat16),
        ),
        grid_spec=pltpu.PrefetchScalarGridSpec(
            num_scalar_prefetch=2,
            grid=(rows // step,),
            in_specs=[wide, state, state, state],
            out_specs=[state, state, state, wide],
            scratch_shapes=[
                pltpu.VMEM((experts, step, cols), jnp.float32),
                pltpu.VMEM((experts, step, cols), jnp.bfloat16),
            ],
        ),
        compiler_params=pltpu.CompilerParams(dimension_semantics=("arbitrary",)),
    )(old, new, grads, master, one, two)


def next_kernel(rows_ref, weight_ref, out_ref):
    cols = weight_ref.shape[2]
    for i in range(weight_ref.shape[0]):
        out_ref[:, i * cols : (i + 1) * cols] = jnp.dot(
            rows_ref[...], weight_ref[i], preferred_element_type=jnp.float32
        ).astype(jnp.bfloat16)


def next_rows(rows_next, weight):
    groups, ff, cols = weight.shape
    rows = rows_next.shape[0]
    return pl.pallas_call(
        next_kernel,
        name="next_rows",
        out_shape=jax.ShapeDtypeStruct((rows, groups * cols), jnp.bfloat16),
        grid=(groups // 2,),
        in_specs=[
            pl.BlockSpec((rows, ff), lambda g: (0, 0)),
            pl.BlockSpec((2, ff, cols), lambda g: (g, 0, 0)),
        ],
        out_specs=pl.BlockSpec((rows, 2 * cols), lambda g: (0, g)),
        compiler_params=pltpu.CompilerParams(dimension_semantics=("arbitrary",)),
    )(rows_next, weight)


def exchange(blocks):
    return lax.all_to_all(blocks, BOTH, split_axis=0, concat_axis=0, tiled=True)


def along_line(mine, line, across):
    low, high, lows, highs = mine, mine, [], []
    for turn in range(line - 1):
        ups = [(g, g + across) for g in range(turn * across, (line - 1) * across)]
        downs = [(g + across, g) for g in range((line - 1 - turn) * across)]
        low = lax.ppermute(low, "group", ups)
        high = lax.ppermute(high, "group", downs)
        lows.append(low)
        highs.append(high)
    return lows, highs


def pick_kernel(pairs, plane_ref, wanted_ref, *rest):
    count = sum(2 if p else 1 for p in pairs)
    blocks, outs, sems = rest[:count], rest[count:-1], rest[-1]
    for j, out in enumerate(outs):
        at = 0
        for i, reach in enumerate(pairs):
            if not reach:
                pltpu.make_async_copy(
                    blocks[at].at[wanted_ref[j]], out.at[i], sems.at[j]
                ).start()
                at += 1
                continue
            for side in range(2):

                @pl.when((plane_ref[0] >= reach) == (side == 0))
                def _(block=blocks[at + side], out=out, i=i, j=j):
                    pltpu.make_async_copy(
                        block.at[wanted_ref[j]], out.at[i], sems.at[j]
                    ).start()

            at += 2
    for j, out in enumerate(outs):
        pltpu.make_async_copy(out, out, sems.at[j]).wait()


def picked(plane, wanted, entries):
    pairs = [entry[2] if len(entry) == 3 else 0 for entry in entries]
    blocks = [block for entry in entries for block in entry[:2]]
    piece = (len(entries),) + blocks[0].shape[1:]
    peers = wanted.shape[0]
    return pl.pallas_call(
        functools.partial(pick_kernel, pairs),
        name="picked",
        out_shape=[jax.ShapeDtypeStruct(piece, jnp.bfloat16)] * peers,
        in_specs=[pl.BlockSpec(memory_space=pltpu.SMEM)] * 2
        + [pl.BlockSpec(memory_space=pl.ANY)] * len(blocks),
        out_specs=[pl.BlockSpec(memory_space=pltpu.VMEM)] * peers,
        scratch_shapes=[pltpu.SemaphoreType.DMA((peers,))],
    )(plane, wanted, *blocks)


def among_peers(picks, peers, devices):
    parts = [picks[0]]
    for j in range(1, peers):
        pairs = [(p, p - p % peers + (p % peers ^ j)) for p in range(devices)]
        parts.append(lax.ppermute(picks[j], BOTH, pairs))
    return jnp.stack(parts)


def add_part(cot_ref, weights, total, first, valid):
    @pl.when(first)
    def _():
        total[...] = jnp.zeros_like(total)

    @pl.when(valid)
    def _():
        weight = jnp.concatenate([w[0, 0] for w in weights], axis=0)
        total[...] += lax.dot_general(
            cot_ref[...], weight, (((1,), (1,)), ((), ())), preferred_element_type=jnp.float32
        )


def near_kernel(across, me_ref, plane_ref, valid_ref, cot_ref, *rest):
    *weights, total = rest
    i = pl.program_id(0)
    add_part(cot_ref, weights, total, i == 0, valid_ref[i // across] == 1)


def far_kernel(
    across, me_ref, plane_ref, valid_ref, count_ref, cot_ref, rows_ref, gate_ref, so_far, *rest
):
    *weights, grad_ref, gate_out, total = rest
    i = pl.program_id(0)
    rows = rows_ref.shape[0]
    add_part(cot_ref, weights, total, i == 0, valid_ref[i // across] == 1)

    @pl.when(i == pl.num_programs(0) - 1)
    def _():
        live = lax.broadcasted_iota(jnp.int32, (rows, 1), 0) < count_ref[0]
        back = jnp.where(live, so_far[...] + total[...], 0.0)
        grad_ref[...] = (column_of(gate_ref[...]) * back).astype(jnp.bfloat16)
        summed = jnp.sum(rows_ref[...].astype(jnp.float32) * back, axis=1, keepdims=True)
        gate_out[...] = jnp.transpose(jnp.broadcast_to(summed, (rows, 128)))[:1]


def back_specs(parts, rows, across, slot_count):
    _, _, part_rows, cols = parts.shape

    def piece(k):
        def index(i, m, *_):
            return (((i % across) * slot_count + k) ^ m[0], i // across, 0, 0)

        return pl.BlockSpec((1, 1, part_rows, cols), index)

    def taken(i, m, plane, *_):
        return (0, plane[i // across] * across + i % across)

    return pl.BlockSpec((rows, cols), taken), [piece(k) for k in range(slot_count)]


def near_back(me, planes, valid, cotangent, parts, across, slot_count):
    rows, ff = cotangent.shape[0], slot_count * parts.shape[2]
    cot_spec, pieces = back_specs(parts, rows, across, slot_count)
    return pl.pallas_call(
        functools.partial(near_kernel, across),
        name="near_back",
        out_shape=jax.ShapeDtypeStruct((rows, ff), jnp.float32),
        grid_spec=pltpu.PrefetchScalarGridSpec(
            num_scalar_prefetch=3,
            grid=(parts.shape[1] * across,),
            in_specs=[cot_spec] + pieces,
            out_specs=pl.BlockSpec((rows, ff), lambda i, *_: (0, 0)),
        ),
        compiler_params=pltpu.CompilerParams(dimension_semantics=("arbitrary",)),
    )(me, planes, valid, cotangent, *([parts] * slot_count))


def far_back(
    me, planes, valid, row_counts, cotangent, rows_in, gate_row, so_far, parts, across, slot_count
):
    rows, ff = rows_in.shape
    cot_spec, pieces = back_specs(parts, rows, across, slot_count)
    whole = pl.BlockSpec((rows, ff), lambda i, *_: (0, 0))
    row = pl.BlockSpec((1, rows), lambda i, *_: (0, 0))
    return pl.pallas_call(
        functools.partial(far_kernel, across),
        name="far_back",
        out_shape=(
            jax.ShapeDtypeStruct((rows, ff), jnp.bfloat16),
            jax.ShapeDtypeStruct((1, rows), jnp.float32),
        ),
        grid_spec=pltpu.PrefetchScalarGridSpec(
            num_scalar_prefetch=4,
            grid=(parts.shape[1] * across,),
            in_specs=[cot_spec, whole, row, whole] + pieces,
            out_specs=[whole, row],
            scratch_shapes=[pltpu.VMEM((rows, ff), jnp.float32)],
        ),
        compiler_params=pltpu.CompilerParams(dimension_semantics=("arbitrary",)),
    )(
        me, planes, valid, row_counts, cotangent, rows_in, gate_row, so_far,
        *([parts] * slot_count),
    )


def shards(
    rows_in, cotangent, gate_prob, row_counts, old_place, new_place, rows_next,
    master, moment_one, moment_two,
):
    slot_count = lax.axis_size("slot")
    group_count = lax.axis_size("group")
    devices = group_count * slot_count
    _, part_rows, part_cols = master.shape
    ff = slot_count * part_rows
    across = 2
    line = group_count // across
    peers = across * slot_count
    g_own, k_own = lax.axis_index("group"), lax.axis_index("slot")
    plane = g_own // across
    me = (g_own % across) * slot_count + k_own
    old, new = old_place[:, 0], new_place[:, 0]
    gate_row = gate_prob.reshape(1, -1)

    mine = master.astype(jnp.bfloat16)
    lows, highs = along_line(mine, line, across)
    wanted = lax.dynamic_slice(old, (plane * peers,), (peers,))[
        me ^ jnp.arange(peers, dtype=jnp.int32)
    ]
    near, near_off, far, far_off = [(mine,)], [0], [], []
    for r in range(1, line):
        blocks, offs = (near, near_off) if r == 1 else (far, far_off)
        if 2 * r < line:
            blocks += [(lows[r - 1],), (highs[r - 1],)]
            offs += [-r, r]
        else:
            blocks.append((lows[r - 1], highs[r - 1], r))
            offs.append(jnp.where(plane >= r, -r, r))

    def table(offs):
        at = plane + jnp.stack([jnp.asarray(o, jnp.int32) for o in offs])
        valid = (at >= 0) & (at < line)
        return jnp.clip(at, 0, line - 1), valid.astype(jnp.int32)

    me_one, plane_one = me.reshape(1), plane.reshape(1)
    grads = slot_grads(row_counts, rows_in, cotangent, gate_row, group_count)
    arrived = exchange(grads.reshape(-1, part_rows, part_cols))
    parts = among_peers(picked(plane_one, wanted, near), peers, devices)
    so_far = near_back(me_one, *table(near_off), cotangent, parts, across, slot_count)

    new_master, new_first, new_second, send = update(
        old, new, arrived, master, moment_one, moment_two
    )
    weight_next = exchange(send).reshape(group_count, ff, part_cols)

    parts = among_peers(picked(plane_one, wanted, far), peers, devices)
    input_grad, gate_grad = far_back(
        me_one, *table(far_off), row_counts, cotangent, rows_in, gate_row, so_far, parts,
        across, slot_count,
    )
    next_out = next_rows(rows_next, weight_next)
    return input_grad, gate_grad.reshape(-1), new_master, new_first, new_second, next_out


def solution(mesh):
    rows = P(BOTH, None)
    row = P(BOTH)
    state = P(None, "slot", "group")
    return jax.shard_map(
        shards,
        mesh=mesh,
        in_specs=(rows, rows, row, row, P(), P(), rows, state, state, state),
        out_specs=(rows, row, state, state, state, rows),
        check_vma=False,
    )
```

time: 252 us -> 275 us (1.091)
  blocking collectives: 0 us -> 78.6 us
  waiting for transfers between devices: 191 us -> 114 us
  starting transfers between devices: 16.7 us -> 30.9 us
    all_to_all x3 -> x1, waiting for transfers between devices: 191 us -> 0.01 us  [exchange(): return lax.all_to_all(blocks, BOTH, split_axis=0, concat_axis=0, tiled=True)]
    ppermute x0 -> x20, waiting for transfers between devices: none -> 114 us  [the longest x3 90.7 us: along_line(): high = lax.ppermute(high, 'group', downs)]
    all_to_all x0 -> x1, blocking collectives: none -> 78.6 us  [exchange(): return lax.all_to_all(blocks, BOTH, split_axis=0, concat_axis=0, tiled=True)]
    ppermute x0 -> x20, starting transfers between devices: none -> 27.1 us  [the longest x14 15.5 us: among_peers(): parts.append(lax.ppermute(picks[j], BOTH, pairs))]
    all_to_all x3 -> x1, starting transfers between devices: 16.7 us -> 3.78 us  [exchange(): return lax.all_to_all(blocks, BOTH, split_axis=0, concat_axis=0, tiled=True)]
    pallas_call x1 -> x4, Pallas kernels: 8.92 us -> 20.7 us  [the longest x2 7.31 us: picked(): pl.pallas_call(functools.partial(pick_kernel, pairs), name='picked', out_...]
    pallas_call x1, Pallas kernels: 12.7 us -> 7.88 us  [update(): pl.pallas_call(update_kernel, name='update', out_shape=(jax.ShapeDtypeStr...]
    unnamed x6 -> x34, local copies, waits for them, and re-layouts: 1.72 us -> 5.65 us
  transfers between devices with their start and end apart: 3 -> 21, of which waited for: 3 -> 11; matrix products, arithmetic and copies ran while one was open for 1% -> 2% of each run, Pallas kernels for 9% -> 8%
where the time goes in v2:
time: 275 us; the launch traced here: 274 us
  waiting for transfers between devices  114 us (41%)
  blocking collectives  78.6 us (29%)
  Pallas kernels  40.3 us (15%)
  starting transfers between devices  30.9 us (11%)
  local copies, waits for them, and re-layouts  6.96 us (3%)
    ppermute x3, waiting for transfers between devices, along_line(): high = lax.ppermute(high, 'group', downs)  90.7 us
    all_to_all x1, blocking collectives, exchange(): return lax.all_to_all(blocks, BOTH, split_axis=0, concat_axis=0, tiled=True)  78.6 us
    ppermute x14, waiting for transfers between devices, among_peers(): parts.append(lax.ppermute(picks[j], BOTH, pairs))  20.4 us
    ppermute x14, starting transfers between devices, among_peers(): parts.append(lax.ppermute(picks[j], BOTH, pairs))  15.5 us
    pallas_call x1, Pallas kernels, update(): pl.pallas_call(update_kernel, name='update', out_shape=(jax.ShapeDtypeStr...  7.88 us
    ppermute x3, starting transfers between devices, along_line(): low = lax.ppermute(low, 'group', ups)  7.72 us
    pallas_call x2, Pallas kernels, picked(): pl.pallas_call(functools.partial(pick_kernel, pairs), name='picked', out_...  7.31 us
    pallas_call x1, Pallas kernels, far_back(): pl.pallas_call(functools.partial(far_kernel, across), name='far_back', ou...  6.79 us
  transfers between devices with their start and end apart: 21, of which 11 were waited for; matrix products, arithmetic and copies ran while one was open for 2% of the time, Pallas kernels for 8%

profile of v2, /device:TPU:0, one launch (start us, length us, event | category | flops | bytes accessed | tf_op | source)
XLA Modules:
  0.0 274.2 jit_solution(15456911758648214549)
XLA Ops:
  1.3 6.4 %slot_grads.1 = bf16[8,768,256]{2,1,0:T(8,128)(2,1)} custom-call(s32[1]{0:T(128)S(6)} %copy.30.count_ref, bf16[512,768]{1,0:T(8,128)(2,1)} %rows_ref.4, bf16[512,2048]{1,0:T(8,128)(2,1)} %cot_ref.5, f32[1,512]{1,0:T(1,128)} %bitcast.47), custom_call_target="tpu_custom_call" | custom-call | tf_op jit(solution)/shard_map/slot_grads/pallas_call | solution.py:47
  7.7 78.6 %all_to_all.10.grads_ref = bf16[32,192,256]{2,1,0:T(8,128)(2,1)} all-to-all(bf16[32,192,256]{2,1,0:T(8,128)(2,1)} %bitcast.46), channel_id=1, replica_groups=mesh['group'=8,'slot'=4] {'group','slot'}, dimensions={0} | all-to-all | bytes 6291456 | tf_op jit(solution)/shard_map/all_to_all | solution.py:152
  86.3 7.9 %update.1 = (f32[8,192,256]{2,1,0:T(8,128)}, bf16[8,192,256]{2,1,0:T(8,128)(2,1)}, bf16[8,192,256]{2,1,0:T(8,128)(2,1)}, bf16[32,192,256]{2,1,0:T(8,128)(2,1)}) custom-call(s32[32]{0:T(128)} %bitcast.50, s32[32]{0:T(128)} %bitcast.49, bf16[32,192,256]{2,1,0:T(8,128)(2,1)} %all_to_all.10.grads_ref, f32[8,192,256]{2,1,0:T(8,128)} %master_ref.1, ...), custom_call_target="tpu_custom_call" | custom-call | tf_op jit(solution)/shard_map/update/pallas_call | solution.py:103
  94.1 3.8 %all-to-all-start.1 = ((bf16[32,192,256]{2,1,0:T(8,128)(2,1)}), bf16[32,192,256]{2,1,0:T(8,128)(2,1)}, u32[]{:S(2)}, u32[]{:S(2)}) async-start(bf16[32,192,256]{2,1,0:T(8,128)(2,1)} %get-tuple-element.49), calls=%async_computation.1 | async-start | bytes 6291456 | tf_op jit(solution)/shard_map/all_to_all | solution.py:152
  97.9 0.0 copy-start.7
  98.0 0.0 copy-start.9
  98.0 0.1 convert_element_type.11.rest_0_
  98.1 0.0 copy-start.3
  98.1 1.3 collective-permute-start.1
  99.4 4.6 %collective-permute-start = (bf16[8,192,256]{2,1,0:T(8,128)(2,1)S(1)}, bf16[8,192,256]{2,1,0:T(8,128)(2,1)S(1)}, u32[]{:S(2)}, u32[]{:S(2)}) collective-permute-start(bf16[8,192,256]{2,1,0:T(8,128)(2,1)S(1)} %convert_element_type.11.rest_0_), channel_id=1, source_target_pairs={{0,8},{4,12},{8,16},{12,20},{16,24},{20,28},{1,9},{5,13},{9,17},{1... | collective-permute-start | bytes 2359304 | tf_op jit(solution)/shard_map/ppermute | solution.py:160
  104.0 0.1 dynamic-slice_bitcast_fusion
  104.1 1.2 gather_fusion
  105.3 0.6 and_convert_fusion.1
  105.9 0.5 and_convert_fusion.valid_ref
  106.4 0.6 add_clamp_fusion.plane_ref
  107.0 57.4 %collective-permute-done.1.rest_2_ = bf16[8,192,256]{2,1,0:T(8,128)(2,1)S(1)} collective-permute-done((bf16[8,192,256]{2,1,0:T(8,128)(2,1)S(1)}, bf16[8,192,256]{2,1,0:T(8,128)(2,1)S(1)}, u32[]{:S(2)}, u32[]{:S(2)}) %collective-permute-start.1) | collective-permute-done | bytes 786464 | tf_op jit(solution)/shard_map/ppermute | solution.py:161
  164.3 2.4 collective-permute-done.rest_1_
  166.8 0.9 copy-done.4
  167.6 3.9 %picked.2 = (bf16[3,192,256]{2,1,0:T(8,128)(2,1)}, bf16[3,192,256]{2,1,0:T(8,128)(2,1)}, bf16[3,192,256]{2,1,0:T(8,128)(2,1)}, bf16[3,192,256]{2,1,0:T(8,128)(2,...) custom-call(s32[1]{0:T(128)} %bitcast.4.plane_ref, ...), custom_call_target="tpu_custom_call" | custom-call | tf_op jit(solution)/shard_map/picked/pallas_call | solution.py:197
  171.6 0.1 collective-permute-start.2
  171.7 0.5 broadcast_clamp_fusion.plane_ref
  172.2 1.1 collective-permute-start.3
  173.3 0.7 collective-permute-start.4
  174.1 1.3 collective-permute-start.10
  175.3 1.5 collective-permute-start.9
  176.9 1.0 bitcast_dynamic-update-slice_fusion.7
  177.9 0.0 collective-permute-done.2
  177.9 2.6 collective-permute-start.5
  180.5 1.8 collective-permute-done.3
  182.3 1.3 collective-permute-start.6
  183.6 4.1 %collective-permute-done.4 = bf16[3,192,256]{2,1,0:T(8,128)(2,1)S(1)} collective-permute-done((bf16[3,192,256]{2,1,0:T(8,128)(2,1)}, bf16[3,192,256]{2,1,0:T(8,128)(2,1)S(1)}, u32[]{:S(2)}, u32[]{:S(2)}) %collective-permute-start.4) | collective-permute-done | bytes 294944 | tf_op jit(solution)/shard_map/ppermute | solution.py:212
  187.7 3.2 %collective-permute-start.7 = (bf16[3,192,256]{2,1,0:T(8,128)(2,1)}, bf16[3,192,256]{2,1,0:T(8,128)(2,1)S(1)}, u32[]{:S(2)}, u32[]{:S(2)}) collective-permute-start(bf16[3,192,256]{2,1,0:T(8,128)(2,1)} %get-tuple-element.34), channel_id=1, source_target_pairs={{0,6},{1,7},{2,4},{3,5},{4,2},{5,3},{6,0},{7,1},{8,14},{9,15},{10,... | collective-permute-start | bytes 884744 | tf_op jit(solution)/shard_map/ppermute | solution.py:212
  190.9 0.0 collective-permute-done.5
  190.9 0.3 collective-permute-start.8
  191.2 23.4 %collective-permute-done.10.rest_1_ = bf16[8,192,256]{2,1,0:T(8,128)(2,1)S(1)} collective-permute-done((bf16[8,192,256]{2,1,0:T(8,128)(2,1)}, bf16[8,192,256]{2,1,0:T(8,128)(2,1)S(1)}, u32[]{:S(2)}, u32[]{:S(2)}) %collective-permute-start.10) | collective-permute-done | bytes 786464 | tf_op jit(solution)/shard_map/ppermute | solution.py:161
  214.6 1.3 collective-permute-start.12
  215.8 0.0 collective-permute-done.9.rest_0_
  215.9 1.6 collective-permute-start.11
  217.5 0.0 collective-permute-done.6
  217.5 0.0 collective-permute-done.7
  217.5 0.0 collective-permute-done.8
  217.6 1.5 copy-done
  219.1 6.7 %near_back.1.so_far = f32[512,768]{1,0:T(8,128)} custom-call(s32[1]{0:T(128)} %bitcast.me_ref, s32[3]{0:T(128)} %add_clamp_fusion.plane_ref, s32[3]{0:T(128)} %and_convert_fusion.valid_ref, bf16[512,2048]{1,0:T(8,128)(2,1)} %cot_ref.5, bf16[8,3,192,256]{3,2,1,0:T(8,128)(2,1)} %copy-done, bf16[8,3,192,256]{3,2,1,0:T(8,128)(2,1)} %copy-done, ...), custom_call_target="tpu_custom_call" | custom-call | tf_op jit(solution)/shard_map/near_back/pallas_call | solution.py:270
  225.7 10.0 %collective-permute-done.12.rest_3_ = bf16[8,192,256]{2,1,0:T(8,128)(2,1)} collective-permute-done((bf16[8,192,256]{2,1,0:T(8,128)(2,1)S(1)}, bf16[8,192,256]{2,1,0:T(8,128)(2,1)}, u32[]{:S(2)}, u32[]{:S(2)}) %collective-permute-start.12) | collective-permute-done | bytes 786464 | tf_op jit(solution)/shard_map/ppermute | solution.py:161
  235.7 0.0 collective-permute-done.11.rest_2_
  235.7 3.4 %picked.3 = (bf16[2,192,256]{2,1,0:T(8,128)(2,1)}, bf16[2,192,256]{2,1,0:T(8,128)(2,1)}, bf16[2,192,256]{2,1,0:T(8,128)(2,1)}, bf16[2,192,256]{2,1,0:T(8,128)(2,...) custom-call(s32[1]{0:T(128)} %bitcast.4.plane_ref, ...), custom_call_target="tpu_custom_call" | custom-call | tf_op jit(solution)/shard_map/picked/pallas_call | solution.py:197
  239.1 0.1 collective-permute-start.13
  239.2 1.1 collective-permute-start.14
  240.3 0.7 collective-permute-start.15
  241.0 1.4 collective-permute-start.16
  242.4 0.3 collective-permute-start.17
  242.7 0.9 bitcast_dynamic-update-slice_fusion.15
  243.7 0.0 collective-permute-done.13
  243.7 2.1 collective-permute-start.18
  245.8 1.5 collective-permute-done.14
  247.2 0.6 collective-permute-start.19
  247.9 2.5 collective-permute-done.15
  250.4 0.0 collective-permute-done.16
  250.4 1.8 collective-permute-done.17
  252.2 5.7 %collective-permute-done.18 = bf16[2,192,256]{2,1,0:T(8,128)(2,1)S(1)} collective-permute-done((bf16[2,192,256]{2,1,0:T(8,128)(2,1)}, bf16[2,192,256]{2,1,0:T(8,128)(2,1)S(1)}, u32[]{:S(2)}, u32[]{:S(2)}) %collective-permute-start.18) | collective-permute-done | bytes 196640 | tf_op jit(solution)/shard_map/ppermute | solution.py:212
  258.0 3.0 %collective-permute-done.19 = bf16[2,192,256]{2,1,0:T(8,128)(2,1)S(1)} collective-permute-done((bf16[2,192,256]{2,1,0:T(8,128)(2,1)}, bf16[2,192,256]{2,1,0:T(8,128)(2,1)S(1)}, u32[]{:S(2)}, u32[]{:S(2)}) %collective-permute-start.19) | collective-permute-done | bytes 196640 | tf_op jit(solution)/shard_map/ppermute | solution.py:212
  261.0 1.1 copy-done.1
  262.1 6.8 %far_back.1 = (bf16[512,768]{1,0:T(8,128)(2,1)}, f32[1,512]{1,0:T(1,128)}) custom-call(s32[1]{0:T(128)} %bitcast.me_ref, s32[2]{0:T(128)} %broadcast_clamp_fusion.plane_ref, s32[2]{0:T(128)} %get-tuple-element.50.valid_ref, s32[1]{0:T(128)S(6)} %copy.30.count_ref, bf16[512,2048]{1,0:T(8,128)(2,1)} %cot_ref.5, bf16[512,768]{1,0:T(8,128)(2,1)} %rows_ref.4, ...), custom_call_target="tpu_custom_call" | custom-call | tf_op jit(solution)/shard_map/far_back/pallas_call | solution.py:291
  268.9 5.3 %next_rows.1 = bf16[512,2048]{1,0:T(8,128)(2,1)} custom-call(bf16[512,768]{1,0:T(8,128)(2,1)} %rows_ref.5, bf16[8,768,256]{2,1,0:T(8,128)(2,1)} %bitcast.27.weight_ref), custom_call_target="tpu_custom_call" | custom-call | tf_op jit(solution)/shard_map/next_rows/pallas_call | solution.py:137
  (31 shorter events, 0.3 us)
Async XLA Ops:
  94.1 3.8 %copy-start.2 = (f32[8,192,256]{2,1,0:T(8,128)S(1)}, f32[8,192,256]{2,1,0:T(8,128)}, u32[]{:S(2)}) copy-start(f32[8,192,256]{2,1,0:T(8,128)} %master_ref.1) | copy-start | bytes 4718596
  94.1 174.7 %all-to-all-start.1 = ((bf16[32,192,256]{2,1,0:T(8,128)(2,1)}), bf16[32,192,256]{2,1,0:T(8,128)(2,1)}, u32[]{:S(2)}, u32[]{:S(2)}) async-start(bf16[32,192,256]{2,1,0:T(8,128)(2,1)} %get-tuple-element.49), calls=%async_computation.1 | async-start | bytes 6291456 | tf_op jit(solution)/shard_map/all_to_all | solution.py:152
  97.9 6.1 %copy-start.7 = (s32[32,1]{0,1:T(1,128)S(1)}, s32[32,1]{0,1:T(1,128)}, u32[]{:S(2)}) copy-start(s32[32,1]{0,1:T(1,128)} %param.14) | copy-start | bytes 388
  98.0 7.9 %copy-start.9 = (s32[3]{0:T(128)S(1)}, s32[3]{0:T(128)}, u32[]{:S(2)}) copy-start(s32[3]{0:T(128)} %constant.52.clone.1) | copy-start | bytes 40
  98.1 68.7 %copy-start.3 = (bf16[8,192,256]{2,1,0:T(8,128)(2,1)}, bf16[8,192,256]{2,1,0:T(8,128)(2,1)S(1)}, u32[]{:S(2)}) copy-start(bf16[8,192,256]{2,1,0:T(8,128)(2,1)S(1)} %convert_element_type.11.rest_0_) | copy-start | bytes 2359300
  98.1 66.3 %collective-permute-start.1 = (bf16[8,192,256]{2,1,0:T(8,128)(2,1)S(1)}, bf16[8,192,256]{2,1,0:T(8,128)(2,1)S(1)}, u32[]{:S(2)}, u32[]{:S(2)}) collective-permute-start(bf16[8,192,256]{2,1,0:T(8,128)(2,1)S(1)} %convert_element_type.11.rest_0_), channel_id=1, source_target_pairs={{8,0},{12,4},{16,8},{20,12},{24,16},{28,20},{9,1},{13,5},{17,9},{2... | collective-permute-start | bytes 2359304 | tf_op jit(solution)/shard_map/ppermute | solution.py:161
  99.4 67.4 %collective-permute-start = (bf16[8,192,256]{2,1,0:T(8,128)(2,1)S(1)}, bf16[8,192,256]{2,1,0:T(8,128)(2,1)S(1)}, u32[]{:S(2)}, u32[]{:S(2)}) collective-permute-start(bf16[8,192,256]{2,1,0:T(8,128)(2,1)S(1)} %convert_element_type.11.rest_0_), channel_id=1, source_target_pairs={{0,8},{4,12},{8,16},{12,20},{16,24},{20,28},{1,9},{5,13},{9,17},{1... | collective-permute-start | bytes 2359304 | tf_op jit(solution)/shard_map/ppermute | solution.py:160
  164.3 2.4 copy-start.5
  166.8 0.9 copy-start.4
  171.6 19.3 %copy-start.8 = (bf16[3,192,256]{2,1,0:T(8,128)(2,1)S(1)}, bf16[3,192,256]{2,1,0:T(8,128)(2,1)}, u32[]{:S(2)}) copy-start(bf16[3,192,256]{2,1,0:T(8,128)(2,1)} %get-tuple-element.35) | copy-start | bytes 884740
  171.6 6.3 %collective-permute-start.2 = (bf16[3,192,256]{2,1,0:T(8,128)(2,1)}, bf16[3,192,256]{2,1,0:T(8,128)(2,1)S(1)}, u32[]{:S(2)}, u32[]{:S(2)}) collective-permute-start(bf16[3,192,256]{2,1,0:T(8,128)(2,1)} %get-tuple-element.29), channel_id=1, source_target_pairs={{0,1},{1,0},{2,3},{3,2},{4,5},{5,4},{6,7},{7,6},{8,9},{9,8},{10,11... | collective-permute-start | bytes 884744 | tf_op jit(solution)/shard_map/ppermute | solution.py:212
  172.2 10.1 %collective-permute-start.3 = (bf16[3,192,256]{2,1,0:T(8,128)(2,1)}, bf16[3,192,256]{2,1,0:T(8,128)(2,1)S(1)}, u32[]{:S(2)}, u32[]{:S(2)}) collective-permute-start(bf16[3,192,256]{2,1,0:T(8,128)(2,1)} %get-tuple-element.30), channel_id=1, source_target_pairs={{0,2},{1,3},{2,0},{3,1},{4,6},{5,7},{6,4},{7,5},{8,10},{9,11},{10,... | collective-permute-start | bytes 884744 | tf_op jit(solution)/shard_map/ppermute | solution.py:212
  173.3 14.3 %collective-permute-start.4 = (bf16[3,192,256]{2,1,0:T(8,128)(2,1)}, bf16[3,192,256]{2,1,0:T(8,128)(2,1)S(1)}, u32[]{:S(2)}, u32[]{:S(2)}) collective-permute-start(bf16[3,192,256]{2,1,0:T(8,128)(2,1)} %get-tuple-element.31), channel_id=1, source_target_pairs={{0,3},{1,2},{2,1},{3,0},{4,7},{5,6},{6,5},{7,4},{8,11},{9,10},{10,... | collective-permute-start | bytes 884744 | tf_op jit(solution)/shard_map/ppermute | solution.py:212
  174.1 40.5 %collective-permute-start.10 = (bf16[8,192,256]{2,1,0:T(8,128)(2,1)}, bf16[8,192,256]{2,1,0:T(8,128)(2,1)S(1)}, u32[]{:S(2)}, u32[]{:S(2)}) collective-permute-start(bf16[8,192,256]{2,1,0:T(8,128)(2,1)} %copy-done.5), channel_id=1, source_target_pairs={{8,0},{12,4},{16,8},{20,12},{9,1},{13,5},{17,9},{21,13},{10,2},{14... | collective-permute-start | bytes 2359304 | tf_op jit(solution)/shard_map/ppermute | solution.py:161
  175.3 40.5 %collective-permute-start.9 = (bf16[8,192,256]{2,1,0:T(8,128)(2,1)}, bf16[8,192,256]{2,1,0:T(8,128)(2,1)}, u32[]{:S(2)}, u32[]{:S(2)}) collective-permute-start(bf16[8,192,256]{2,1,0:T(8,128)(2,1)} %copy-done.4), channel_id=1, source_target_pairs={{8,16},{12,20},{16,24},{20,28},{9,17},{13,21},{17,25},{21,29},{10,... | collective-permute-start | bytes 2359304 | tf_op jit(solution)/shard_map/ppermute | solution.py:160
  177.9 13.0 %collective-permute-start.5 = (bf16[3,192,256]{2,1,0:T(8,128)(2,1)}, bf16[3,192,256]{2,1,0:T(8,128)(2,1)S(1)}, u32[]{:S(2)}, u32[]{:S(2)}) collective-permute-start(bf16[3,192,256]{2,1,0:T(8,128)(2,1)} %get-tuple-element.32), channel_id=1, source_target_pairs={{0,4},{1,5},{2,6},{3,7},{4,0},{5,1},{6,2},{7,3},{8,12},{9,13},{10,... | collective-permute-start | bytes 884744 | tf_op jit(solution)/shard_map/ppermute | solution.py:212
  182.3 35.2 %collective-permute-start.6 = (bf16[3,192,256]{2,1,0:T(8,128)(2,1)}, bf16[3,192,256]{2,1,0:T(8,128)(2,1)S(1)}, u32[]{:S(2)}, u32[]{:S(2)}) collective-permute-start(bf16[3,192,256]{2,1,0:T(8,128)(2,1)} %get-tuple-element.33), channel_id=1, source_target_pairs={{0,5},{1,4},{2,7},{3,6},{4,1},{5,0},{6,3},{7,2},{8,13},{9,12},{10,... | collective-permute-start | bytes 884744 | tf_op jit(solution)/shard_map/ppermute | solution.py:212
  187.7 29.8 %collective-permute-start.7 = (bf16[3,192,256]{2,1,0:T(8,128)(2,1)}, bf16[3,192,256]{2,1,0:T(8,128)(2,1)S(1)}, u32[]{:S(2)}, u32[]{:S(2)}) collective-permute-start(bf16[3,192,256]{2,1,0:T(8,128)(2,1)} %get-tuple-element.34), channel_id=1, source_target_pairs={{0,6},{1,7},{2,4},{3,5},{4,2},{5,3},{6,0},{7,1},{8,14},{9,15},{10,... | collective-permute-start | bytes 884744 | tf_op jit(solution)/shard_map/ppermute | solution.py:212
  190.9 26.6 %collective-permute-start.8 = (bf16[3,192,256]{2,1,0:T(8,128)(2,1)S(1)}, bf16[3,192,256]{2,1,0:T(8,128)(2,1)S(1)}, u32[]{:S(2)}, u32[]{:S(2)}) collective-permute-start(bf16[3,192,256]{2,1,0:T(8,128)(2,1)S(1)} %copy-done.8), channel_id=1, source_target_pairs={{0,7},{1,6},{2,5},{3,4},{4,3},{5,2},{6,1},{7,0},{8,15},{9,14},{10,... | collective-permute-start | bytes 884744 | tf_op jit(solution)/shard_map/ppermute | solution.py:212
  214.6 11.2 %copy-start.6 = (bf16[8,192,256]{2,1,0:T(8,128)(2,1)}, bf16[8,192,256]{2,1,0:T(8,128)(2,1)S(1)}, u32[]{:S(2)}) copy-start(bf16[8,192,256]{2,1,0:T(8,128)(2,1)S(1)} %collective-permute-done.10.rest_1_) | copy-start | bytes 2359300
  214.6 21.1 %collective-permute-start.12 = (bf16[8,192,256]{2,1,0:T(8,128)(2,1)S(1)}, bf16[8,192,256]{2,1,0:T(8,128)(2,1)}, u32[]{:S(2)}, u32[]{:S(2)}) collective-permute-start(bf16[8,192,256]{2,1,0:T(8,128)(2,1)S(1)} %collective-permute-done.10.rest_1_), channel_id=1, source_target_pairs={{8,0},{12,4},{9,1},{13,5},{10,2},{14,6},{11,3},{15,7}} | collective-permute-start | bytes 2359304 | tf_op jit(solution)/shard_map/ppermute | solution.py:161
  215.9 19.9 %collective-permute-start.11 = (bf16[8,192,256]{2,1,0:T(8,128)(2,1)}, bf16[8,192,256]{2,1,0:T(8,128)(2,1)}, u32[]{:S(2)}, u32[]{:S(2)}) collective-permute-start(bf16[8,192,256]{2,1,0:T(8,128)(2,1)} %collective-permute-done.9.rest_0_), channel_id=1, source_target_pairs={{16,24},{20,28},{17,25},{21,29},{18,26},{22,30},{19,27},{23,31}} | collective-permute-start | bytes 2359304 | tf_op jit(solution)/shard_map/ppermute | solution.py:160
  217.6 1.5 copy-start
  239.1 4.6 %collective-permute-start.13 = (bf16[2,192,256]{2,1,0:T(8,128)(2,1)}, bf16[2,192,256]{2,1,0:T(8,128)(2,1)S(1)}, u32[]{:S(2)}, u32[]{:S(2)}) collective-permute-start(bf16[2,192,256]{2,1,0:T(8,128)(2,1)} %get-tuple-element.37), channel_id=1, source_target_pairs={{0,1},{1,0},{2,3},{3,2},{4,5},{5,4},{6,7},{7,6},{8,9},{9,8},{10,11... | collective-permute-start | bytes 589832 | tf_op jit(solution)/shard_map/ppermute | solution.py:212
  239.2 8.1 %collective-permute-start.14 = (bf16[2,192,256]{2,1,0:T(8,128)(2,1)}, bf16[2,192,256]{2,1,0:T(8,128)(2,1)S(1)}, u32[]{:S(2)}, u32[]{:S(2)}) collective-permute-start(bf16[2,192,256]{2,1,0:T(8,128)(2,1)} %get-tuple-element.38), channel_id=1, source_target_pairs={{0,2},{1,3},{2,0},{3,1},{4,6},{5,7},{6,4},{7,5},{8,10},{9,11},{10,... | collective-permute-start | bytes 589832 | tf_op jit(solution)/shard_map/ppermute | solution.py:212
  240.3 10.0 %collective-permute-start.15 = (bf16[2,192,256]{2,1,0:T(8,128)(2,1)}, bf16[2,192,256]{2,1,0:T(8,128)(2,1)S(1)}, u32[]{:S(2)}, u32[]{:S(2)}) collective-permute-start(bf16[2,192,256]{2,1,0:T(8,128)(2,1)} %get-tuple-element.39), channel_id=1, source_target_pairs={{0,3},{1,2},{2,1},{3,0},{4,7},{5,6},{6,5},{7,4},{8,11},{9,10},{10,... | collective-permute-start | bytes 589832 | tf_op jit(solution)/shard_map/ppermute | solution.py:212
  241.0 9.4 %collective-permute-start.16 = (bf16[2,192,256]{2,1,0:T(8,128)(2,1)}, bf16[2,192,256]{2,1,0:T(8,128)(2,1)S(1)}, u32[]{:S(2)}, u32[]{:S(2)}) collective-permute-start(bf16[2,192,256]{2,1,0:T(8,128)(2,1)} %get-tuple-element.40), channel_id=1, source_target_pairs={{0,4},{1,5},{2,6},{3,7},{4,0},{5,1},{6,2},{7,3},{8,12},{9,13},{10,... | collective-permute-start | bytes 589832 | tf_op jit(solution)/shard_map/ppermute | solution.py:212
  242.4 9.8 %collective-permute-start.17 = (bf16[2,192,256]{2,1,0:T(8,128)(2,1)}, bf16[2,192,256]{2,1,0:T(8,128)(2,1)S(1)}, u32[]{:S(2)}, u32[]{:S(2)}) collective-permute-start(bf16[2,192,256]{2,1,0:T(8,128)(2,1)} %get-tuple-element.41), channel_id=1, source_target_pairs={{0,5},{1,4},{2,7},{3,6},{4,1},{5,0},{6,3},{7,2},{8,13},{9,12},{10,... | collective-permute-start | bytes 589832 | tf_op jit(solution)/shard_map/ppermute | solution.py:212
  243.7 14.3 %collective-permute-start.18 = (bf16[2,192,256]{2,1,0:T(8,128)(2,1)}, bf16[2,192,256]{2,1,0:T(8,128)(2,1)S(1)}, u32[]{:S(2)}, u32[]{:S(2)}) collective-permute-start(bf16[2,192,256]{2,1,0:T(8,128)(2,1)} %get-tuple-element.42), channel_id=1, source_target_pairs={{0,6},{1,7},{2,4},{3,5},{4,2},{5,3},{6,0},{7,1},{8,14},{9,15},{10,... | collective-permute-start | bytes 589832 | tf_op jit(solution)/shard_map/ppermute | solution.py:212
  247.2 13.7 %collective-permute-start.19 = (bf16[2,192,256]{2,1,0:T(8,128)(2,1)}, bf16[2,192,256]{2,1,0:T(8,128)(2,1)S(1)}, u32[]{:S(2)}, u32[]{:S(2)}) collective-permute-start(bf16[2,192,256]{2,1,0:T(8,128)(2,1)} %get-tuple-element.43), channel_id=1, source_target_pairs={{0,7},{1,6},{2,5},{3,4},{4,3},{5,2},{6,1},{7,0},{8,15},{9,14},{10,... | collective-permute-start | bytes 589832 | tf_op jit(solution)/shard_map/ppermute | solution.py:212
  260.9 1.2 copy-start.1

commit v3 on v2

v3 whole, which is shorter than its diff:
```python
import functools

import jax
import jax.numpy as jnp
from jax import lax
from jax.experimental import pallas as pl
from jax.experimental.pallas import tpu as pltpu
from jax.sharding import Mesh
from jax.sharding import PartitionSpec as P

beta_one = 0.9
beta_two = 0.999
adam_eps = 1e-08
learn_rate = 0.006
fix_one = 0.9999734386011124
fix_two = 0.0952078528862904

WHOLE_VMEM = 67_000_000

LINE = ("half", "inner")
HALF = ("inner", "slot")
ALL = ("half", "inner", "slot")


def column_of(row):
    return jnp.transpose(jnp.broadcast_to(row, (8, row.shape[1])))[:, :1]


def slot_grad_kernel(count_ref, rows_ref, cot_ref, gate_ref, out_ref, turned):
    rows = rows_ref.shape[0]
    live = lax.broadcasted_iota(jnp.int32, (rows, 1), 0) < count_ref[0]

    @pl.when(pl.program_id(0) == 0)
    def _():
        kept = jnp.where(live, rows_ref[...].astype(jnp.float32), 0.0)
        turned[...] = jnp.transpose(kept).astype(jnp.bfloat16)

    scaled = column_of(gate_ref[...]) * cot_ref[...].astype(jnp.float32)
    scaled = jnp.where(live, scaled, 0.0).astype(jnp.bfloat16)
    cols = out_ref.shape[2]
    for i in range(out_ref.shape[0]):
        out_ref[i] = jnp.dot(
            turned[...],
            scaled[:, i * cols : (i + 1) * cols],
            preferred_element_type=jnp.float32,
        ).astype(jnp.bfloat16)


def slot_grads(row_counts, rows_in, cotangent, gate_row, group_count):
    rows, ff = rows_in.shape
    cols = cotangent.shape[1] // group_count
    return pl.pallas_call(
        slot_grad_kernel,
        name="slot_grads",
        out_shape=jax.ShapeDtypeStruct((group_count, ff, cols), jnp.bfloat16),
        grid_spec=pltpu.PrefetchScalarGridSpec(
            num_scalar_prefetch=1,
            grid=(group_count // 2,),
            in_specs=[
                pl.BlockSpec((rows, ff), lambda g, c: (0, 0)),
                pl.BlockSpec((rows, 2 * cols), lambda g, c: (0, g)),
                pl.BlockSpec((1, rows), lambda g, c: (0, 0)),
            ],
            out_specs=pl.BlockSpec((2, ff, cols), lambda g, c: (g, 0, 0)),
            scratch_shapes=[pltpu.VMEM((ff, rows), jnp.bfloat16)],
        ),
        compiler_params=pltpu.CompilerParams(
            dimension_semantics=("arbitrary",), vmem_limit_bytes=WHOLE_VMEM
        ),
    )(row_counts, rows_in, cotangent, gate_row)


def add_slots(place_ref, grads_ref, total):
    def add(s, _):
        e = place_ref[s]
        total[e] = total[e] + grads_ref[s].astype(jnp.float32)
        return 0

    lax.fori_loop(0, grads_ref.shape[0], add, 0, unroll=8)


def rows_step(rows):
    return max(d for d in (16, 32, 48) if rows % d == 0)


def update_kernel(
    old_ref, new_ref, grads_ref, master_ref, one_ref, two_ref,
    master_out, one_out, two_out, fresh_ref, send_ref, total,
):
    total[...] = jnp.zeros_like(total)
    add_slots(old_ref, grads_ref, total)
    grad = total[...]
    first = beta_one * one_ref[...].astype(jnp.float32) + (1.0 - beta_one) * grad
    second = beta_two * two_ref[...].astype(jnp.float32) + (1.0 - beta_two) * grad * grad
    master = master_ref[...] - (learn_rate / fix_one) * first / (
        jnp.sqrt(second * (1.0 / fix_two)) + adam_eps
    )
    master_out[...] = master
    one_out[...] = first.astype(jnp.bfloat16)
    two_out[...] = second.astype(jnp.bfloat16)
    fresh_ref[...] = master.astype(jnp.bfloat16)

    def pick(s, _):
        send_ref[s] = fresh_ref[new_ref[s]]
        return 0

    lax.fori_loop(0, send_ref.shape[0], pick, 0, unroll=8)


def update(old, new, grads, master, one, two):
    slots, rows, cols = grads.shape
    experts = master.shape[0]
    step = rows_step(rows)
    state = pl.BlockSpec((experts, step, cols), lambda i, a, b: (0, i, 0))
    wide = pl.BlockSpec((slots, step, cols), lambda i, a, b: (0, i, 0))
    near = pl.BlockSpec((new.shape[0], step, cols), lambda i, a, b: (0, i, 0))
    return pl.pallas_call(
        update_kernel,
        name="update",
        out_shape=(
            jax.ShapeDtypeStruct(master.shape, jnp.float32),
            jax.ShapeDtypeStruct(master.shape, jnp.bfloat16),
            jax.ShapeDtypeStruct(master.shape, jnp.bfloat16),
            jax.ShapeDtypeStruct(master.shape, jnp.bfloat16),
            jax.ShapeDtypeStruct(new.shape + (rows, cols), jnp.bfloat16),
        ),
        grid_spec=pltpu.PrefetchScalarGridSpec(
            num_scalar_prefetch=2,
            grid=(rows // step,),
            in_specs=[wide, state, state, state],
            out_specs=[state, state, state, state, near],
            scratch_shapes=[pltpu.VMEM((experts, step, cols), jnp.float32)],
        ),
        compiler_params=pltpu.CompilerParams(
            dimension_semantics=("arbitrary",), vmem_limit_bytes=WHOLE_VMEM
        ),
    )(old, new, grads, master, one, two)


def next_kernel(half_ref, rows_ref, weight_ref, *rest):
    out_ref = rest[-1]
    cols = weight_ref.shape[2]
    for i in range(2):
        out_ref[:, i * cols : (i + 1) * cols] = jnp.dot(
            rows_ref[...],
            weight_ref[2 * pl.program_id(0) + i],
            preferred_element_type=jnp.float32,
        ).astype(jnp.bfloat16)


def next_rows(half, rows_next, weight, so_far=None):
    inner, _, cols = weight.shape
    rows = rows_next.shape[0]
    pair = inner // 2
    more = () if so_far is None else (so_far,)
    return pl.pallas_call(
        next_kernel,
        name="next_rows",
        out_shape=jax.ShapeDtypeStruct((rows, 2 * inner * cols), jnp.bfloat16),
        grid_spec=pltpu.PrefetchScalarGridSpec(
            num_scalar_prefetch=1,
            grid=(pair,),
            in_specs=[pl.BlockSpec(memory_space=pltpu.VMEM)] * 2
            + [pl.BlockSpec(memory_space=pl.ANY)] * len(more),
            out_specs=pl.BlockSpec((rows, 2 * cols), lambda g, h: (0, h[0] * pair + g)),
        ),
        input_output_aliases={3: 0} if more else {},
        compiler_params=pltpu.CompilerParams(
            dimension_semantics=("arbitrary",), vmem_limit_bytes=WHOLE_VMEM
        ),
    )(half, rows_next, weight, *more)


def half_pick_kernel(wanted_ref, block_ref, out_ref):
    def pick(p, _):
        out_ref[p] = block_ref[wanted_ref[p]]
        return 0

    lax.fori_loop(0, out_ref.shape[0], pick, 0, unroll=4)


def half_picked(wanted, block):
    return pl.pallas_call(
        half_pick_kernel,
        name="half_picked",
        out_shape=jax.ShapeDtypeStruct(wanted.shape + block.shape[1:], jnp.bfloat16),
        in_specs=[
            pl.BlockSpec(memory_space=pltpu.SMEM),
            pl.BlockSpec(memory_space=pltpu.VMEM),
        ],
        out_specs=pl.BlockSpec(memory_space=pltpu.VMEM),
        compiler_params=pltpu.CompilerParams(vmem_limit_bytes=WHOLE_VMEM),
    )(wanted, block)


def along_line(mine, line, wide):
    low, high, lows, highs = mine, mine, [], []
    for turn in range(line - 1):
        ups = [(g, g + wide) for g in range(turn * wide, (line - 1) * wide)]
        downs = [(g + wide, g) for g in range((line - 1 - turn) * wide)]
        low = lax.ppermute(low, LINE, ups)
        high = lax.ppermute(high, LINE, downs)
        lows.append(low)
        highs.append(high)
    return lows, highs


def pick_kernel(pairs, plane_ref, wanted_ref, *rest):
    count = sum(2 if p else 1 for p in pairs)
    blocks, outs, sems = rest[:count], rest[count:-1], rest[-1]
    for j, out in enumerate(outs):
        at = 0
        for i, reach in enumerate(pairs):
            if not reach:
                pltpu.make_async_copy(
                    blocks[at].at[wanted_ref[j]], out.at[i], sems.at[j]
                ).start()
                at += 1
                continue
            for side in range(2):

                @pl.when((plane_ref[0] >= reach) == (side == 0))
                def _(block=blocks[at + side], out=out, i=i, j=j):
                    pltpu.make_async_copy(
                        block.at[wanted_ref[j]], out.at[i], sems.at[j]
                    ).start()

            at += 2
    for j, out in enumerate(outs):
        pltpu.make_async_copy(out, out, sems.at[j]).wait()


def picked(plane, wanted, entries, held=False):
    pairs = [entry[2] if len(entry) == 3 else 0 for entry in entries]
    blocks = [block for entry in entries for block in entry[:2]]
    piece = (len(entries),) + blocks[0].shape[1:]
    peers = wanted.shape[0]
    return pl.pallas_call(
        functools.partial(held_pick_kernel if held else pick_kernel, pairs),
        name="picked",
        out_shape=[jax.ShapeDtypeStruct(piece, jnp.bfloat16)] * peers,
        in_specs=[pl.BlockSpec(memory_space=pltpu.SMEM)] * 2
        + [pl.BlockSpec(memory_space=pltpu.VMEM if held else pl.ANY)] * len(blocks),
        out_specs=[pl.BlockSpec(memory_space=pltpu.VMEM)] * peers,
        scratch_shapes=[] if held else [pltpu.SemaphoreType.DMA((peers,))],
        compiler_params=pltpu.CompilerParams(vmem_limit_bytes=WHOLE_VMEM),
    )(plane, wanted, *blocks)


def held_pick_kernel(pairs, plane_ref, wanted_ref, *rest):
    count = sum(2 if p else 1 for p in pairs)
    blocks, outs = rest[:count], rest[count:]
    at = 0
    for i, reach in enumerate(pairs):
        if not reach:
            for j, out in enumerate(outs):
                out[i] = blocks[at][wanted_ref[j]]
            at += 1
            continue
        for side in range(2):

            @pl.when((plane_ref[0] >= reach) == (side == 0))
            def _(block=blocks[at + side], i=i):
                for j, out in enumerate(outs):
                    out[i] = block[wanted_ref[j]]

        at += 2


def among_peers(picks, peers, devices):
    parts = [picks[0]]
    for j in range(1, peers):
        pairs = [(p, p - p % peers + (p % peers ^ j)) for p in range(devices)]
        parts.append(lax.ppermute(picks[j], ALL, pairs))
    return parts


def back_kernel(wide, peers, slot_count, last, me_ref, plane_ref, valid_ref, *rest):
    parts, rest = rest[:peers], rest[peers:]
    cot_ref, rest = rest[0], rest[1:]
    if last:
        count_ref, rows_ref, gate_ref, so_far, grad_ref, gate_out, total, held, sems = rest
    elif len(rest) == 4:
        so_far, total, held, sems = rest
    else:
        so_far, (total, held, sems) = None, rest
    i = pl.program_id(0)

    @pl.when(i == 0)
    def _():
        copies = [pltpu.make_async_copy(part, held.at[j], sems.at[j]) for j, part in enumerate(parts)]
        for copy in copies:
            copy.start()
        total[...] = jnp.zeros_like(total) if so_far is None else so_far[...]
        for copy in copies:
            copy.wait()

    @pl.when(valid_ref[i // wide] == 1)
    def _():
        weight = jnp.concatenate(
            [
                held[((i % wide) * slot_count + k) ^ me_ref[0], i // wide]
                for k in range(slot_count)
            ],
            axis=0,
        )
        total[...] += lax.dot_general(
            cot_ref[...], weight, (((1,), (1,)), ((), ())), preferred_element_type=jnp.float32
        )

    if last:

        @pl.when(i == pl.num_programs(0) - 1)
        def _():
            rows = rows_ref.shape[0]
            live = lax.broadcasted_iota(jnp.int32, (rows, 1), 0) < count_ref[0]
            back = jnp.where(live, total[...], 0.0)
            grad_ref[...] = (column_of(gate_ref[...]) * back).astype(jnp.bfloat16)
            summed = jnp.sum(rows_ref[...].astype(jnp.float32) * back, axis=1, keepdims=True)
            gate_out[...] = jnp.transpose(jnp.broadcast_to(summed, (rows, 128)))[:1]


def back(me, planes, valid, cotangent, parts, wide, slot_count, so_far=None, last=None):
    peers = len(parts)
    entries, part_rows, cols = parts[0].shape
    rows, ff = cotangent.shape[0], slot_count * part_rows
    whole = pl.BlockSpec((rows, ff), lambda i, *_: (0, 0))
    row = pl.BlockSpec((1, rows), lambda i, *_: (0, 0))

    def taken(i, m, plane, *_):
        return (0, plane[i // wide] * wide + i % wide)

    total = jax.ShapeDtypeStruct((rows, ff), jnp.float32)
    specs = [pl.BlockSpec(memory_space=pl.ANY)] * peers + [pl.BlockSpec((rows, cols), taken)]
    scratch = [
        pltpu.VMEM((peers, entries, part_rows, cols), jnp.bfloat16),
        pltpu.SemaphoreType.DMA((peers,)),
    ]
    more = ()
    if last is not None:
        specs += [pl.BlockSpec(memory_space=pltpu.SMEM), whole, row]
        more = last
        total = (
            jax.ShapeDtypeStruct((rows, ff), jnp.bfloat16),
            jax.ShapeDtypeStruct((1, rows), jnp.float32),
        )
        scratch = [pltpu.VMEM((rows, ff), jnp.float32)] + scratch
    if so_far is not None:
        specs.append(whole)
        more += (so_far,)
    return pl.pallas_call(
        functools.partial(back_kernel, wide, peers, slot_count, last is not None),
        name="back",
        out_shape=total,
        grid_spec=pltpu.PrefetchScalarGridSpec(
            num_scalar_prefetch=3,
            grid=(entries * wide,),
            in_specs=specs,
            out_specs=whole if last is None else [whole, row],
            scratch_shapes=scratch,
        ),
        compiler_params=pltpu.CompilerParams(
            dimension_semantics=("arbitrary",), vmem_limit_bytes=WHOLE_VMEM
        ),
    )(me, planes, valid, *parts, cotangent, *more)


def exchange(blocks, axes):
    return lax.all_to_all(blocks, axes, split_axis=0, concat_axis=0, tiled=True)


def across(block):
    return lax.ppermute(block, "half", [(0, 1), (1, 0)])


def shards(
    rows_in, cotangent, gate_prob, row_counts, old_place, new_place, rows_next,
    master, moment_one, moment_two,
):
    inner, slot_count = lax.axis_size("inner"), lax.axis_size("slot")
    group_count, near_count = 2 * inner, inner * slot_count
    devices = group_count * slot_count
    _, part_rows, part_cols = master.shape
    ff = slot_count * part_rows
    wide = 2
    line = group_count // wide
    peers = wide * slot_count
    half = lax.axis_index("half")
    g_own, k_own = half * inner + lax.axis_index("inner"), lax.axis_index("slot")
    plane = g_own // wide
    me = (g_own % wide) * slot_count + k_own
    old = old_place[:, 0]
    new = lax.dynamic_slice(new_place[:, 0], (half * near_count,), (near_count,))
    gate_row = gate_prob.reshape(1, -1)
    own, other = half.reshape(1), (1 - half).reshape(1)
    me_one, plane_one = me.reshape(1), plane.reshape(1)

    mine = master.astype(jnp.bfloat16)
    lows, highs = along_line(mine, line, wide)
    wanted = lax.dynamic_slice(old, (plane * peers,), (peers,))[
        me ^ jnp.arange(peers, dtype=jnp.int32)
    ]
    sets = {"near": ([(mine,)], [0]), "mid": ([], []), "far": ([], [])}
    for r in range(1, line):
        blocks, offs = sets["near" if r == 1 else "far" if r == line - 1 else "mid"]
        if 2 * r < line:
            blocks += [(lows[r - 1],), (highs[r - 1],)]
            offs += [-r, r]
        else:
            blocks.append((lows[r - 1], highs[r - 1], r))
            offs.append(jnp.where(plane >= r, -r, r))

    def table(offs):
        at = plane + jnp.stack([jnp.asarray(o, jnp.int32) for o in offs])
        valid = (at >= 0) & (at < line)
        return jnp.clip(at, 0, line - 1), valid.astype(jnp.int32)

    def back_part(name, so_far, last=None):
        blocks, offs = sets[name]
        parts = among_peers(picked(plane_one, wanted, blocks, name == "far"), peers, devices)
        return back(me_one, *table(offs), cotangent, parts, wide, slot_count, so_far, last)

    grads = slot_grads(row_counts, rows_in, cotangent, gate_row, group_count)
    arrived = exchange(grads.reshape(-1, part_rows, part_cols), ALL)
    so_far = back_part("near", None)
    new_master, new_first, new_second, fresh, send = update(
        old, new, arrived, master, moment_one, moment_two
    )
    weight = exchange(send, HALF).reshape(inner, ff, part_cols)
    fresh = across(fresh)
    so_far = back_part("mid", so_far)
    next_out = next_rows(own, rows_next, weight)
    picks = half_picked(new, fresh)
    weight = exchange(picks, HALF).reshape(inner, ff, part_cols)
    input_grad, gate_grad = back_part("far", so_far, (row_counts, rows_in, gate_row))
    next_out = next_rows(other, rows_next, weight, next_out)
    return input_grad, gate_grad.reshape(-1), new_master, new_first, new_second, next_out


def solution(mesh):
    groups, slot_count = mesh.devices.shape
    mesh = Mesh(mesh.devices.reshape(2, groups // 2, slot_count), ALL)
    rows = P(ALL, None)
    row = P(ALL)
    state = P(None, "slot", ("half", "inner"))
    return jax.shard_map(
        shards,
        mesh=mesh,
        in_specs=(rows, rows, row, row, P(), P(), rows, state, state, state),
        out_specs=(rows, row, state, state, state, rows),
        check_vma=False,
    )
```

time: 275 us -> 281 us (1.022)
  blocking collectives: 78.6 us -> 0 us
  waiting for transfers between devices: 114 us -> 172 us
  starting transfers between devices: 30.9 us -> 51.1 us
  Pallas kernels: 40.3 us -> 50.6 us
  local copies, waits for them, and re-layouts: 6.96 us -> 1.91 us
    all_to_all x1 -> x0, blocking collectives: 78.6 us -> none  [exchange(): return lax.all_to_all(blocks, BOTH, split_axis=0, concat_axis=0, tiled=True)]
    all_to_all x1 -> x3, waiting for transfers between devices: 0.01 us -> 72.3 us  [exchange(): return lax.all_to_all(blocks, axes, split_axis=0, concat_axis=0, tiled=True)]
    all_to_all x1 -> x3, starting transfers between devices: 3.78 us -> 18.8 us  [exchange(): return lax.all_to_all(blocks, axes, split_axis=0, concat_axis=0, tiled=True)]
    ppermute x20 -> x28, waiting for transfers between devices: 114 us -> 100 us  [the longest x3 43.1 us: along_line(): high = lax.ppermute(high, LINE, downs)]
    pallas_call x4 -> x7, Pallas kernels: 20.7 us -> 29.4 us  [the longest x3 18 us: back(): pl.pallas_call(functools.partial(back_kernel, wide, peers, slot_count, la...]
    unnamed x34 -> x12, local copies, waits for them, and re-layouts: 5.65 us -> 0.03 us
    ppermute x20 -> x28, starting transfers between devices: 27.1 us -> 32.4 us  [the longest x21 18 us: among_peers(): parts.append(lax.ppermute(picks[j], ALL, pairs))]
    pallas_call x1 -> x2, Pallas kernels: 5.31 us -> 7.27 us  [next_rows(): pl.pallas_call(next_kernel, name='next_rows', out_shape=jax.ShapeDtypeStr...]
  transfers between devices with their start and end apart: 21 -> 31, of which waited for: 11 -> 15; matrix products, arithmetic and copies ran while one was open for 2% -> 1% of each run, Pallas kernels for 8% -> 12%
where the time goes in v3:
time: 281 us; the launch traced here: 279 us
  waiting for transfers between devices  172 us (61%)
  starting transfers between devices  51.1 us (18%)
  Pallas kernels  50.6 us (18%)
    all_to_all x3, waiting for transfers between devices, exchange(): return lax.all_to_all(blocks, axes, split_axis=0, concat_axis=0, tiled=True)  72.3 us
    ppermute x3, waiting for transfers between devices, along_line(): high = lax.ppermute(high, LINE, downs)  43.1 us
    ppermute x1, waiting for transfers between devices, across(): return lax.ppermute(block, 'half', [(0, 1), (1, 0)])  33 us
    ppermute x21, waiting for transfers between devices, among_peers(): parts.append(lax.ppermute(picks[j], ALL, pairs))  24 us
    all_to_all x3, starting transfers between devices, exchange(): return lax.all_to_all(blocks, axes, split_axis=0, concat_axis=0, tiled=True)  18.8 us
    pallas_call x3, Pallas kernels, back(): pl.pallas_call(functools.partial(back_kernel, wide, peers, slot_count, la...  18 us
    ppermute x21, starting transfers between devices, among_peers(): parts.append(lax.ppermute(picks[j], ALL, pairs))  18 us
    pallas_call x3, Pallas kernels, picked(): pl.pallas_call(functools.partial(held_pick_kernel if held else pick_kerne...  8.97 us
  transfers between devices with their start and end apart: 31, of which 15 were waited for; matrix products, arithmetic and copies ran while one was open for 1% of the time, Pallas kernels for 12%

profile of v3, /device:TPU:0, one launch (start us, length us, event | category | flops | bytes accessed | tf_op | source)
XLA Modules:
  0.0 278.8 jit_solution(5188477305283198283)
XLA Ops:
  0.6 0.0 copy-start
  1.3 6.4 %slot_grads.1 = bf16[8,768,256]{2,1,0:T(8,128)(2,1)} custom-call(s32[1]{0:T(128)S(6)} %copy.18.rest_9_.count_ref, bf16[512,768]{1,0:T(8,128)(2,1)} %rows_ref.3, bf16[512,2048]{1,0:T(8,128)(2,1)} %cot_ref.1, f32[1,512]{1,0:T(1,128)} %bitcast.19), custom_call_target="tpu_custom_call" | custom-call | tf_op jit(solution)/shard_map/slot_grads/pallas_call | solution.py:52
  7.7 7.4 %all-to-all-start = ((bf16[32,192,256]{2,1,0:T(8,128)(2,1)}), bf16[32,192,256]{2,1,0:T(8,128)(2,1)}, u32[]{:S(2)}, u32[]{:S(2)}) async-start(bf16[32,192,256]{2,1,0:T(8,128)(2,1)} %bitcast.18), calls=%async_computation | async-start | bytes 6291456 | tf_op jit(solution)/shard_map/all_to_all | solution.py:369
  15.2 0.6 dynamic-slice_bitcast_fusion.new_ref.wanted_ref
  15.8 71.0 %all-to-all-done.grads_ref = bf16[32,192,256]{2,1,0:T(8,128)(2,1)} async-done(((bf16[32,192,256]{2,1,0:T(8,128)(2,1)}), bf16[32,192,256]{2,1,0:T(8,128)(2,1)}, u32[]{:S(2)}, u32[]{:S(2)}) %all-to-all-start) | async-done | bytes 3145760 | tf_op jit(solution)/shard_map/all_to_all | solution.py:369
  86.7 7.5 %update.1 = (f32[8,192,256]{2,1,0:T(8,128)}, bf16[8,192,256]{2,1,0:T(8,128)(2,1)}, bf16[8,192,256]{2,1,0:T(8,128)(2,1)}, bf16[8,192,256]{2,1,0:T(8,128)(2,1)}, bf16[16,192,256]{2,1,0:T(8,128)(2,1)}) custom-call(s32[32]{0:T(128)} %bitcast.21, s32[16]{0:T(128)} %dynamic-slice_bitcast_fusion.new_ref.wanted_ref, bf16[32,192,256]{2,1,0:T(8,128)(2,1)} %all-to-all-done.grads_ref, ...), custom_call_target="tpu_custom_call" | custom-call | tf_op jit(solution)/shard_map/update/pallas_call | solution.py:117
  94.3 4.5 %all-to-all-start.2 = ((bf16[16,192,256]{2,1,0:T(8,128)(2,1)}), bf16[16,192,256]{2,1,0:T(8,128)(2,1)}, u32[]{:S(2)}, u32[]{:S(2)}) async-start(bf16[16,192,256]{2,1,0:T(8,128)(2,1)} %get-tuple-element.67), calls=%async_computation.2 | async-start | bytes 3145728 | tf_op jit(solution)/shard_map/all_to_all | solution.py:369
  98.8 1.9 collective-permute-start.27
  100.7 33.0 %collective-permute-done.27.block_ref = bf16[8,192,256]{2,1,0:T(8,128)(2,1)} collective-permute-done((bf16[8,192,256]{2,1,0:T(8,128)(2,1)S(1)}, bf16[8,192,256]{2,1,0:T(8,128)(2,1)}, u32[]{:S(2)}, u32[]{:S(2)}) %collective-permute-start.27) | collective-permute-done | bytes 786464 | tf_op jit(solution)/shard_map/ppermute | solution.py:373
  133.7 2.4 half_picked.1
  136.2 1.3 all-to-all-done.2
  137.5 6.8 %all-to-all-start.1 = ((bf16[16,192,256]{2,1,0:T(8,128)(2,1)}), bf16[16,192,256]{2,1,0:T(8,128)(2,1)}, u32[]{:S(2)}, u32[]{:S(2)}) async-start(bf16[16,192,256]{2,1,0:T(8,128)(2,1)} %half_picked.1), calls=%async_computation.1 | async-start | bytes 3145728 | tf_op jit(solution)/shard_map/all_to_all | solution.py:369
  144.3 0.0 copy-start.3
  144.3 0.1 convert_element_type.13.rest_0_
  144.4 0.0 copy-start.2
  144.4 1.3 collective-permute-start.3
  145.7 5.5 %collective-permute-start = (bf16[8,192,256]{2,1,0:T(8,128)(2,1)S(1)}, bf16[8,192,256]{2,1,0:T(8,128)(2,1)}, u32[]{:S(2)}, u32[]{:S(2)}) collective-permute-start(bf16[8,192,256]{2,1,0:T(8,128)(2,1)S(1)} %convert_element_type.13.rest_0_), channel_id=1, source_target_pairs={{0,8},{4,12},{8,16},{12,20},{16,24},{20,28},{1,9},{5,13},{9,17},{1... | collective-permute-start | bytes 2359304 | tf_op jit(solution)/shard_map/ppermute | solution.py:201
  151.2 30.0 %collective-permute-done.3.rest_2_ = bf16[8,192,256]{2,1,0:T(8,128)(2,1)} collective-permute-done((bf16[8,192,256]{2,1,0:T(8,128)(2,1)S(1)}, bf16[8,192,256]{2,1,0:T(8,128)(2,1)}, u32[]{:S(2)}, u32[]{:S(2)}) %collective-permute-start.3) | collective-permute-done | bytes 786464 | tf_op jit(solution)/shard_map/ppermute | solution.py:202
  181.2 1.3 collective-permute-start.4
  182.5 0.0 collective-permute-done.rest_1_
  182.5 1.6 collective-permute-start.1
  184.1 0.1 dynamic-slice_bitcast_fusion.1
  184.2 1.2 gather_fusion
  185.4 3.8 %picked.5 = (bf16[3,192,256]{2,1,0:T(8,128)(2,1)}, bf16[3,192,256]{2,1,0:T(8,128)(2,1)}, bf16[3,192,256]{2,1,0:T(8,128)(2,1)}, bf16[3,192,256]{2,1,0:T(8,128)(2,...) custom-call(s32[1]{0:T(128)} %bitcast.1.plane_ref, ...), custom_call_target="tpu_custom_call" | custom-call | tf_op jit(solution)/shard_map/picked/pallas_call | solution.py:238
  189.3 0.1 collective-permute-start.20
  189.3 13.1 %collective-permute-done.4.rest_1_ = bf16[8,192,256]{2,1,0:T(8,128)(2,1)} collective-permute-done((bf16[8,192,256]{2,1,0:T(8,128)(2,1)}, bf16[8,192,256]{2,1,0:T(8,128)(2,1)}, u32[]{:S(2)}, u32[]{:S(2)}) %collective-permute-start.4) | collective-permute-done | bytes 786464 | tf_op jit(solution)/shard_map/ppermute | solution.py:202
  202.4 1.3 collective-permute-start.5
  203.7 0.0 collective-permute-done.1.rest_0_
  203.7 1.6 collective-permute-start.2
  205.3 2.9 %collective-permute-start.21 = (bf16[3,192,256]{2,1,0:T(8,128)(2,1)}, bf16[3,192,256]{2,1,0:T(8,128)(2,1)}, u32[]{:S(2)}, u32[]{:S(2)}) collective-permute-start(bf16[3,192,256]{2,1,0:T(8,128)(2,1)} %get-tuple-element.55), channel_id=1, source_target_pairs={{0,2},{1,3},{2,0},{3,1},{4,6},{5,7},{6,4},{7,5},{8,10},{9,11},{10,... | collective-permute-start | bytes 884744 | tf_op jit(solution)/shard_map/ppermute | solution.py:274
  208.2 0.9 collective-permute-start.23
  209.1 7.2 %collective-permute-done.21.rest_2_ = bf16[3,192,256]{2,1,0:T(8,128)(2,1)} collective-permute-done((bf16[3,192,256]{2,1,0:T(8,128)(2,1)}, bf16[3,192,256]{2,1,0:T(8,128)(2,1)}, u32[]{:S(2)}, u32[]{:S(2)}) %collective-permute-start.21) | collective-permute-done | bytes 294944 | tf_op jit(solution)/shard_map/ppermute | solution.py:274
  216.3 3.6 %collective-permute-done.22.rest_3_ = bf16[3,192,256]{2,1,0:T(8,128)(2,1)} collective-permute-done((bf16[3,192,256]{2,1,0:T(8,128)(2,1)}, bf16[3,192,256]{2,1,0:T(8,128)(2,1)}, u32[]{:S(2)}, u32[]{:S(2)}) %collective-permute-start.22) | collective-permute-done | bytes 294944 | tf_op jit(solution)/shard_map/ppermute | solution.py:274
  219.9 0.7 collective-permute-start.25
  220.6 2.4 collective-permute-start.26
  223.0 2.8 %picked.4 = (bf16[1,192,256]{2,1,0:T(8,128)(2,1)}, bf16[1,192,256]{2,1,0:T(8,128)(2,1)}, bf16[1,192,256]{2,1,0:T(8,128)(2,1)}, bf16[1,192,256]{2,1,0:T(8,128)(2,...) custom-call(s32[1]{0:T(128)} %bitcast.1.plane_ref, ...), custom_call_target="tpu_custom_call" | custom-call | tf_op jit(solution)/shard_map/picked/pallas_call | solution.py:238
  225.9 0.1 collective-permute-done.24.rest_5_
  226.0 6.8 %collective-permute-done.25.rest_6_ = bf16[3,192,256]{2,1,0:T(8,128)(2,1)} collective-permute-done((bf16[3,192,256]{2,1,0:T(8,128)(2,1)}, bf16[3,192,256]{2,1,0:T(8,128)(2,1)}, u32[]{:S(2)}, u32[]{:S(2)}) %collective-permute-start.25) | collective-permute-done | bytes 294944 | tf_op jit(solution)/shard_map/ppermute | solution.py:274
  232.7 0.0 collective-permute-start.14
  232.7 2.2 collective-permute-start.15
  234.9 0.9 collective-permute-start.16
  235.9 2.3 picked.3
  238.2 1.9 collective-permute-done.26.rest_7_
  240.1 0.2 collective-permute-start.18
  240.3 1.4 collective-permute-done.14.rest_2_
  241.7 1.8 collective-permute-start.19
  243.4 0.3 collective-permute-done.15.rest_3_
  243.8 0.1 collective-permute-start.6
  243.9 0.5 collective-permute-start.7
  244.4 0.6 and_convert_fusion.valid_ref
  245.0 0.6 collective-permute-done.17.rest_5_
  245.5 0.7 collective-permute-start.8
  246.2 0.7 collective-permute-done.18.rest_6_
  246.9 0.8 collective-permute-start.9
  247.7 1.5 collective-permute-done.19.rest_7_
  249.2 0.4 collective-permute-start.10
  249.6 1.9 collective-permute-start.11
  251.4 1.6 collective-permute-start.12
  253.0 0.5 add_clamp_fusion.plane_ref
  253.5 7.7 %back.3.rest_9_ = f32[512,768]{1,0:T(8,128)} custom-call(s32[1]{0:T(128)} %bitcast.me_ref, s32[3]{0:T(128)} %add_clamp_fusion.plane_ref, s32[3]{0:T(128)} %and_convert_fusion.valid_ref, bf16[3,192,256]{2,1,0:T(8,128)(2,1)} %get-tuple-element.53.rest_0_, bf16[3,192,256]{2,1,0:T(8,128)(2,1)} %collective-permute-done.20.rest_1_, ...), custom_call_target="tpu_custom_call" | custom-call | tf_op jit(solution)/shard_map/back/pallas_call | solution.py:351
  261.2 4.9 %back.4.rest_12_ = f32[512,768]{1,0:T(8,128)} custom-call(s32[1]{0:T(128)} %bitcast.me_ref, s32[1]{0:T(128)S(6)} %min.19.plane_ref, s32[1]{0:T(128)S(6)} %convert_element_type.14.valid_ref, bf16[1,192,256]{2,1,0:T(8,128)(2,1)} %get-tuple-element.45.rest_0_, bf16[1,192,256]{2,1,0:T(8,128)(2,1)} %collective-permute-done.13.rest_1_, ...), custom_call_target="tpu_custom_call" | custom-call | tf_op jit(solution)/shard_map/back/pallas_call | solution.py:351
  266.1 5.4 %back.5 = (bf16[512,768]{1,0:T(8,128)(2,1)}, f32[1,512]{1,0:T(1,128)}) custom-call(s32[1]{0:T(128)} %bitcast.me_ref, s32[1]{0:T(128)S(6)} %min.18.plane_ref, s32[1]{0:T(128)S(6)} %convert_element_type.12.valid_ref, bf16[1,192,256]{2,1,0:T(8,128)(2,1)} %get-tuple-element.37.rest_0_, bf16[1,192,256]{2,1,0:T(8,128)(2,1)} %collective-permute-done.6.rest_1_, ...), custom_call_target="tpu_custom_call" | custom-call | tf_op jit(solution)/shard_map/back/pallas_call | solution.py:351
  271.6 3.7 %next_rows.2.rest_0_ = bf16[512,2048]{1,0:T(8,128)(2,1)} custom-call(s32[1]{0:T(128)} %bitcast.13.half_ref, bf16[512,768]{1,0:T(8,128)(2,1)} %rows_ref.5, bf16[4,768,256]{2,1,0:T(8,128)(2,1)} %bitcast.14.weight_ref), custom_call_target="tpu_custom_call" | custom-call | tf_op jit(solution)/shard_map/next_rows/pallas_call | solution.py:156
  275.2 3.6 %next_rows.3 = bf16[512,2048]{1,0:T(8,128)(2,1)} custom-call(s32[1]{0:T(128)} %bitcast.11.half_ref, bf16[512,768]{1,0:T(8,128)(2,1)} %rows_ref.5, bf16[4,768,256]{2,1,0:T(8,128)(2,1)} %bitcast.12.weight_ref, bf16[512,2048]{1,0:T(8,128)(2,1)} %next_rows.2.rest_0_), custom_call_target="tpu_custom_call", output_to_operand_aliasing={{}: (3, {})} | custom-call | tf_op jit(solution)/shard_map/next_rows/pallas_call | solution.py:156
  (29 shorter events, 0.1 us)
Async XLA Ops:
  0.6 14.5 %copy-start = (s32[32,1]{0,1:T(1,128)S(1)}, s32[32,1]{0,1:T(1,128)}, u32[]{:S(2)}) copy-start(s32[32,1]{0,1:T(1,128)} %param.15) | copy-start | bytes 388
  7.7 79.1 %all-to-all-start = ((bf16[32,192,256]{2,1,0:T(8,128)(2,1)}), bf16[32,192,256]{2,1,0:T(8,128)(2,1)}, u32[]{:S(2)}, u32[]{:S(2)}) async-start(bf16[32,192,256]{2,1,0:T(8,128)(2,1)} %bitcast.18), calls=%async_computation | async-start | bytes 6291456 | tf_op jit(solution)/shard_map/all_to_all | solution.py:369
  94.3 4.5 %copy-start.4 = (bf16[8,192,256]{2,1,0:T(8,128)(2,1)S(1)}, bf16[8,192,256]{2,1,0:T(8,128)(2,1)}, u32[]{:S(2)}) copy-start(bf16[8,192,256]{2,1,0:T(8,128)(2,1)} %get-tuple-element.66) | copy-start | bytes 2359300
  94.3 43.2 %all-to-all-start.2 = ((bf16[16,192,256]{2,1,0:T(8,128)(2,1)}), bf16[16,192,256]{2,1,0:T(8,128)(2,1)}, u32[]{:S(2)}, u32[]{:S(2)}) async-start(bf16[16,192,256]{2,1,0:T(8,128)(2,1)} %get-tuple-element.67), calls=%async_computation.2 | async-start | bytes 3145728 | tf_op jit(solution)/shard_map/all_to_all | solution.py:369
  98.8 34.9 %collective-permute-start.27 = (bf16[8,192,256]{2,1,0:T(8,128)(2,1)S(1)}, bf16[8,192,256]{2,1,0:T(8,128)(2,1)}, u32[]{:S(2)}, u32[]{:S(2)}) collective-permute-start(bf16[8,192,256]{2,1,0:T(8,128)(2,1)S(1)} %copy-done.4), channel_id=1, source_target_pairs={{0,16},{16,0},{1,17},{17,1},{2,18},{18,2},{3,19},{19,3},{4,20},{20... | collective-permute-start | bytes 2359304 | tf_op jit(solution)/shard_map/ppermute | solution.py:373
  136.2 8.1 %copy-start.1 = (f32[8,192,256]{2,1,0:T(8,128)S(1)}, f32[8,192,256]{2,1,0:T(8,128)}, u32[]{:S(2)}) copy-start(f32[8,192,256]{2,1,0:T(8,128)} %master_ref.1) | copy-start | bytes 4718596
  137.5 137.8 %all-to-all-start.1 = ((bf16[16,192,256]{2,1,0:T(8,128)(2,1)}), bf16[16,192,256]{2,1,0:T(8,128)(2,1)}, u32[]{:S(2)}, u32[]{:S(2)}) async-start(bf16[16,192,256]{2,1,0:T(8,128)(2,1)} %half_picked.1), calls=%async_computation.1 | async-start | bytes 3145728 | tf_op jit(solution)/shard_map/all_to_all | solution.py:369
  144.3 39.9 %copy-start.3 = (s32[32,1]{0,1:T(1,128)S(1)}, s32[32,1]{0,1:T(1,128)}, u32[]{:S(2)}) copy-start(s32[32,1]{0,1:T(1,128)} %param.14) | copy-start | bytes 388
  144.4 1.3 copy-start.2
  144.4 36.8 %collective-permute-start.3 = (bf16[8,192,256]{2,1,0:T(8,128)(2,1)S(1)}, bf16[8,192,256]{2,1,0:T(8,128)(2,1)}, u32[]{:S(2)}, u32[]{:S(2)}) collective-permute-start(bf16[8,192,256]{2,1,0:T(8,128)(2,1)S(1)} %convert_element_type.13.rest_0_), channel_id=1, source_target_pairs={{8,0},{12,4},{16,8},{20,12},{24,16},{28,20},{9,1},{13,5},{17,9},{2... | collective-permute-start | bytes 2359304 | tf_op jit(solution)/shard_map/ppermute | solution.py:202
  145.7 36.8 %collective-permute-start = (bf16[8,192,256]{2,1,0:T(8,128)(2,1)S(1)}, bf16[8,192,256]{2,1,0:T(8,128)(2,1)}, u32[]{:S(2)}, u32[]{:S(2)}) collective-permute-start(bf16[8,192,256]{2,1,0:T(8,128)(2,1)S(1)} %convert_element_type.13.rest_0_), channel_id=1, source_target_pairs={{0,8},{4,12},{8,16},{12,20},{16,24},{20,28},{1,9},{5,13},{9,17},{1... | collective-permute-start | bytes 2359304 | tf_op jit(solution)/shard_map/ppermute | solution.py:201
  181.2 21.2 %collective-permute-start.4 = (bf16[8,192,256]{2,1,0:T(8,128)(2,1)}, bf16[8,192,256]{2,1,0:T(8,128)(2,1)}, u32[]{:S(2)}, u32[]{:S(2)}) collective-permute-start(bf16[8,192,256]{2,1,0:T(8,128)(2,1)} %collective-permute-done.3.rest_2_), channel_id=1, source_target_pairs={{8,0},{12,4},{16,8},{20,12},{9,1},{13,5},{17,9},{21,13},{10,2},{14... | collective-permute-start | bytes 2359304 | tf_op jit(solution)/shard_map/ppermute | solution.py:202
  182.5 21.2 %collective-permute-start.1 = (bf16[8,192,256]{2,1,0:T(8,128)(2,1)}, bf16[8,192,256]{2,1,0:T(8,128)(2,1)}, u32[]{:S(2)}, u32[]{:S(2)}) collective-permute-start(bf16[8,192,256]{2,1,0:T(8,128)(2,1)} %collective-permute-done.rest_1_), channel_id=1, source_target_pairs={{8,16},{12,20},{16,24},{20,28},{9,17},{13,21},{17,25},{21,29},{10,... | collective-permute-start | bytes 2359304 | tf_op jit(solution)/shard_map/ppermute | solution.py:201
  189.3 18.9 %collective-permute-start.20 = (bf16[3,192,256]{2,1,0:T(8,128)(2,1)}, bf16[3,192,256]{2,1,0:T(8,128)(2,1)}, u32[]{:S(2)}, u32[]{:S(2)}) collective-permute-start(bf16[3,192,256]{2,1,0:T(8,128)(2,1)} %get-tuple-element.54), channel_id=1, source_target_pairs={{0,1},{1,0},{2,3},{3,2},{4,5},{5,4},{6,7},{7,6},{8,9},{9,8},{10,11... | collective-permute-start | bytes 884744 | tf_op jit(solution)/shard_map/ppermute | solution.py:274
  202.4 30.3 %collective-permute-start.5 = (bf16[8,192,256]{2,1,0:T(8,128)(2,1)}, bf16[8,192,256]{2,1,0:T(8,128)(2,1)}, u32[]{:S(2)}, u32[]{:S(2)}) collective-permute-start(bf16[8,192,256]{2,1,0:T(8,128)(2,1)} %collective-permute-done.4.rest_1_), channel_id=1, source_target_pairs={{8,0},{12,4},{9,1},{13,5},{10,2},{14,6},{11,3},{15,7}} | collective-permute-start | bytes 2359304 | tf_op jit(solution)/shard_map/ppermute | solution.py:202
  203.7 31.2 %collective-permute-start.2 = (bf16[8,192,256]{2,1,0:T(8,128)(2,1)}, bf16[8,192,256]{2,1,0:T(8,128)(2,1)}, u32[]{:S(2)}, u32[]{:S(2)}) collective-permute-start(bf16[8,192,256]{2,1,0:T(8,128)(2,1)} %collective-permute-done.1.rest_0_), channel_id=1, source_target_pairs={{16,24},{20,28},{17,25},{21,29},{18,26},{22,30},{19,27},{23,31}} | collective-permute-start | bytes 2359304 | tf_op jit(solution)/shard_map/ppermute | solution.py:201
  205.3 11.0 %collective-permute-start.21 = (bf16[3,192,256]{2,1,0:T(8,128)(2,1)}, bf16[3,192,256]{2,1,0:T(8,128)(2,1)}, u32[]{:S(2)}, u32[]{:S(2)}) collective-permute-start(bf16[3,192,256]{2,1,0:T(8,128)(2,1)} %get-tuple-element.55), channel_id=1, source_target_pairs={{0,2},{1,3},{2,0},{3,1},{4,6},{5,7},{6,4},{7,5},{8,10},{9,11},{10,... | collective-permute-start | bytes 884744 | tf_op jit(solution)/shard_map/ppermute | solution.py:274
  208.2 11.8 %collective-permute-start.22 = (bf16[3,192,256]{2,1,0:T(8,128)(2,1)}, bf16[3,192,256]{2,1,0:T(8,128)(2,1)}, u32[]{:S(2)}, u32[]{:S(2)}) collective-permute-start(bf16[3,192,256]{2,1,0:T(8,128)(2,1)} %get-tuple-element.56), channel_id=1, source_target_pairs={{0,3},{1,2},{2,1},{3,0},{4,7},{5,6},{6,5},{7,4},{8,11},{9,10},{10,... | collective-permute-start | bytes 884744 | tf_op jit(solution)/shard_map/ppermute | solution.py:274
  208.2 12.4 %collective-permute-start.23 = (bf16[3,192,256]{2,1,0:T(8,128)(2,1)}, bf16[3,192,256]{2,1,0:T(8,128)(2,1)}, u32[]{:S(2)}, u32[]{:S(2)}) collective-permute-start(bf16[3,192,256]{2,1,0:T(8,128)(2,1)} %get-tuple-element.57), channel_id=1, source_target_pairs={{0,4},{1,5},{2,6},{3,7},{4,0},{5,1},{6,2},{7,3},{8,12},{9,13},{10,... | collective-permute-start | bytes 884744 | tf_op jit(solution)/shard_map/ppermute | solution.py:274
  216.3 9.6 %collective-permute-start.24 = (bf16[3,192,256]{2,1,0:T(8,128)(2,1)}, bf16[3,192,256]{2,1,0:T(8,128)(2,1)}, u32[]{:S(2)}, u32[]{:S(2)}) collective-permute-start(bf16[3,192,256]{2,1,0:T(8,128)(2,1)} %get-tuple-element.58), channel_id=1, source_target_pairs={{0,5},{1,4},{2,7},{3,6},{4,1},{5,0},{6,3},{7,2},{8,13},{9,12},{10,... | collective-permute-start | bytes 884744 | tf_op jit(solution)/shard_map/ppermute | solution.py:274
  219.9 12.8 %collective-permute-start.25 = (bf16[3,192,256]{2,1,0:T(8,128)(2,1)}, bf16[3,192,256]{2,1,0:T(8,128)(2,1)}, u32[]{:S(2)}, u32[]{:S(2)}) collective-permute-start(bf16[3,192,256]{2,1,0:T(8,128)(2,1)} %get-tuple-element.59), channel_id=1, source_target_pairs={{0,6},{1,7},{2,4},{3,5},{4,2},{5,3},{6,0},{7,1},{8,14},{9,15},{10,... | collective-permute-start | bytes 884744 | tf_op jit(solution)/shard_map/ppermute | solution.py:274
  220.6 23.8 %copy-start.5 = (s32[3]{0:T(128)S(1)}, s32[3]{0:T(128)}, u32[]{:S(2)}) copy-start(s32[3]{0:T(128)} %constant.66.clone.1) | copy-start | bytes 40
  220.6 19.5 %collective-permute-start.26 = (bf16[3,192,256]{2,1,0:T(8,128)(2,1)}, bf16[3,192,256]{2,1,0:T(8,128)(2,1)}, u32[]{:S(2)}, u32[]{:S(2)}) collective-permute-start(bf16[3,192,256]{2,1,0:T(8,128)(2,1)} %get-tuple-element.60), channel_id=1, source_target_pairs={{0,7},{1,6},{2,5},{3,4},{4,3},{5,2},{6,1},{7,0},{8,15},{9,14},{10,... | collective-permute-start | bytes 884744 | tf_op jit(solution)/shard_map/ppermute | solution.py:274
  226.0 14.1 %collective-permute-start.13 = (bf16[1,192,256]{2,1,0:T(8,128)(2,1)}, bf16[1,192,256]{2,1,0:T(8,128)(2,1)}, u32[]{:S(2)}, u32[]{:S(2)}) collective-permute-start(bf16[1,192,256]{2,1,0:T(8,128)(2,1)} %get-tuple-element.46), channel_id=1, source_target_pairs={{0,1},{1,0},{2,3},{3,2},{4,5},{5,4},{6,7},{7,6},{8,9},{9,8},{10,11... | collective-permute-start | bytes 294920 | tf_op jit(solution)/shard_map/ppermute | solution.py:274
  232.7 8.9 %collective-permute-start.14 = (bf16[1,192,256]{2,1,0:T(8,128)(2,1)}, bf16[1,192,256]{2,1,0:T(8,128)(2,1)}, u32[]{:S(2)}, u32[]{:S(2)}) collective-permute-start(bf16[1,192,256]{2,1,0:T(8,128)(2,1)} %get-tuple-element.47), channel_id=1, source_target_pairs={{0,2},{1,3},{2,0},{3,1},{4,6},{5,7},{6,4},{7,5},{8,10},{9,11},{10,... | collective-permute-start | bytes 294920 | tf_op jit(solution)/shard_map/ppermute | solution.py:274
  232.7 11.0 %collective-permute-start.15 = (bf16[1,192,256]{2,1,0:T(8,128)(2,1)}, bf16[1,192,256]{2,1,0:T(8,128)(2,1)}, u32[]{:S(2)}, u32[]{:S(2)}) collective-permute-start(bf16[1,192,256]{2,1,0:T(8,128)(2,1)} %get-tuple-element.48), channel_id=1, source_target_pairs={{0,3},{1,2},{2,1},{3,0},{4,7},{5,6},{6,5},{7,4},{8,11},{9,10},{10,... | collective-permute-start | bytes 294920 | tf_op jit(solution)/shard_map/ppermute | solution.py:274
  234.9 9.0 %collective-permute-start.16 = (bf16[1,192,256]{2,1,0:T(8,128)(2,1)}, bf16[1,192,256]{2,1,0:T(8,128)(2,1)}, u32[]{:S(2)}, u32[]{:S(2)}) collective-permute-start(bf16[1,192,256]{2,1,0:T(8,128)(2,1)} %get-tuple-element.49), channel_id=1, source_target_pairs={{0,4},{1,5},{2,6},{3,7},{4,0},{5,1},{6,2},{7,3},{8,12},{9,13},{10,... | collective-permute-start | bytes 294920 | tf_op jit(solution)/shard_map/ppermute | solution.py:274
  240.1 5.4 %collective-permute-start.17 = (bf16[1,192,256]{2,1,0:T(8,128)(2,1)}, bf16[1,192,256]{2,1,0:T(8,128)(2,1)}, u32[]{:S(2)}, u32[]{:S(2)}) collective-permute-start(bf16[1,192,256]{2,1,0:T(8,128)(2,1)} %get-tuple-element.50), channel_id=1, source_target_pairs={{0,5},{1,4},{2,7},{3,6},{4,1},{5,0},{6,3},{7,2},{8,13},{9,12},{10,... | collective-permute-start | bytes 294920 | tf_op jit(solution)/shard_map/ppermute | solution.py:274
  240.1 6.8 %collective-permute-start.18 = (bf16[1,192,256]{2,1,0:T(8,128)(2,1)}, bf16[1,192,256]{2,1,0:T(8,128)(2,1)}, u32[]{:S(2)}, u32[]{:S(2)}) collective-permute-start(bf16[1,192,256]{2,1,0:T(8,128)(2,1)} %get-tuple-element.51), channel_id=1, source_target_pairs={{0,6},{1,7},{2,4},{3,5},{4,2},{5,3},{6,0},{7,1},{8,14},{9,15},{10,... | collective-permute-start | bytes 294920 | tf_op jit(solution)/shard_map/ppermute | solution.py:274
  241.7 7.5 %collective-permute-start.19 = (bf16[1,192,256]{2,1,0:T(8,128)(2,1)}, bf16[1,192,256]{2,1,0:T(8,128)(2,1)}, u32[]{:S(2)}, u32[]{:S(2)}) collective-permute-start(bf16[1,192,256]{2,1,0:T(8,128)(2,1)} %get-tuple-element.52), channel_id=1, source_target_pairs={{0,7},{1,6},{2,5},{3,4},{4,3},{5,2},{6,1},{7,0},{8,15},{9,14},{10,... | collective-permute-start | bytes 294920 | tf_op jit(solution)/shard_map/ppermute | solution.py:274
  243.8 5.8 %collective-permute-start.6 = (bf16[1,192,256]{2,1,0:T(8,128)(2,1)}, bf16[1,192,256]{2,1,0:T(8,128)(2,1)}, u32[]{:S(2)}, u32[]{:S(2)}) collective-permute-start(bf16[1,192,256]{2,1,0:T(8,128)(2,1)} %get-tuple-element.38), channel_id=1, source_target_pairs={{0,1},{1,0},{2,3},{3,2},{4,5},{5,4},{6,7},{7,6},{8,9},{9,8},{10,11... | collective-permute-start | bytes 294920 | tf_op jit(solution)/shard_map/ppermute | solution.py:274
  243.9 7.5 %collective-permute-start.7 = (bf16[1,192,256]{2,1,0:T(8,128)(2,1)}, bf16[1,192,256]{2,1,0:T(8,128)(2,1)}, u32[]{:S(2)}, u32[]{:S(2)}) collective-permute-start(bf16[1,192,256]{2,1,0:T(8,128)(2,1)} %get-tuple-element.39), channel_id=1, source_target_pairs={{0,2},{1,3},{2,0},{3,1},{4,6},{5,7},{6,4},{7,5},{8,10},{9,11},{10,... | collective-permute-start | bytes 294920 | tf_op jit(solution)/shard_map/ppermute | solution.py:274
  245.5 20.6 %collective-permute-start.8 = (bf16[1,192,256]{2,1,0:T(8,128)(2,1)}, bf16[1,192,256]{2,1,0:T(8,128)(2,1)}, u32[]{:S(2)}, u32[]{:S(2)}) collective-permute-start(bf16[1,192,256]{2,1,0:T(8,128)(2,1)} %get-tuple-element.40), channel_id=1, source_target_pairs={{0,3},{1,2},{2,1},{3,0},{4,7},{5,6},{6,5},{7,4},{8,11},{9,10},{10,... | collective-permute-start | bytes 294920 | tf_op jit(solution)/shard_map/ppermute | solution.py:274
  246.9 19.2 %collective-permute-start.9 = (bf16[1,192,256]{2,1,0:T(8,128)(2,1)}, bf16[1,192,256]{2,1,0:T(8,128)(2,1)}, u32[]{:S(2)}, u32[]{:S(2)}) collective-permute-start(bf16[1,192,256]{2,1,0:T(8,128)(2,1)} %get-tuple-element.41), channel_id=1, source_target_pairs={{0,4},{1,5},{2,6},{3,7},{4,0},{5,1},{6,2},{7,3},{8,12},{9,13},{10,... | collective-permute-start | bytes 294920 | tf_op jit(solution)/shard_map/ppermute | solution.py:274
  249.2 16.9 %collective-permute-start.10 = (bf16[1,192,256]{2,1,0:T(8,128)(2,1)}, bf16[1,192,256]{2,1,0:T(8,128)(2,1)}, u32[]{:S(2)}, u32[]{:S(2)}) collective-permute-start(bf16[1,192,256]{2,1,0:T(8,128)(2,1)} %get-tuple-element.42), channel_id=1, source_target_pairs={{0,5},{1,4},{2,7},{3,6},{4,1},{5,0},{6,3},{7,2},{8,13},{9,12},{10,... | collective-permute-start | bytes 294920 | tf_op jit(solution)/shard_map/ppermute | solution.py:274
  249.6 16.6 %collective-permute-start.11 = (bf16[1,192,256]{2,1,0:T(8,128)(2,1)}, bf16[1,192,256]{2,1,0:T(8,128)(2,1)}, u32[]{:S(2)}, u32[]{:S(2)}) collective-permute-start(bf16[1,192,256]{2,1,0:T(8,128)(2,1)} %get-tuple-element.43), channel_id=1, source_target_pairs={{0,6},{1,7},{2,4},{3,5},{4,2},{5,3},{6,0},{7,1},{8,14},{9,15},{10,... | collective-permute-start | bytes 294920 | tf_op jit(solution)/shard_map/ppermute | solution.py:274
  251.4 14.7 %collective-permute-start.12 = (bf16[1,192,256]{2,1,0:T(8,128)(2,1)}, bf16[1,192,256]{2,1,0:T(8,128)(2,1)}, u32[]{:S(2)}, u32[]{:S(2)}) collective-permute-start(bf16[1,192,256]{2,1,0:T(8,128)(2,1)} %get-tuple-element.44), channel_id=1, source_target_pairs={{0,7},{1,6},{2,5},{3,4},{4,3},{5,2},{6,1},{7,0},{8,15},{9,14},{10,... | collective-permute-start | bytes 294920 | tf_op jit(solution)/shard_map/ppermute | solution.py:274

commit v4 on v3

--- a/solution.py
+++ b/solution.py
@@ -26,7 +26,7 @@
     return jnp.transpose(jnp.broadcast_to(row, (8, row.shape[1])))[:, :1]
 
 
-def slot_grad_kernel(count_ref, rows_ref, cot_ref, gate_ref, out_ref, turned):
+def slot_grad_kernel(half_ref, count_ref, rows_ref, cot_ref, gate_ref, out_ref, turned):
     rows = rows_ref.shape[0]
     live = lax.broadcasted_iota(jnp.int32, (rows, 1), 0) < count_ref[0]
 
@@ -46,28 +46,29 @@
         ).astype(jnp.bfloat16)
 
 
-def slot_grads(row_counts, rows_in, cotangent, gate_row, group_count):
+def slot_grads(half, row_counts, rows_in, cotangent, gate_row, inner):
     rows, ff = rows_in.shape
-    cols = cotangent.shape[1] // group_count
+    cols = cotangent.shape[1] // (2 * inner)
+    pair = inner // 2
     return pl.pallas_call(
         slot_grad_kernel,
         name="slot_grads",
-        out_shape=jax.ShapeDtypeStruct((group_count, ff, cols), jnp.bfloat16),
+        out_shape=jax.ShapeDtypeStruct((inner, ff, cols), jnp.bfloat16),
         grid_spec=pltpu.PrefetchScalarGridSpec(
-            num_scalar_prefetch=1,
-            grid=(group_count // 2,),
+            num_scalar_prefetch=2,
+            grid=(pair,),
             in_specs=[
-                pl.BlockSpec((rows, ff), lambda g, c: (0, 0)),
-                pl.BlockSpec((rows, 2 * cols), lambda g, c: (0, g)),
-                pl.BlockSpec((1, rows), lambda g, c: (0, 0)),
+                pl.BlockSpec((rows, ff), lambda g, h, c: (0, 0)),
+                pl.BlockSpec((rows, 2 * cols), lambda g, h, c: (0, h[0] * pair + g)),
+                pl.BlockSpec((1, rows), lambda g, h, c: (0, 0)),
             ],
-            out_specs=pl.BlockSpec((2, ff, cols), lambda g, c: (g, 0, 0)),
+            out_specs=pl.BlockSpec((2, ff, cols), lambda g, h, c: (g, 0, 0)),
             scratch_shapes=[pltpu.VMEM((ff, rows), jnp.bfloat16)],
         ),
         compiler_params=pltpu.CompilerParams(
             dimension_semantics=("arbitrary",), vmem_limit_bytes=WHOLE_VMEM
         ),
-    )(row_counts, rows_in, cotangent, gate_row)
+    )(half, row_counts, rows_in, cotangent, gate_row)
 
 
 def add_slots(place_ref, grads_ref, total):
@@ -83,11 +84,37 @@
     return max(d for d in (16, 32, 48) if rows % d == 0)
 
 
+def sum_kernel(place_ref, grads_ref, out_ref, total):
+    total[...] = jnp.zeros_like(total)
+    add_slots(place_ref, grads_ref, total)
+    out_ref[...] = total[...].astype(jnp.bfloat16)
+
+
+def expert_sums(place, grads, experts):
+    slots, rows, cols = grads.shape
+    step = rows_step(rows)
+    return pl.pallas_call(
+        sum_kernel,
+        name="expert_sums",
+        out_shape=jax.ShapeDtypeStruct((experts, rows, cols), jnp.bfloat16),
+        grid_spec=pltpu.PrefetchScalarGridSpec(
+            num_scalar_prefetch=1,
+            grid=(rows // step,),
+            in_specs=[pl.BlockSpec((slots, step, cols), lambda i, a: (0, i, 0))],
+            out_specs=pl.BlockSpec((experts, step, cols), lambda i, a: (0, i, 0)),
+            scratch_shapes=[pltpu.VMEM((experts, step, cols), jnp.float32)],
+        ),
+        compiler_params=pltpu.CompilerParams(
+            dimension_semantics=("arbitrary",), vmem_limit_bytes=WHOLE_VMEM
+        ),
+    )(place, grads)
+
+
 def update_kernel(
-    old_ref, new_ref, grads_ref, master_ref, one_ref, two_ref,
+    old_ref, new_ref, grads_ref, sums_ref, master_ref, one_ref, two_ref,
     master_out, one_out, two_out, fresh_ref, send_ref, total,
 ):
-    total[...] = jnp.zeros_like(total)
+    total[...] = sums_ref[...].astype(jnp.float32)
     add_slots(old_ref, grads_ref, total)
     grad = total[...]
     first = beta_one * one_ref[...].astype(jnp.float32) + (1.0 - beta_one) * grad
@@ -107,7 +134,7 @@
     lax.fori_loop(0, send_ref.shape[0], pick, 0, unroll=8)
 
 
-def update(old, new, grads, master, one, two):
+def update(old, new, grads, sums, master, one, two):
     slots, rows, cols = grads.shape
     experts = master.shape[0]
     step = rows_step(rows)
@@ -127,14 +154,14 @@
         grid_spec=pltpu.PrefetchScalarGridSpec(
             num_scalar_prefetch=2,
             grid=(rows // step,),
-            in_specs=[wide, state, state, state],
+            in_specs=[wide, state, state, state, state],
             out_specs=[state, state, state, state, near],
             scratch_shapes=[pltpu.VMEM((experts, step, cols), jnp.float32)],
         ),
         compiler_params=pltpu.CompilerParams(
             dimension_semantics=("arbitrary",), vmem_limit_bytes=WHOLE_VMEM
         ),
-    )(old, new, grads, master, one, two)
+    )(old, new, grads, sums, master, one, two)
 
 
 def next_kernel(half_ref, rows_ref, weight_ref, *rest):
@@ -365,8 +392,8 @@
     )(me, planes, valid, *parts, cotangent, *more)
 
 
-def exchange(blocks, axes):
-    return lax.all_to_all(blocks, axes, split_axis=0, concat_axis=0, tiled=True)
+def exchange(blocks):
+    return lax.all_to_all(blocks, HALF, split_axis=0, concat_axis=0, tiled=True)
 
 
 def across(block):
@@ -380,7 +407,7 @@
     inner, slot_count = lax.axis_size("inner"), lax.axis_size("slot")
     group_count, near_count = 2 * inner, inner * slot_count
     devices = group_count * slot_count
-    _, part_rows, part_cols = master.shape
+    experts, part_rows, part_cols = master.shape
     ff = slot_count * part_rows
     wide = 2
     line = group_count // wide
@@ -390,6 +417,7 @@
     plane = g_own // wide
     me = (g_own % wide) * slot_count + k_own
     old = old_place[:, 0]
+    old_near = lax.dynamic_slice(old, (half * near_count,), (near_count,))
     new = lax.dynamic_slice(new_place[:, 0], (half * near_count,), (near_count,))
     gate_row = gate_prob.reshape(1, -1)
     own, other = half.reshape(1), (1 - half).reshape(1)
@@ -420,18 +448,25 @@
         parts = among_peers(picked(plane_one, wanted, blocks, name == "far"), peers, devices)
         return back(me_one, *table(offs), cotangent, parts, wide, slot_count, so_far, last)
 
-    grads = slot_grads(row_counts, rows_in, cotangent, gate_row, group_count)
-    arrived = exchange(grads.reshape(-1, part_rows, part_cols), ALL)
+    def blocks_of(grads):
+        return grads.reshape(near_count, part_rows, part_cols)
+
+    grads = slot_grads(other, row_counts, rows_in, cotangent, gate_row, inner)
+    arrived = exchange(blocks_of(grads))
+    grads = slot_grads(own, row_counts, rows_in, cotangent, gate_row, inner)
+    sums = expert_sums(old_near, arrived, experts)
+    sums = across(sums)
+    arrived = exchange(blocks_of(grads))
     so_far = back_part("near", None)
     new_master, new_first, new_second, fresh, send = update(
-        old, new, arrived, master, moment_one, moment_two
+        old_near, new, arrived, sums, master, moment_one, moment_two
     )
-    weight = exchange(send, HALF).reshape(inner, ff, part_cols)
+    weight = exchange(send).reshape(inner, ff, part_cols)
     fresh = across(fresh)
     so_far = back_part("mid", so_far)
     next_out = next_rows(own, rows_next, weight)
     picks = half_picked(new, fresh)
-    weight = exchange(picks, HALF).reshape(inner, ff, part_cols)
+    weight = exchange(picks).reshape(inner, ff, part_cols)
     input_grad, gate_grad = back_part("far", so_far, (row_counts, rows_in, gate_row))
     next_out = next_rows(other, rows_next, weight, next_out)
     return input_grad, gate_grad.reshape(-1), new_master, new_first, new_second, next_out

time: 281 us -> 277 us (0.986)
  waiting for transfers between devices: 172 us -> 154 us
  starting transfers between devices: 51.1 us -> 59.6 us
  Pallas kernels: 50.6 us -> 56.5 us
    all_to_all x3 -> x4, waiting for transfers between devices: 72.3 us -> 48 us  [exchange(): return lax.all_to_all(blocks, HALF, split_axis=0, concat_axis=0, tiled=True)]
    ppermute x1 -> x2, waiting for transfers between devices: 33 us -> 38.3 us  [across(): return lax.ppermute(block, 'half', [(0, 1), (1, 0)])]
    all_to_all x3 -> x4, starting transfers between devices: 18.8 us -> 23.4 us  [exchange(): return lax.all_to_all(blocks, HALF, split_axis=0, concat_axis=0, tiled=True)]
    pallas_call x0 -> x1, Pallas kernels: none -> 4.37 us  [expert_sums(): pl.pallas_call(sum_kernel, name='expert_sums', out_shape=jax.ShapeDtypeSt...]
    ppermute x1 -> x2, starting transfers between devices: 1.86 us -> 5.81 us  [across(): return lax.ppermute(block, 'half', [(0, 1), (1, 0)])]
    pallas_call x1 -> x2, Pallas kernels: 6.39 us -> 8.39 us  [slot_grads(): pl.pallas_call(slot_grad_kernel, name='slot_grads', out_shape=jax.ShapeDt...]
  transfers between devices with their start and end apart: 31 -> 33, of which waited for: 15 -> 17; matrix products, arithmetic and copies ran while one was open for 1% -> 1% of each run, Pallas kernels for 12% -> 15%
where the time goes in v4:
time: 277 us; the launch traced here: 275 us
  waiting for transfers between devices  154 us (56%)
  starting transfers between devices  59.6 us (22%)
  Pallas kernels  56.5 us (20%)
    all_to_all x4, waiting for transfers between devices, exchange(): return lax.all_to_all(blocks, HALF, split_axis=0, concat_axis=0, tiled=True)  48 us
    ppermute x3, waiting for transfers between devices, along_line(): high = lax.ppermute(high, LINE, downs)  43.2 us
    ppermute x2, waiting for transfers between devices, across(): return lax.ppermute(block, 'half', [(0, 1), (1, 0)])  38.3 us
    ppermute x21, waiting for transfers between devices, among_peers(): parts.append(lax.ppermute(picks[j], ALL, pairs))  24.2 us
    all_to_all x4, starting transfers between devices, exchange(): return lax.all_to_all(blocks, HALF, split_axis=0, concat_axis=0, tiled=True)  23.4 us
    pallas_call x3, Pallas kernels, back(): pl.pallas_call(functools.partial(back_kernel, wide, peers, slot_count, la...  18 us
    ppermute x21, starting transfers between devices, among_peers(): parts.append(lax.ppermute(picks[j], ALL, pairs))  17.8 us
    pallas_call x3, Pallas kernels, picked(): pl.pallas_call(functools.partial(held_pick_kernel if held else pick_kerne...  8.95 us
  transfers between devices with their start and end apart: 33, of which 17 were waited for; matrix products, arithmetic and copies ran while one was open for 1% of the time, Pallas kernels for 15%

profile of v4, /device:TPU:0, one launch (start us, length us, event | category | flops | bytes accessed | tf_op | source)
XLA Modules:
  0.0 274.9 jit_solution(10001370056502542859)
XLA Ops:
  1.3 4.2 %slot_grads.3 = bf16[4,768,256]{2,1,0:T(8,128)(2,1)} custom-call(s32[1]{0:T(128)} %bitcast.12.half_ref, s32[1]{0:T(128)S(6)} %copy.18.rest_9_.count_ref, bf16[512,768]{1,0:T(8,128)(2,1)} %rows_ref.5, bf16[512,2048]{1,0:T(8,128)(2,1)} %cot_ref.3, f32[1,512]{1,0:T(1,128)} %bitcast.22), custom_call_target="tpu_custom_call" | custom-call | tf_op jit(solution)/shard_map/slot_grads/pallas_call | solution.py:53
  5.5 6.4 %all-to-all-start.1 = ((bf16[16,192,256]{2,1,0:T(8,128)(2,1)}), bf16[16,192,256]{2,1,0:T(8,128)(2,1)}, u32[]{:S(2)}, u32[]{:S(2)}) async-start(bf16[16,192,256]{2,1,0:T(8,128)(2,1)} %bitcast.21), calls=%async_computation.1 | async-start | bytes 3145728 | tf_op jit(solution)/shard_map/all_to_all | solution.py:396
  11.9 4.2 %slot_grads.2 = bf16[4,768,256]{2,1,0:T(8,128)(2,1)} custom-call(s32[1]{0:T(128)} %bitcast.10.half_ref, s32[1]{0:T(128)S(6)} %copy.18.rest_9_.count_ref, bf16[512,768]{1,0:T(8,128)(2,1)} %rows_ref.5, bf16[512,2048]{1,0:T(8,128)(2,1)} %cot_ref.3, f32[1,512]{1,0:T(1,128)} %bitcast.23), custom_call_target="tpu_custom_call" | custom-call | tf_op jit(solution)/shard_map/slot_grads/pallas_call | solution.py:53
  16.1 18.6 %all-to-all-done.1.grads_ref = bf16[16,192,256]{2,1,0:T(8,128)(2,1)} async-done(((bf16[16,192,256]{2,1,0:T(8,128)(2,1)}), bf16[16,192,256]{2,1,0:T(8,128)(2,1)}, u32[]{:S(2)}, u32[]{:S(2)}) %all-to-all-start.1) | async-done | bytes 1572896 | tf_op jit(solution)/shard_map/all_to_all | solution.py:396
  34.6 4.4 %all-to-all-start = ((bf16[16,192,256]{2,1,0:T(8,128)(2,1)}), bf16[16,192,256]{2,1,0:T(8,128)(2,1)}, u32[]{:S(2)}, u32[]{:S(2)}) async-start(bf16[16,192,256]{2,1,0:T(8,128)(2,1)} %bitcast.20), calls=%async_computation | async-start | bytes 3145728 | tf_op jit(solution)/shard_map/all_to_all | solution.py:396
  39.1 0.6 fusion.1.place_ref.old_ref
  39.7 4.4 %expert_sums.1 = bf16[8,192,256]{2,1,0:T(8,128)(2,1)} custom-call(s32[16]{0:T(128)} %fusion.1.place_ref.old_ref, bf16[16,192,256]{2,1,0:T(8,128)(2,1)} %all-to-all-done.1.grads_ref), custom_call_target="tpu_custom_call" | custom-call | tf_op jit(solution)/shard_map/expert_sums/pallas_call | solution.py:96
  44.0 2.6 collective-permute-start.27
  46.6 0.6 fusion.2.new_ref.wanted_ref
  47.2 28.1 %all-to-all-done.grads_ref = bf16[16,192,256]{2,1,0:T(8,128)(2,1)} async-done(((bf16[16,192,256]{2,1,0:T(8,128)(2,1)}), bf16[16,192,256]{2,1,0:T(8,128)(2,1)}, u32[]{:S(2)}, u32[]{:S(2)}) %all-to-all-start) | async-done | bytes 1572896 | tf_op jit(solution)/shard_map/all_to_all | solution.py:396
  75.2 6.6 %collective-permute-done.27.sums_ref = bf16[8,192,256]{2,1,0:T(8,128)(2,1)} collective-permute-done((bf16[8,192,256]{2,1,0:T(8,128)(2,1)}, bf16[8,192,256]{2,1,0:T(8,128)(2,1)}, u32[]{:S(2)}, u32[]{:S(2)}) %collective-permute-start.27) | collective-permute-done | bytes 786464 | tf_op jit(solution)/shard_map/ppermute | solution.py:400
  81.8 7.1 %update.1 = (f32[8,192,256]{2,1,0:T(8,128)}, bf16[8,192,256]{2,1,0:T(8,128)(2,1)}, bf16[8,192,256]{2,1,0:T(8,128)(2,1)}, bf16[8,192,256]{2,1,0:T(8,128)(2,1)}, bf16[16,192,256]{2,1,0:T(8,128)(2,1)}) custom-call(s32[16]{0:T(128)} %fusion.1.place_ref.old_ref, s32[16]{0:T(128)} %fusion.2.new_ref.wanted_ref, bf16[16,192,256]{2,1,0:T(8,128)(2,1)} %all-to-all-done.grads_ref, ...), custom_call_target="tpu_custom_call" | custom-call | tf_op jit(solution)/shard_map/update/pallas_call | solution.py:144
  89.0 4.5 %all-to-all-start.3 = ((bf16[16,192,256]{2,1,0:T(8,128)(2,1)}), bf16[16,192,256]{2,1,0:T(8,128)(2,1)}, u32[]{:S(2)}, u32[]{:S(2)}) async-start(bf16[16,192,256]{2,1,0:T(8,128)(2,1)} %get-tuple-element.67), calls=%async_computation.3 | async-start | bytes 3145728 | tf_op jit(solution)/shard_map/all_to_all | solution.py:396
  93.5 3.2 %collective-permute-start.28 = (bf16[8,192,256]{2,1,0:T(8,128)(2,1)S(1)}, bf16[8,192,256]{2,1,0:T(8,128)(2,1)}, u32[]{:S(2)}, u32[]{:S(2)}) collective-permute-start(bf16[8,192,256]{2,1,0:T(8,128)(2,1)S(1)} %copy-done.3), channel_id=1, source_target_pairs={{0,16},{16,0},{1,17},{17,1},{2,18},{18,2},{3,19},{19,3},{4,20},{20... | collective-permute-start | bytes 2359304 | tf_op jit(solution)/shard_map/ppermute | solution.py:400
  96.7 31.7 %collective-permute-done.28.block_ref = bf16[8,192,256]{2,1,0:T(8,128)(2,1)} collective-permute-done((bf16[8,192,256]{2,1,0:T(8,128)(2,1)S(1)}, bf16[8,192,256]{2,1,0:T(8,128)(2,1)}, u32[]{:S(2)}, u32[]{:S(2)}) %collective-permute-start.28) | collective-permute-done | bytes 786464 | tf_op jit(solution)/shard_map/ppermute | solution.py:400
  128.4 2.4 half_picked.1
  130.8 1.3 all-to-all-done.3
  132.2 8.1 %all-to-all-start.2 = ((bf16[16,192,256]{2,1,0:T(8,128)(2,1)}), bf16[16,192,256]{2,1,0:T(8,128)(2,1)}, u32[]{:S(2)}, u32[]{:S(2)}) async-start(bf16[16,192,256]{2,1,0:T(8,128)(2,1)} %half_picked.1), calls=%async_computation.2 | async-start | bytes 3145728 | tf_op jit(solution)/shard_map/all_to_all | solution.py:396
  140.3 0.1 convert_element_type.13.rest_0_
  140.4 1.3 collective-permute-start.3
  141.7 5.5 %collective-permute-start = (bf16[8,192,256]{2,1,0:T(8,128)(2,1)S(1)}, bf16[8,192,256]{2,1,0:T(8,128)(2,1)}, u32[]{:S(2)}, u32[]{:S(2)}) collective-permute-start(bf16[8,192,256]{2,1,0:T(8,128)(2,1)S(1)} %convert_element_type.13.rest_0_), channel_id=1, source_target_pairs={{0,8},{4,12},{8,16},{12,20},{16,24},{20,28},{1,9},{5,13},{9,17},{1... | collective-permute-start | bytes 2359304 | tf_op jit(solution)/shard_map/ppermute | solution.py:228
  147.2 30.1 %collective-permute-done.3.rest_2_ = bf16[8,192,256]{2,1,0:T(8,128)(2,1)} collective-permute-done((bf16[8,192,256]{2,1,0:T(8,128)(2,1)S(1)}, bf16[8,192,256]{2,1,0:T(8,128)(2,1)}, u32[]{:S(2)}, u32[]{:S(2)}) %collective-permute-start.3) | collective-permute-done | bytes 786464 | tf_op jit(solution)/shard_map/ppermute | solution.py:229
  177.3 1.3 collective-permute-start.4
  178.6 1.6 collective-permute-start.1
  180.2 1.2 gather_fusion
  181.4 3.8 %picked.5 = (bf16[3,192,256]{2,1,0:T(8,128)(2,1)}, bf16[3,192,256]{2,1,0:T(8,128)(2,1)}, bf16[3,192,256]{2,1,0:T(8,128)(2,1)}, bf16[3,192,256]{2,1,0:T(8,128)(2,...) custom-call(s32[1]{0:T(128)} %bitcast.1.plane_ref, ...), custom_call_target="tpu_custom_call" | custom-call | tf_op jit(solution)/shard_map/picked/pallas_call | solution.py:265
  185.2 0.1 collective-permute-start.20
  185.3 13.1 %collective-permute-done.4.rest_1_ = bf16[8,192,256]{2,1,0:T(8,128)(2,1)} collective-permute-done((bf16[8,192,256]{2,1,0:T(8,128)(2,1)}, bf16[8,192,256]{2,1,0:T(8,128)(2,1)}, u32[]{:S(2)}, u32[]{:S(2)}) %collective-permute-start.4) | collective-permute-done | bytes 786464 | tf_op jit(solution)/shard_map/ppermute | solution.py:229
  198.4 1.3 collective-permute-start.5
  199.7 1.6 collective-permute-start.2
  201.3 2.9 %collective-permute-start.21 = (bf16[3,192,256]{2,1,0:T(8,128)(2,1)}, bf16[3,192,256]{2,1,0:T(8,128)(2,1)}, u32[]{:S(2)}, u32[]{:S(2)}) collective-permute-start(bf16[3,192,256]{2,1,0:T(8,128)(2,1)} %get-tuple-element.55), channel_id=1, source_target_pairs={{0,2},{1,3},{2,0},{3,1},{4,6},{5,7},{6,4},{7,5},{8,10},{9,11},{10,... | collective-permute-start | bytes 884744 | tf_op jit(solution)/shard_map/ppermute | solution.py:301
  204.2 0.9 collective-permute-start.23
  205.2 7.2 %collective-permute-done.21.rest_2_ = bf16[3,192,256]{2,1,0:T(8,128)(2,1)} collective-permute-done((bf16[3,192,256]{2,1,0:T(8,128)(2,1)}, bf16[3,192,256]{2,1,0:T(8,128)(2,1)}, u32[]{:S(2)}, u32[]{:S(2)}) %collective-permute-start.21) | collective-permute-done | bytes 294944 | tf_op jit(solution)/shard_map/ppermute | solution.py:301
  212.4 3.6 %collective-permute-done.22.rest_3_ = bf16[3,192,256]{2,1,0:T(8,128)(2,1)} collective-permute-done((bf16[3,192,256]{2,1,0:T(8,128)(2,1)}, bf16[3,192,256]{2,1,0:T(8,128)(2,1)}, u32[]{:S(2)}, u32[]{:S(2)}) %collective-permute-start.22) | collective-permute-done | bytes 294944 | tf_op jit(solution)/shard_map/ppermute | solution.py:301
  215.9 0.7 collective-permute-start.25
  216.6 2.4 collective-permute-start.26
  219.1 2.8 %picked.4 = (bf16[1,192,256]{2,1,0:T(8,128)(2,1)}, bf16[1,192,256]{2,1,0:T(8,128)(2,1)}, bf16[1,192,256]{2,1,0:T(8,128)(2,1)}, bf16[1,192,256]{2,1,0:T(8,128)(2,...) custom-call(s32[1]{0:T(128)} %bitcast.1.plane_ref, ...), custom_call_target="tpu_custom_call" | custom-call | tf_op jit(solution)/shard_map/picked/pallas_call | solution.py:265
  221.9 0.1 collective-permute-done.24.rest_5_
  222.0 6.8 %collective-permute-done.25.rest_6_ = bf16[3,192,256]{2,1,0:T(8,128)(2,1)} collective-permute-done((bf16[3,192,256]{2,1,0:T(8,128)(2,1)}, bf16[3,192,256]{2,1,0:T(8,128)(2,1)}, u32[]{:S(2)}, u32[]{:S(2)}) %collective-permute-start.25) | collective-permute-done | bytes 294944 | tf_op jit(solution)/shard_map/ppermute | solution.py:301
  228.8 2.2 collective-permute-start.15
  230.9 0.9 collective-permute-start.16
  231.9 2.3 picked.3
  234.2 1.9 collective-permute-done.26.rest_7_
  236.1 0.2 collective-permute-start.18
  236.3 1.4 collective-permute-done.14.rest_2_
  237.7 1.8 collective-permute-start.19
  239.5 0.3 collective-permute-done.15.rest_3_
  239.8 0.1 collective-permute-start.6
  239.9 0.5 collective-permute-start.7
  240.4 0.5 and_convert_fusion.valid_ref
  240.9 0.7 collective-permute-done.17.rest_5_
  241.5 0.6 collective-permute-start.8
  242.2 0.8 collective-permute-done.18.rest_6_
  242.9 0.8 collective-permute-start.9
  243.8 1.5 collective-permute-done.19.rest_7_
  245.2 0.4 collective-permute-start.10
  245.6 1.9 collective-permute-start.11
  247.4 1.6 collective-permute-start.12
  249.0 0.6 add_clamp_fusion.plane_ref
  249.6 7.7 %back.3.rest_9_ = f32[512,768]{1,0:T(8,128)} custom-call(s32[1]{0:T(128)} %bitcast.me_ref, s32[3]{0:T(128)} %add_clamp_fusion.plane_ref, s32[3]{0:T(128)} %and_convert_fusion.valid_ref, bf16[3,192,256]{2,1,0:T(8,128)(2,1)} %get-tuple-element.53.rest_0_, bf16[3,192,256]{2,1,0:T(8,128)(2,1)} %collective-permute-done.20.rest_1_, ...), custom_call_target="tpu_custom_call" | custom-call | tf_op jit(solution)/shard_map/back/pallas_call | solution.py:378
  257.3 4.9 %back.4.rest_12_ = f32[512,768]{1,0:T(8,128)} custom-call(s32[1]{0:T(128)} %bitcast.me_ref, s32[1]{0:T(128)S(6)} %min.19.plane_ref, s32[1]{0:T(128)S(6)} %convert_element_type.14.valid_ref, bf16[1,192,256]{2,1,0:T(8,128)(2,1)} %get-tuple-element.45.rest_0_, bf16[1,192,256]{2,1,0:T(8,128)(2,1)} %collective-permute-done.13.rest_1_, ...), custom_call_target="tpu_custom_call" | custom-call | tf_op jit(solution)/shard_map/back/pallas_call | solution.py:378
  262.2 5.4 %back.5 = (bf16[512,768]{1,0:T(8,128)(2,1)}, f32[1,512]{1,0:T(1,128)}) custom-call(s32[1]{0:T(128)} %bitcast.me_ref, s32[1]{0:T(128)S(6)} %min.18.plane_ref, s32[1]{0:T(128)S(6)} %convert_element_type.12.valid_ref, bf16[1,192,256]{2,1,0:T(8,128)(2,1)} %get-tuple-element.37.rest_0_, bf16[1,192,256]{2,1,0:T(8,128)(2,1)} %collective-permute-done.6.rest_1_, ...), custom_call_target="tpu_custom_call" | custom-call | tf_op jit(solution)/shard_map/back/pallas_call | solution.py:378
  267.6 3.7 %next_rows.2.rest_0_ = bf16[512,2048]{1,0:T(8,128)(2,1)} custom-call(s32[1]{0:T(128)} %bitcast.10.half_ref, bf16[512,768]{1,0:T(8,128)(2,1)} %rows_ref.7, bf16[4,768,256]{2,1,0:T(8,128)(2,1)} %bitcast.15.weight_ref), custom_call_target="tpu_custom_call" | custom-call | tf_op jit(solution)/shard_map/next_rows/pallas_call | solution.py:183
  271.3 3.6 %next_rows.3 = bf16[512,2048]{1,0:T(8,128)(2,1)} custom-call(s32[1]{0:T(128)} %bitcast.12.half_ref, bf16[512,768]{1,0:T(8,128)(2,1)} %rows_ref.7, bf16[4,768,256]{2,1,0:T(8,128)(2,1)} %bitcast.14.weight_ref, bf16[512,2048]{1,0:T(8,128)(2,1)} %next_rows.2.rest_0_), custom_call_target="tpu_custom_call", output_to_operand_aliasing={{}: (3, {})} | custom-call | tf_op jit(solution)/shard_map/next_rows/pallas_call | solution.py:183
  (36 shorter events, 0.2 us)
Async XLA Ops:
  0.6 38.4 %copy-start = (s32[32,1]{0,1:T(1,128)S(1)}, s32[32,1]{0,1:T(1,128)}, u32[]{:S(2)}) copy-start(s32[32,1]{0,1:T(1,128)} %param.14) | copy-start | bytes 388
  5.5 29.1 %all-to-all-start.1 = ((bf16[16,192,256]{2,1,0:T(8,128)(2,1)}), bf16[16,192,256]{2,1,0:T(8,128)(2,1)}, u32[]{:S(2)}, u32[]{:S(2)}) async-start(bf16[16,192,256]{2,1,0:T(8,128)(2,1)} %bitcast.21), calls=%async_computation.1 | async-start | bytes 3145728 | tf_op jit(solution)/shard_map/all_to_all | solution.py:396
  34.6 40.6 %all-to-all-start = ((bf16[16,192,256]{2,1,0:T(8,128)(2,1)}), bf16[16,192,256]{2,1,0:T(8,128)(2,1)}, u32[]{:S(2)}, u32[]{:S(2)}) async-start(bf16[16,192,256]{2,1,0:T(8,128)(2,1)} %bitcast.20), calls=%async_computation | async-start | bytes 3145728 | tf_op jit(solution)/shard_map/all_to_all | solution.py:396
  39.1 7.6 %copy-start.4 = (s32[32,1]{0,1:T(1,128)S(1)}, s32[32,1]{0,1:T(1,128)}, u32[]{:S(2)}) copy-start(s32[32,1]{0,1:T(1,128)} %param.15) | copy-start | bytes 388
  44.0 37.8 %collective-permute-start.27 = (bf16[8,192,256]{2,1,0:T(8,128)(2,1)}, bf16[8,192,256]{2,1,0:T(8,128)(2,1)}, u32[]{:S(2)}, u32[]{:S(2)}) collective-permute-start(bf16[8,192,256]{2,1,0:T(8,128)(2,1)} %expert_sums.1), channel_id=1, source_target_pairs={{0,16},{16,0},{1,17},{17,1},{2,18},{18,2},{3,19},{19,3},{4,20},{20... | collective-permute-start | bytes 2359304 | tf_op jit(solution)/shard_map/ppermute | solution.py:400
  88.9 4.6 %copy-start.3 = (bf16[8,192,256]{2,1,0:T(8,128)(2,1)S(1)}, bf16[8,192,256]{2,1,0:T(8,128)(2,1)}, u32[]{:S(2)}) copy-start(bf16[8,192,256]{2,1,0:T(8,128)(2,1)} %get-tuple-element.66) | copy-start | bytes 2359300
  89.0 43.2 %all-to-all-start.3 = ((bf16[16,192,256]{2,1,0:T(8,128)(2,1)}), bf16[16,192,256]{2,1,0:T(8,128)(2,1)}, u32[]{:S(2)}, u32[]{:S(2)}) async-start(bf16[16,192,256]{2,1,0:T(8,128)(2,1)} %get-tuple-element.67), calls=%async_computation.3 | async-start | bytes 3145728 | tf_op jit(solution)/shard_map/all_to_all | solution.py:396
  93.5 34.9 %collective-permute-start.28 = (bf16[8,192,256]{2,1,0:T(8,128)(2,1)S(1)}, bf16[8,192,256]{2,1,0:T(8,128)(2,1)}, u32[]{:S(2)}, u32[]{:S(2)}) collective-permute-start(bf16[8,192,256]{2,1,0:T(8,128)(2,1)S(1)} %copy-done.3), channel_id=1, source_target_pairs={{0,16},{16,0},{1,17},{17,1},{2,18},{18,2},{3,19},{19,3},{4,20},{20... | collective-permute-start | bytes 2359304 | tf_op jit(solution)/shard_map/ppermute | solution.py:400
  130.8 9.5 %copy-start.1 = (f32[8,192,256]{2,1,0:T(8,128)S(1)}, f32[8,192,256]{2,1,0:T(8,128)}, u32[]{:S(2)}) copy-start(f32[8,192,256]{2,1,0:T(8,128)} %master_ref.1) | copy-start | bytes 4718596
  132.2 139.1 %all-to-all-start.2 = ((bf16[16,192,256]{2,1,0:T(8,128)(2,1)}), bf16[16,192,256]{2,1,0:T(8,128)(2,1)}, u32[]{:S(2)}, u32[]{:S(2)}) async-start(bf16[16,192,256]{2,1,0:T(8,128)(2,1)} %half_picked.1), calls=%async_computation.2 | async-start | bytes 3145728 | tf_op jit(solution)/shard_map/all_to_all | solution.py:396
  140.4 1.3 copy-start.2
  140.4 36.9 %collective-permute-start.3 = (bf16[8,192,256]{2,1,0:T(8,128)(2,1)S(1)}, bf16[8,192,256]{2,1,0:T(8,128)(2,1)}, u32[]{:S(2)}, u32[]{:S(2)}) collective-permute-start(bf16[8,192,256]{2,1,0:T(8,128)(2,1)S(1)} %convert_element_type.13.rest_0_), channel_id=1, source_target_pairs={{8,0},{12,4},{16,8},{20,12},{24,16},{28,20},{9,1},{13,5},{17,9},{2... | collective-permute-start | bytes 2359304 | tf_op jit(solution)/shard_map/ppermute | solution.py:229
  141.7 36.8 %collective-permute-start = (bf16[8,192,256]{2,1,0:T(8,128)(2,1)S(1)}, bf16[8,192,256]{2,1,0:T(8,128)(2,1)}, u32[]{:S(2)}, u32[]{:S(2)}) collective-permute-start(bf16[8,192,256]{2,1,0:T(8,128)(2,1)S(1)} %convert_element_type.13.rest_0_), channel_id=1, source_target_pairs={{0,8},{4,12},{8,16},{12,20},{16,24},{20,28},{1,9},{5,13},{9,17},{1... | collective-permute-start | bytes 2359304 | tf_op jit(solution)/shard_map/ppermute | solution.py:228
  177.3 21.2 %collective-permute-start.4 = (bf16[8,192,256]{2,1,0:T(8,128)(2,1)}, bf16[8,192,256]{2,1,0:T(8,128)(2,1)}, u32[]{:S(2)}, u32[]{:S(2)}) collective-permute-start(bf16[8,192,256]{2,1,0:T(8,128)(2,1)} %collective-permute-done.3.rest_2_), channel_id=1, source_target_pairs={{8,0},{12,4},{16,8},{20,12},{9,1},{13,5},{17,9},{21,13},{10,2},{14... | collective-permute-start | bytes 2359304 | tf_op jit(solution)/shard_map/ppermute | solution.py:229
  178.6 21.2 %collective-permute-start.1 = (bf16[8,192,256]{2,1,0:T(8,128)(2,1)}, bf16[8,192,256]{2,1,0:T(8,128)(2,1)}, u32[]{:S(2)}, u32[]{:S(2)}) collective-permute-start(bf16[8,192,256]{2,1,0:T(8,128)(2,1)} %collective-permute-done.rest_1_), channel_id=1, source_target_pairs={{8,16},{12,20},{16,24},{20,28},{9,17},{13,21},{17,25},{21,29},{10,... | collective-permute-start | bytes 2359304 | tf_op jit(solution)/shard_map/ppermute | solution.py:228
  185.2 19.0 %collective-permute-start.20 = (bf16[3,192,256]{2,1,0:T(8,128)(2,1)}, bf16[3,192,256]{2,1,0:T(8,128)(2,1)}, u32[]{:S(2)}, u32[]{:S(2)}) collective-permute-start(bf16[3,192,256]{2,1,0:T(8,128)(2,1)} %get-tuple-element.54), channel_id=1, source_target_pairs={{0,1},{1,0},{2,3},{3,2},{4,5},{5,4},{6,7},{7,6},{8,9},{9,8},{10,11... | collective-permute-start | bytes 884744 | tf_op jit(solution)/shard_map/ppermute | solution.py:301
  198.4 30.3 %collective-permute-start.5 = (bf16[8,192,256]{2,1,0:T(8,128)(2,1)}, bf16[8,192,256]{2,1,0:T(8,128)(2,1)}, u32[]{:S(2)}, u32[]{:S(2)}) collective-permute-start(bf16[8,192,256]{2,1,0:T(8,128)(2,1)} %collective-permute-done.4.rest_1_), channel_id=1, source_target_pairs={{8,0},{12,4},{9,1},{13,5},{10,2},{14,6},{11,3},{15,7}} | collective-permute-start | bytes 2359304 | tf_op jit(solution)/shard_map/ppermute | solution.py:229
  199.7 31.2 %collective-permute-start.2 = (bf16[8,192,256]{2,1,0:T(8,128)(2,1)}, bf16[8,192,256]{2,1,0:T(8,128)(2,1)}, u32[]{:S(2)}, u32[]{:S(2)}) collective-permute-start(bf16[8,192,256]{2,1,0:T(8,128)(2,1)} %collective-permute-done.1.rest_0_), channel_id=1, source_target_pairs={{16,24},{20,28},{17,25},{21,29},{18,26},{22,30},{19,27},{23,31}} | collective-permute-start | bytes 2359304 | tf_op jit(solution)/shard_map/ppermute | solution.py:228
  201.3 11.0 %collective-permute-start.21 = (bf16[3,192,256]{2,1,0:T(8,128)(2,1)}, bf16[3,192,256]{2,1,0:T(8,128)(2,1)}, u32[]{:S(2)}, u32[]{:S(2)}) collective-permute-start(bf16[3,192,256]{2,1,0:T(8,128)(2,1)} %get-tuple-element.55), channel_id=1, source_target_pairs={{0,2},{1,3},{2,0},{3,1},{4,6},{5,7},{6,4},{7,5},{8,10},{9,11},{10,... | collective-permute-start | bytes 884744 | tf_op jit(solution)/shard_map/ppermute | solution.py:301
  204.2 11.8 %collective-permute-start.22 = (bf16[3,192,256]{2,1,0:T(8,128)(2,1)}, bf16[3,192,256]{2,1,0:T(8,128)(2,1)}, u32[]{:S(2)}, u32[]{:S(2)}) collective-permute-start(bf16[3,192,256]{2,1,0:T(8,128)(2,1)} %get-tuple-element.56), channel_id=1, source_target_pairs={{0,3},{1,2},{2,1},{3,0},{4,7},{5,6},{6,5},{7,4},{8,11},{9,10},{10,... | collective-permute-start | bytes 884744 | tf_op jit(solution)/shard_map/ppermute | solution.py:301
  204.2 12.4 %collective-permute-start.23 = (bf16[3,192,256]{2,1,0:T(8,128)(2,1)}, bf16[3,192,256]{2,1,0:T(8,128)(2,1)}, u32[]{:S(2)}, u32[]{:S(2)}) collective-permute-start(bf16[3,192,256]{2,1,0:T(8,128)(2,1)} %get-tuple-element.57), channel_id=1, source_target_pairs={{0,4},{1,5},{2,6},{3,7},{4,0},{5,1},{6,2},{7,3},{8,12},{9,13},{10,... | collective-permute-start | bytes 884744 | tf_op jit(solution)/shard_map/ppermute | solution.py:301
  212.4 9.6 %collective-permute-start.24 = (bf16[3,192,256]{2,1,0:T(8,128)(2,1)}, bf16[3,192,256]{2,1,0:T(8,128)(2,1)}, u32[]{:S(2)}, u32[]{:S(2)}) collective-permute-start(bf16[3,192,256]{2,1,0:T(8,128)(2,1)} %get-tuple-element.58), channel_id=1, source_target_pairs={{0,5},{1,4},{2,7},{3,6},{4,1},{5,0},{6,3},{7,2},{8,13},{9,12},{10,... | collective-permute-start | bytes 884744 | tf_op jit(solution)/shard_map/ppermute | solution.py:301
  215.9 12.8 %collective-permute-start.25 = (bf16[3,192,256]{2,1,0:T(8,128)(2,1)}, bf16[3,192,256]{2,1,0:T(8,128)(2,1)}, u32[]{:S(2)}, u32[]{:S(2)}) collective-permute-start(bf16[3,192,256]{2,1,0:T(8,128)(2,1)} %get-tuple-element.59), channel_id=1, source_target_pairs={{0,6},{1,7},{2,4},{3,5},{4,2},{5,3},{6,0},{7,1},{8,14},{9,15},{10,... | collective-permute-start | bytes 884744 | tf_op jit(solution)/shard_map/ppermute | solution.py:301
  216.6 23.8 %copy-start.5 = (s32[3]{0:T(128)S(1)}, s32[3]{0:T(128)}, u32[]{:S(2)}) copy-start(s32[3]{0:T(128)} %constant.67.clone.1) | copy-start | bytes 40
  216.6 19.5 %collective-permute-start.26 = (bf16[3,192,256]{2,1,0:T(8,128)(2,1)}, bf16[3,192,256]{2,1,0:T(8,128)(2,1)}, u32[]{:S(2)}, u32[]{:S(2)}) collective-permute-start(bf16[3,192,256]{2,1,0:T(8,128)(2,1)} %get-tuple-element.60), channel_id=1, source_target_pairs={{0,7},{1,6},{2,5},{3,4},{4,3},{5,2},{6,1},{7,0},{8,15},{9,14},{10,... | collective-permute-start | bytes 884744 | tf_op jit(solution)/shard_map/ppermute | solution.py:301
  222.0 14.1 %collective-permute-start.13 = (bf16[1,192,256]{2,1,0:T(8,128)(2,1)}, bf16[1,192,256]{2,1,0:T(8,128)(2,1)}, u32[]{:S(2)}, u32[]{:S(2)}) collective-permute-start(bf16[1,192,256]{2,1,0:T(8,128)(2,1)} %get-tuple-element.46), channel_id=1, source_target_pairs={{0,1},{1,0},{2,3},{3,2},{4,5},{5,4},{6,7},{7,6},{8,9},{9,8},{10,11... | collective-permute-start | bytes 294920 | tf_op jit(solution)/shard_map/ppermute | solution.py:301
  228.8 8.9 %collective-permute-start.14 = (bf16[1,192,256]{2,1,0:T(8,128)(2,1)}, bf16[1,192,256]{2,1,0:T(8,128)(2,1)}, u32[]{:S(2)}, u32[]{:S(2)}) collective-permute-start(bf16[1,192,256]{2,1,0:T(8,128)(2,1)} %get-tuple-element.47), channel_id=1, source_target_pairs={{0,2},{1,3},{2,0},{3,1},{4,6},{5,7},{6,4},{7,5},{8,10},{9,11},{10,... | collective-permute-start | bytes 294920 | tf_op jit(solution)/shard_map/ppermute | solution.py:301
  228.8 11.0 %collective-permute-start.15 = (bf16[1,192,256]{2,1,0:T(8,128)(2,1)}, bf16[1,192,256]{2,1,0:T(8,128)(2,1)}, u32[]{:S(2)}, u32[]{:S(2)}) collective-permute-start(bf16[1,192,256]{2,1,0:T(8,128)(2,1)} %get-tuple-element.48), channel_id=1, source_target_pairs={{0,3},{1,2},{2,1},{3,0},{4,7},{5,6},{6,5},{7,4},{8,11},{9,10},{10,... | collective-permute-start | bytes 294920 | tf_op jit(solution)/shard_map/ppermute | solution.py:301
  230.9 9.0 %collective-permute-start.16 = (bf16[1,192,256]{2,1,0:T(8,128)(2,1)}, bf16[1,192,256]{2,1,0:T(8,128)(2,1)}, u32[]{:S(2)}, u32[]{:S(2)}) collective-permute-start(bf16[1,192,256]{2,1,0:T(8,128)(2,1)} %get-tuple-element.49), channel_id=1, source_target_pairs={{0,4},{1,5},{2,6},{3,7},{4,0},{5,1},{6,2},{7,3},{8,12},{9,13},{10,... | collective-permute-start | bytes 294920 | tf_op jit(solution)/shard_map/ppermute | solution.py:301
  236.1 5.4 %collective-permute-start.17 = (bf16[1,192,256]{2,1,0:T(8,128)(2,1)}, bf16[1,192,256]{2,1,0:T(8,128)(2,1)}, u32[]{:S(2)}, u32[]{:S(2)}) collective-permute-start(bf16[1,192,256]{2,1,0:T(8,128)(2,1)} %get-tuple-element.50), channel_id=1, source_target_pairs={{0,5},{1,4},{2,7},{3,6},{4,1},{5,0},{6,3},{7,2},{8,13},{9,12},{10,... | collective-permute-start | bytes 294920 | tf_op jit(solution)/shard_map/ppermute | solution.py:301
  236.1 6.8 %collective-permute-start.18 = (bf16[1,192,256]{2,1,0:T(8,128)(2,1)}, bf16[1,192,256]{2,1,0:T(8,128)(2,1)}, u32[]{:S(2)}, u32[]{:S(2)}) collective-permute-start(bf16[1,192,256]{2,1,0:T(8,128)(2,1)} %get-tuple-element.51), channel_id=1, source_target_pairs={{0,6},{1,7},{2,4},{3,5},{4,2},{5,3},{6,0},{7,1},{8,14},{9,15},{10,... | collective-permute-start | bytes 294920 | tf_op jit(solution)/shard_map/ppermute | solution.py:301
  237.7 7.5 %collective-permute-start.19 = (bf16[1,192,256]{2,1,0:T(8,128)(2,1)}, bf16[1,192,256]{2,1,0:T(8,128)(2,1)}, u32[]{:S(2)}, u32[]{:S(2)}) collective-permute-start(bf16[1,192,256]{2,1,0:T(8,128)(2,1)} %get-tuple-element.52), channel_id=1, source_target_pairs={{0,7},{1,6},{2,5},{3,4},{4,3},{5,2},{6,1},{7,0},{8,15},{9,14},{10,... | collective-permute-start | bytes 294920 | tf_op jit(solution)/shard_map/ppermute | solution.py:301
  239.8 5.8 %collective-permute-start.6 = (bf16[1,192,256]{2,1,0:T(8,128)(2,1)}, bf16[1,192,256]{2,1,0:T(8,128)(2,1)}, u32[]{:S(2)}, u32[]{:S(2)}) collective-permute-start(bf16[1,192,256]{2,1,0:T(8,128)(2,1)} %get-tuple-element.38), channel_id=1, source_target_pairs={{0,1},{1,0},{2,3},{3,2},{4,5},{5,4},{6,7},{7,6},{8,9},{9,8},{10,11... | collective-permute-start | bytes 294920 | tf_op jit(solution)/shard_map/ppermute | solution.py:301
  239.9 7.5 %collective-permute-start.7 = (bf16[1,192,256]{2,1,0:T(8,128)(2,1)}, bf16[1,192,256]{2,1,0:T(8,128)(2,1)}, u32[]{:S(2)}, u32[]{:S(2)}) collective-permute-start(bf16[1,192,256]{2,1,0:T(8,128)(2,1)} %get-tuple-element.39), channel_id=1, source_target_pairs={{0,2},{1,3},{2,0},{3,1},{4,6},{5,7},{6,4},{7,5},{8,10},{9,11},{10,... | collective-permute-start | bytes 294920 | tf_op jit(solution)/shard_map/ppermute | solution.py:301
  241.5 20.6 %collective-permute-start.8 = (bf16[1,192,256]{2,1,0:T(8,128)(2,1)}, bf16[1,192,256]{2,1,0:T(8,128)(2,1)}, u32[]{:S(2)}, u32[]{:S(2)}) collective-permute-start(bf16[1,192,256]{2,1,0:T(8,128)(2,1)} %get-tuple-element.40), channel_id=1, source_target_pairs={{0,3},{1,2},{2,1},{3,0},{4,7},{5,6},{6,5},{7,4},{8,11},{9,10},{10,... | collective-permute-start | bytes 294920 | tf_op jit(solution)/shard_map/ppermute | solution.py:301
  242.9 19.2 %collective-permute-start.9 = (bf16[1,192,256]{2,1,0:T(8,128)(2,1)}, bf16[1,192,256]{2,1,0:T(8,128)(2,1)}, u32[]{:S(2)}, u32[]{:S(2)}) collective-permute-start(bf16[1,192,256]{2,1,0:T(8,128)(2,1)} %get-tuple-element.41), channel_id=1, source_target_pairs={{0,4},{1,5},{2,6},{3,7},{4,0},{5,1},{6,2},{7,3},{8,12},{9,13},{10,... | collective-permute-start | bytes 294920 | tf_op jit(solution)/shard_map/ppermute | solution.py:301
  245.2 17.0 %collective-permute-start.10 = (bf16[1,192,256]{2,1,0:T(8,128)(2,1)}, bf16[1,192,256]{2,1,0:T(8,128)(2,1)}, u32[]{:S(2)}, u32[]{:S(2)}) collective-permute-start(bf16[1,192,256]{2,1,0:T(8,128)(2,1)} %get-tuple-element.42), channel_id=1, source_target_pairs={{0,5},{1,4},{2,7},{3,6},{4,1},{5,0},{6,3},{7,2},{8,13},{9,12},{10,... | collective-permute-start | bytes 294920 | tf_op jit(solution)/shard_map/ppermute | solution.py:301
  245.6 16.6 %collective-permute-start.11 = (bf16[1,192,256]{2,1,0:T(8,128)(2,1)}, bf16[1,192,256]{2,1,0:T(8,128)(2,1)}, u32[]{:S(2)}, u32[]{:S(2)}) collective-permute-start(bf16[1,192,256]{2,1,0:T(8,128)(2,1)} %get-tuple-element.43), channel_id=1, source_target_pairs={{0,6},{1,7},{2,4},{3,5},{4,2},{5,3},{6,0},{7,1},{8,14},{9,15},{10,... | collective-permute-start | bytes 294920 | tf_op jit(solution)/shard_map/ppermute | solution.py:301
  247.4 14.8 %collective-permute-start.12 = (bf16[1,192,256]{2,1,0:T(8,128)(2,1)}, bf16[1,192,256]{2,1,0:T(8,128)(2,1)}, u32[]{:S(2)}, u32[]{:S(2)}) collective-permute-start(bf16[1,192,256]{2,1,0:T(8,128)(2,1)} %get-tuple-element.44), channel_id=1, source_target_pairs={{0,7},{1,6},{2,5},{3,4},{4,3},{5,2},{6,1},{7,0},{8,15},{9,14},{10,... | collective-permute-start | bytes 294920 | tf_op jit(solution)/shard_map/ppermute | solution.py:301

commit v5 on v4

--- a/solution.py
+++ b/solution.py
@@ -80,8 +80,8 @@
     lax.fori_loop(0, grads_ref.shape[0], add, 0, unroll=8)
 
 
-def rows_step(rows):
-    return max(d for d in (16, 32, 48) if rows % d == 0)
+def rows_step(rows, most):
+    return max(d for d in (16, 32, 48, 96) if d <= most and rows % d == 0)
 
 
 def sum_kernel(place_ref, grads_ref, out_ref, total):
@@ -92,7 +92,7 @@
 
 def expert_sums(place, grads, experts):
     slots, rows, cols = grads.shape
-    step = rows_step(rows)
+    step = rows_step(rows, 48)
     return pl.pallas_call(
         sum_kernel,
         name="expert_sums",
@@ -137,7 +137,7 @@
 def update(old, new, grads, sums, master, one, two):
     slots, rows, cols = grads.shape
     experts = master.shape[0]
-    step = rows_step(rows)
+    step = rows_step(rows, 96)
     state = pl.BlockSpec((experts, step, cols), lambda i, a, b: (0, i, 0))
     wide = pl.BlockSpec((slots, step, cols), lambda i, a, b: (0, i, 0))
     near = pl.BlockSpec((new.shape[0], step, cols), lambda i, a, b: (0, i, 0))
@@ -170,13 +170,13 @@
     for i in range(2):
         out_ref[:, i * cols : (i + 1) * cols] = jnp.dot(
             rows_ref[...],
-            weight_ref[2 * pl.program_id(0) + i],
+            weight_ref[i],
             preferred_element_type=jnp.float32,
         ).astype(jnp.bfloat16)
 
 
 def next_rows(half, rows_next, weight, so_far=None):
-    inner, _, cols = weight.shape
+    inner, ff, cols = weight.shape
     rows = rows_next.shape[0]
     pair = inner // 2
     more = () if so_far is None else (so_far,)
@@ -187,7 +187,10 @@
         grid_spec=pltpu.PrefetchScalarGridSpec(
             num_scalar_prefetch=1,
             grid=(pair,),
-            in_specs=[pl.BlockSpec(memory_space=pltpu.VMEM)] * 2
+            in_specs=[
+                pl.BlockSpec(memory_space=pltpu.VMEM),
+                pl.BlockSpec((2, ff, cols), lambda g, h: (g, 0, 0)),
+            ]
             + [pl.BlockSpec(memory_space=pl.ANY)] * len(more),
             out_specs=pl.BlockSpec((rows, 2 * cols), lambda g, h: (0, h[0] * pair + g)),
         ),

time: 277 us -> 275 us (level)
  no operation moved by 1% of the time
where the time goes in v5:
time: 275 us; the launch traced here: 273 us
  waiting for transfers between devices  154 us (56%)
  starting transfers between devices  59.6 us (22%)
  Pallas kernels  54.9 us (20%)
    all_to_all x4, waiting for transfers between devices, exchange(): return lax.all_to_all(blocks, HALF, split_axis=0, concat_axis=0, tiled=True)  48 us
    ppermute x3, waiting for transfers between devices, along_line(): high = lax.ppermute(high, LINE, downs)  43.2 us
    ppermute x2, waiting for transfers between devices, across(): return lax.ppermute(block, 'half', [(0, 1), (1, 0)])  38.3 us
    ppermute x21, waiting for transfers between devices, among_peers(): parts.append(lax.ppermute(picks[j], ALL, pairs))  24.2 us
    all_to_all x4, starting transfers between devices, exchange(): return lax.all_to_all(blocks, HALF, split_axis=0, concat_axis=0, tiled=True)  23.4 us
    pallas_call x3, Pallas kernels, back(): pl.pallas_call(functools.partial(back_kernel, wide, peers, slot_count, la...  18 us
    ppermute x21, starting transfers between devices, among_peers(): parts.append(lax.ppermute(picks[j], ALL, pairs))  17.8 us
    pallas_call x3, Pallas kernels, picked(): pl.pallas_call(functools.partial(held_pick_kernel if held else pick_kerne...  8.95 us
  transfers between devices with their start and end apart: 33, of which 17 were waited for; matrix products, arithmetic and copies ran while one was open for 1% of the time, Pallas kernels for 15%

profile of v5, /device:TPU:0, one launch (start us, length us, event | category | flops | bytes accessed | tf_op | source)
XLA Modules:
  0.0 273.3 jit_solution(17586530433617785200)
XLA Ops:
  1.3 4.2 %slot_grads.3 = bf16[4,768,256]{2,1,0:T(8,128)(2,1)} custom-call(s32[1]{0:T(128)} %bitcast.12.half_ref, s32[1]{0:T(128)S(6)} %copy.18.rest_9_.count_ref, bf16[512,768]{1,0:T(8,128)(2,1)} %rows_ref.5, bf16[512,2048]{1,0:T(8,128)(2,1)} %cot_ref.3, f32[1,512]{1,0:T(1,128)} %bitcast.22), custom_call_target="tpu_custom_call" | custom-call | tf_op jit(solution)/shard_map/slot_grads/pallas_call | solution.py:53
  5.5 6.4 %all-to-all-start.1 = ((bf16[16,192,256]{2,1,0:T(8,128)(2,1)}), bf16[16,192,256]{2,1,0:T(8,128)(2,1)}, u32[]{:S(2)}, u32[]{:S(2)}) async-start(bf16[16,192,256]{2,1,0:T(8,128)(2,1)} %bitcast.21), calls=%async_computation.1 | async-start | bytes 3145728 | tf_op jit(solution)/shard_map/all_to_all | solution.py:399
  11.9 4.2 %slot_grads.2 = bf16[4,768,256]{2,1,0:T(8,128)(2,1)} custom-call(s32[1]{0:T(128)} %bitcast.10.half_ref, s32[1]{0:T(128)S(6)} %copy.18.rest_9_.count_ref, bf16[512,768]{1,0:T(8,128)(2,1)} %rows_ref.5, bf16[512,2048]{1,0:T(8,128)(2,1)} %cot_ref.3, f32[1,512]{1,0:T(1,128)} %bitcast.23), custom_call_target="tpu_custom_call" | custom-call | tf_op jit(solution)/shard_map/slot_grads/pallas_call | solution.py:53
  16.1 18.6 %all-to-all-done.1.grads_ref = bf16[16,192,256]{2,1,0:T(8,128)(2,1)} async-done(((bf16[16,192,256]{2,1,0:T(8,128)(2,1)}), bf16[16,192,256]{2,1,0:T(8,128)(2,1)}, u32[]{:S(2)}, u32[]{:S(2)}) %all-to-all-start.1) | async-done | bytes 1572896 | tf_op jit(solution)/shard_map/all_to_all | solution.py:399
  34.6 4.4 %all-to-all-start = ((bf16[16,192,256]{2,1,0:T(8,128)(2,1)}), bf16[16,192,256]{2,1,0:T(8,128)(2,1)}, u32[]{:S(2)}, u32[]{:S(2)}) async-start(bf16[16,192,256]{2,1,0:T(8,128)(2,1)} %bitcast.20), calls=%async_computation | async-start | bytes 3145728 | tf_op jit(solution)/shard_map/all_to_all | solution.py:399
  39.1 0.6 fusion.1.place_ref.old_ref
  39.7 4.4 %expert_sums.1 = bf16[8,192,256]{2,1,0:T(8,128)(2,1)} custom-call(s32[16]{0:T(128)} %fusion.1.place_ref.old_ref, bf16[16,192,256]{2,1,0:T(8,128)(2,1)} %all-to-all-done.1.grads_ref), custom_call_target="tpu_custom_call" | custom-call | tf_op jit(solution)/shard_map/expert_sums/pallas_call | solution.py:96
  44.0 2.6 collective-permute-start.27
  46.6 0.6 fusion.2.new_ref.wanted_ref
  47.2 28.1 %all-to-all-done.grads_ref = bf16[16,192,256]{2,1,0:T(8,128)(2,1)} async-done(((bf16[16,192,256]{2,1,0:T(8,128)(2,1)}), bf16[16,192,256]{2,1,0:T(8,128)(2,1)}, u32[]{:S(2)}, u32[]{:S(2)}) %all-to-all-start) | async-done | bytes 1572896 | tf_op jit(solution)/shard_map/all_to_all | solution.py:399
  75.2 6.6 %collective-permute-done.27.sums_ref = bf16[8,192,256]{2,1,0:T(8,128)(2,1)} collective-permute-done((bf16[8,192,256]{2,1,0:T(8,128)(2,1)}, bf16[8,192,256]{2,1,0:T(8,128)(2,1)}, u32[]{:S(2)}, u32[]{:S(2)}) %collective-permute-start.27) | collective-permute-done | bytes 786464 | tf_op jit(solution)/shard_map/ppermute | solution.py:403
  81.8 6.1 %update.1 = (f32[8,192,256]{2,1,0:T(8,128)}, bf16[8,192,256]{2,1,0:T(8,128)(2,1)}, bf16[8,192,256]{2,1,0:T(8,128)(2,1)}, bf16[8,192,256]{2,1,0:T(8,128)(2,1)}, bf16[16,192,256]{2,1,0:T(8,128)(2,1)}) custom-call(s32[16]{0:T(128)} %fusion.1.place_ref.old_ref, s32[16]{0:T(128)} %fusion.2.new_ref.wanted_ref, bf16[16,192,256]{2,1,0:T(8,128)(2,1)} %all-to-all-done.grads_ref, ...), custom_call_target="tpu_custom_call" | custom-call | tf_op jit(solution)/shard_map/update/pallas_call | solution.py:144
  87.9 4.5 %all-to-all-start.3 = ((bf16[16,192,256]{2,1,0:T(8,128)(2,1)}), bf16[16,192,256]{2,1,0:T(8,128)(2,1)}, u32[]{:S(2)}, u32[]{:S(2)}) async-start(bf16[16,192,256]{2,1,0:T(8,128)(2,1)} %get-tuple-element.67), calls=%async_computation.3 | async-start | bytes 3145728 | tf_op jit(solution)/shard_map/all_to_all | solution.py:399
  92.5 3.2 %collective-permute-start.28 = (bf16[8,192,256]{2,1,0:T(8,128)(2,1)S(1)}, bf16[8,192,256]{2,1,0:T(8,128)(2,1)}, u32[]{:S(2)}, u32[]{:S(2)}) collective-permute-start(bf16[8,192,256]{2,1,0:T(8,128)(2,1)S(1)} %copy-done.3), channel_id=1, source_target_pairs={{0,16},{16,0},{1,17},{17,1},{2,18},{18,2},{3,19},{19,3},{4,20},{20... | collective-permute-start | bytes 2359304 | tf_op jit(solution)/shard_map/ppermute | solution.py:403
  95.7 31.7 %collective-permute-done.28.block_ref = bf16[8,192,256]{2,1,0:T(8,128)(2,1)} collective-permute-done((bf16[8,192,256]{2,1,0:T(8,128)(2,1)S(1)}, bf16[8,192,256]{2,1,0:T(8,128)(2,1)}, u32[]{:S(2)}, u32[]{:S(2)}) %collective-permute-start.28) | collective-permute-done | bytes 786464 | tf_op jit(solution)/shard_map/ppermute | solution.py:403
  127.3 2.4 half_picked.1
  129.8 1.3 all-to-all-done.3
  131.1 8.1 %all-to-all-start.2 = ((bf16[16,192,256]{2,1,0:T(8,128)(2,1)}), bf16[16,192,256]{2,1,0:T(8,128)(2,1)}, u32[]{:S(2)}, u32[]{:S(2)}) async-start(bf16[16,192,256]{2,1,0:T(8,128)(2,1)} %half_picked.1), calls=%async_computation.2 | async-start | bytes 3145728 | tf_op jit(solution)/shard_map/all_to_all | solution.py:399
  139.2 0.1 convert_element_type.13.rest_0_
  139.3 1.3 collective-permute-start.3
  140.7 5.5 %collective-permute-start = (bf16[8,192,256]{2,1,0:T(8,128)(2,1)S(1)}, bf16[8,192,256]{2,1,0:T(8,128)(2,1)}, u32[]{:S(2)}, u32[]{:S(2)}) collective-permute-start(bf16[8,192,256]{2,1,0:T(8,128)(2,1)S(1)} %convert_element_type.13.rest_0_), channel_id=1, source_target_pairs={{0,8},{4,12},{8,16},{12,20},{16,24},{20,28},{1,9},{5,13},{9,17},{1... | collective-permute-start | bytes 2359304 | tf_op jit(solution)/shard_map/ppermute | solution.py:231
  146.1 30.1 %collective-permute-done.3.rest_2_ = bf16[8,192,256]{2,1,0:T(8,128)(2,1)} collective-permute-done((bf16[8,192,256]{2,1,0:T(8,128)(2,1)S(1)}, bf16[8,192,256]{2,1,0:T(8,128)(2,1)}, u32[]{:S(2)}, u32[]{:S(2)}) %collective-permute-start.3) | collective-permute-done | bytes 786464 | tf_op jit(solution)/shard_map/ppermute | solution.py:232
  176.2 1.3 collective-permute-start.4
  177.5 1.6 collective-permute-start.1
  179.2 1.2 gather_fusion
  180.3 3.8 %picked.5 = (bf16[3,192,256]{2,1,0:T(8,128)(2,1)}, bf16[3,192,256]{2,1,0:T(8,128)(2,1)}, bf16[3,192,256]{2,1,0:T(8,128)(2,1)}, bf16[3,192,256]{2,1,0:T(8,128)(2,...) custom-call(s32[1]{0:T(128)} %bitcast.1.plane_ref, ...), custom_call_target="tpu_custom_call" | custom-call | tf_op jit(solution)/shard_map/picked/pallas_call | solution.py:268
  184.2 0.1 collective-permute-start.20
  184.2 13.1 %collective-permute-done.4.rest_1_ = bf16[8,192,256]{2,1,0:T(8,128)(2,1)} collective-permute-done((bf16[8,192,256]{2,1,0:T(8,128)(2,1)}, bf16[8,192,256]{2,1,0:T(8,128)(2,1)}, u32[]{:S(2)}, u32[]{:S(2)}) %collective-permute-start.4) | collective-permute-done | bytes 786464 | tf_op jit(solution)/shard_map/ppermute | solution.py:232
  197.4 1.3 collective-permute-start.5
  198.7 1.6 collective-permute-start.2
  200.3 2.9 %collective-permute-start.21 = (bf16[3,192,256]{2,1,0:T(8,128)(2,1)}, bf16[3,192,256]{2,1,0:T(8,128)(2,1)}, u32[]{:S(2)}, u32[]{:S(2)}) collective-permute-start(bf16[3,192,256]{2,1,0:T(8,128)(2,1)} %get-tuple-element.55), channel_id=1, source_target_pairs={{0,2},{1,3},{2,0},{3,1},{4,6},{5,7},{6,4},{7,5},{8,10},{9,11},{10,... | collective-permute-start | bytes 884744 | tf_op jit(solution)/shard_map/ppermute | solution.py:304
  203.1 0.9 collective-permute-start.23
  204.1 7.2 %collective-permute-done.21.rest_2_ = bf16[3,192,256]{2,1,0:T(8,128)(2,1)} collective-permute-done((bf16[3,192,256]{2,1,0:T(8,128)(2,1)}, bf16[3,192,256]{2,1,0:T(8,128)(2,1)}, u32[]{:S(2)}, u32[]{:S(2)}) %collective-permute-start.21) | collective-permute-done | bytes 294944 | tf_op jit(solution)/shard_map/ppermute | solution.py:304
  211.3 3.6 %collective-permute-done.22.rest_3_ = bf16[3,192,256]{2,1,0:T(8,128)(2,1)} collective-permute-done((bf16[3,192,256]{2,1,0:T(8,128)(2,1)}, bf16[3,192,256]{2,1,0:T(8,128)(2,1)}, u32[]{:S(2)}, u32[]{:S(2)}) %collective-permute-start.22) | collective-permute-done | bytes 294944 | tf_op jit(solution)/shard_map/ppermute | solution.py:304
  214.9 0.7 collective-permute-start.25
  215.6 2.4 collective-permute-start.26
  218.0 2.8 %picked.4 = (bf16[1,192,256]{2,1,0:T(8,128)(2,1)}, bf16[1,192,256]{2,1,0:T(8,128)(2,1)}, bf16[1,192,256]{2,1,0:T(8,128)(2,1)}, bf16[1,192,256]{2,1,0:T(8,128)(2,...) custom-call(s32[1]{0:T(128)} %bitcast.1.plane_ref, ...), custom_call_target="tpu_custom_call" | custom-call | tf_op jit(solution)/shard_map/picked/pallas_call | solution.py:268
  220.8 0.1 collective-permute-done.24.rest_5_
  220.9 6.8 %collective-permute-done.25.rest_6_ = bf16[3,192,256]{2,1,0:T(8,128)(2,1)} collective-permute-done((bf16[3,192,256]{2,1,0:T(8,128)(2,1)}, bf16[3,192,256]{2,1,0:T(8,128)(2,1)}, u32[]{:S(2)}, u32[]{:S(2)}) %collective-permute-start.25) | collective-permute-done | bytes 294944 | tf_op jit(solution)/shard_map/ppermute | solution.py:304
  227.7 2.2 collective-permute-start.15
  229.9 0.9 collective-permute-start.16
  230.8 2.3 picked.3
  233.1 1.9 collective-permute-done.26.rest_7_
  235.1 0.2 collective-permute-start.18
  235.3 1.4 collective-permute-done.14.rest_2_
  236.7 1.8 collective-permute-start.19
  238.4 0.3 collective-permute-done.15.rest_3_
  238.7 0.1 collective-permute-start.6
  238.9 0.5 collective-permute-start.7
  239.3 0.5 and_convert_fusion.valid_ref
  239.8 0.7 collective-permute-done.17.rest_5_
  240.5 0.6 collective-permute-start.8
  241.1 0.8 collective-permute-done.18.rest_6_
  241.9 0.8 collective-permute-start.9
  242.7 1.5 collective-permute-done.19.rest_7_
  244.2 0.4 collective-permute-start.10
  244.5 1.9 collective-permute-start.11
  246.4 1.6 collective-permute-start.12
  247.9 0.6 add_clamp_fusion.plane_ref
  248.5 7.7 %back.3.rest_9_ = f32[512,768]{1,0:T(8,128)} custom-call(s32[1]{0:T(128)} %bitcast.me_ref, s32[3]{0:T(128)} %add_clamp_fusion.plane_ref, s32[3]{0:T(128)} %and_convert_fusion.valid_ref, bf16[3,192,256]{2,1,0:T(8,128)(2,1)} %get-tuple-element.53.rest_0_, bf16[3,192,256]{2,1,0:T(8,128)(2,1)} %collective-permute-done.20.rest_1_, ...), custom_call_target="tpu_custom_call" | custom-call | tf_op jit(solution)/shard_map/back/pallas_call | solution.py:381
  256.2 4.9 %back.4.rest_12_ = f32[512,768]{1,0:T(8,128)} custom-call(s32[1]{0:T(128)} %bitcast.me_ref, s32[1]{0:T(128)S(6)} %min.19.plane_ref, s32[1]{0:T(128)S(6)} %convert_element_type.14.valid_ref, bf16[1,192,256]{2,1,0:T(8,128)(2,1)} %get-tuple-element.45.rest_0_, bf16[1,192,256]{2,1,0:T(8,128)(2,1)} %collective-permute-done.13.rest_1_, ...), custom_call_target="tpu_custom_call" | custom-call | tf_op jit(solution)/shard_map/back/pallas_call | solution.py:381
  261.2 5.4 %back.5 = (bf16[512,768]{1,0:T(8,128)(2,1)}, f32[1,512]{1,0:T(1,128)}) custom-call(s32[1]{0:T(128)} %bitcast.me_ref, s32[1]{0:T(128)S(6)} %min.18.plane_ref, s32[1]{0:T(128)S(6)} %convert_element_type.12.valid_ref, bf16[1,192,256]{2,1,0:T(8,128)(2,1)} %get-tuple-element.37.rest_0_, bf16[1,192,256]{2,1,0:T(8,128)(2,1)} %collective-permute-done.6.rest_1_, ...), custom_call_target="tpu_custom_call" | custom-call | tf_op jit(solution)/shard_map/back/pallas_call | solution.py:381
  266.6 3.4 %next_rows.2.rest_0_ = bf16[512,2048]{1,0:T(8,128)(2,1)} custom-call(s32[1]{0:T(128)} %bitcast.10.half_ref, bf16[512,768]{1,0:T(8,128)(2,1)} %rows_ref.7, bf16[4,768,256]{2,1,0:T(8,128)(2,1)} %bitcast.15.weight_ref), custom_call_target="tpu_custom_call" | custom-call | tf_op jit(solution)/shard_map/next_rows/pallas_call | solution.py:183
  270.0 3.4 %next_rows.3 = bf16[512,2048]{1,0:T(8,128)(2,1)} custom-call(s32[1]{0:T(128)} %bitcast.12.half_ref, bf16[512,768]{1,0:T(8,128)(2,1)} %rows_ref.7, bf16[4,768,256]{2,1,0:T(8,128)(2,1)} %bitcast.14.weight_ref, bf16[512,2048]{1,0:T(8,128)(2,1)} %next_rows.2.rest_0_), custom_call_target="tpu_custom_call", output_to_operand_aliasing={{}: (3, {})} | custom-call | tf_op jit(solution)/shard_map/next_rows/pallas_call | solution.py:183
  (36 shorter events, 0.2 us)
Async XLA Ops:
  0.6 38.4 %copy-start = (s32[32,1]{0,1:T(1,128)S(1)}, s32[32,1]{0,1:T(1,128)}, u32[]{:S(2)}) copy-start(s32[32,1]{0,1:T(1,128)} %param.14) | copy-start | bytes 388
  5.5 29.1 %all-to-all-start.1 = ((bf16[16,192,256]{2,1,0:T(8,128)(2,1)}), bf16[16,192,256]{2,1,0:T(8,128)(2,1)}, u32[]{:S(2)}, u32[]{:S(2)}) async-start(bf16[16,192,256]{2,1,0:T(8,128)(2,1)} %bitcast.21), calls=%async_computation.1 | async-start | bytes 3145728 | tf_op jit(solution)/shard_map/all_to_all | solution.py:399
  34.6 40.6 %all-to-all-start = ((bf16[16,192,256]{2,1,0:T(8,128)(2,1)}), bf16[16,192,256]{2,1,0:T(8,128)(2,1)}, u32[]{:S(2)}, u32[]{:S(2)}) async-start(bf16[16,192,256]{2,1,0:T(8,128)(2,1)} %bitcast.20), calls=%async_computation | async-start | bytes 3145728 | tf_op jit(solution)/shard_map/all_to_all | solution.py:399
  39.1 7.6 %copy-start.4 = (s32[32,1]{0,1:T(1,128)S(1)}, s32[32,1]{0,1:T(1,128)}, u32[]{:S(2)}) copy-start(s32[32,1]{0,1:T(1,128)} %param.15) | copy-start | bytes 388
  44.0 37.8 %collective-permute-start.27 = (bf16[8,192,256]{2,1,0:T(8,128)(2,1)}, bf16[8,192,256]{2,1,0:T(8,128)(2,1)}, u32[]{:S(2)}, u32[]{:S(2)}) collective-permute-start(bf16[8,192,256]{2,1,0:T(8,128)(2,1)} %expert_sums.1), channel_id=1, source_target_pairs={{0,16},{16,0},{1,17},{17,1},{2,18},{18,2},{3,19},{19,3},{4,20},{20... | collective-permute-start | bytes 2359304 | tf_op jit(solution)/shard_map/ppermute | solution.py:403
  87.9 4.6 %copy-start.3 = (bf16[8,192,256]{2,1,0:T(8,128)(2,1)S(1)}, bf16[8,192,256]{2,1,0:T(8,128)(2,1)}, u32[]{:S(2)}) copy-start(bf16[8,192,256]{2,1,0:T(8,128)(2,1)} %get-tuple-element.66) | copy-start | bytes 2359300
  87.9 43.2 %all-to-all-start.3 = ((bf16[16,192,256]{2,1,0:T(8,128)(2,1)}), bf16[16,192,256]{2,1,0:T(8,128)(2,1)}, u32[]{:S(2)}, u32[]{:S(2)}) async-start(bf16[16,192,256]{2,1,0:T(8,128)(2,1)} %get-tuple-element.67), calls=%async_computation.3 | async-start | bytes 3145728 | tf_op jit(solution)/shard_map/all_to_all | solution.py:399
  92.5 34.9 %collective-permute-start.28 = (bf16[8,192,256]{2,1,0:T(8,128)(2,1)S(1)}, bf16[8,192,256]{2,1,0:T(8,128)(2,1)}, u32[]{:S(2)}, u32[]{:S(2)}) collective-permute-start(bf16[8,192,256]{2,1,0:T(8,128)(2,1)S(1)} %copy-done.3), channel_id=1, source_target_pairs={{0,16},{16,0},{1,17},{17,1},{2,18},{18,2},{3,19},{19,3},{4,20},{20... | collective-permute-start | bytes 2359304 | tf_op jit(solution)/shard_map/ppermute | solution.py:403
  129.8 9.5 %copy-start.1 = (f32[8,192,256]{2,1,0:T(8,128)S(1)}, f32[8,192,256]{2,1,0:T(8,128)}, u32[]{:S(2)}) copy-start(f32[8,192,256]{2,1,0:T(8,128)} %master_ref.1) | copy-start | bytes 4718596
  131.1 138.8 %all-to-all-start.2 = ((bf16[16,192,256]{2,1,0:T(8,128)(2,1)}), bf16[16,192,256]{2,1,0:T(8,128)(2,1)}, u32[]{:S(2)}, u32[]{:S(2)}) async-start(bf16[16,192,256]{2,1,0:T(8,128)(2,1)} %half_picked.1), calls=%async_computation.2 | async-start | bytes 3145728 | tf_op jit(solution)/shard_map/all_to_all | solution.py:399
  139.3 1.3 copy-start.2
  139.3 36.9 %collective-permute-start.3 = (bf16[8,192,256]{2,1,0:T(8,128)(2,1)S(1)}, bf16[8,192,256]{2,1,0:T(8,128)(2,1)}, u32[]{:S(2)}, u32[]{:S(2)}) collective-permute-start(bf16[8,192,256]{2,1,0:T(8,128)(2,1)S(1)} %convert_element_type.13.rest_0_), channel_id=1, source_target_pairs={{8,0},{12,4},{16,8},{20,12},{24,16},{28,20},{9,1},{13,5},{17,9},{2... | collective-permute-start | bytes 2359304 | tf_op jit(solution)/shard_map/ppermute | solution.py:232
  140.7 36.8 %collective-permute-start = (bf16[8,192,256]{2,1,0:T(8,128)(2,1)S(1)}, bf16[8,192,256]{2,1,0:T(8,128)(2,1)}, u32[]{:S(2)}, u32[]{:S(2)}) collective-permute-start(bf16[8,192,256]{2,1,0:T(8,128)(2,1)S(1)} %convert_element_type.13.rest_0_), channel_id=1, source_target_pairs={{0,8},{4,12},{8,16},{12,20},{16,24},{20,28},{1,9},{5,13},{9,17},{1... | collective-permute-start | bytes 2359304 | tf_op jit(solution)/shard_map/ppermute | solution.py:231
  176.2 21.2 %collective-permute-start.4 = (bf16[8,192,256]{2,1,0:T(8,128)(2,1)}, bf16[8,192,256]{2,1,0:T(8,128)(2,1)}, u32[]{:S(2)}, u32[]{:S(2)}) collective-permute-start(bf16[8,192,256]{2,1,0:T(8,128)(2,1)} %collective-permute-done.3.rest_2_), channel_id=1, source_target_pairs={{8,0},{12,4},{16,8},{20,12},{9,1},{13,5},{17,9},{21,13},{10,2},{14... | collective-permute-start | bytes 2359304 | tf_op jit(solution)/shard_map/ppermute | solution.py:232
  177.5 21.2 %collective-permute-start.1 = (bf16[8,192,256]{2,1,0:T(8,128)(2,1)}, bf16[8,192,256]{2,1,0:T(8,128)(2,1)}, u32[]{:S(2)}, u32[]{:S(2)}) collective-permute-start(bf16[8,192,256]{2,1,0:T(8,128)(2,1)} %collective-permute-done.rest_1_), channel_id=1, source_target_pairs={{8,16},{12,20},{16,24},{20,28},{9,17},{13,21},{17,25},{21,29},{10,... | collective-permute-start | bytes 2359304 | tf_op jit(solution)/shard_map/ppermute | solution.py:231
  184.2 19.0 %collective-permute-start.20 = (bf16[3,192,256]{2,1,0:T(8,128)(2,1)}, bf16[3,192,256]{2,1,0:T(8,128)(2,1)}, u32[]{:S(2)}, u32[]{:S(2)}) collective-permute-start(bf16[3,192,256]{2,1,0:T(8,128)(2,1)} %get-tuple-element.54), channel_id=1, source_target_pairs={{0,1},{1,0},{2,3},{3,2},{4,5},{5,4},{6,7},{7,6},{8,9},{9,8},{10,11... | collective-permute-start | bytes 884744 | tf_op jit(solution)/shard_map/ppermute | solution.py:304
  197.4 30.3 %collective-permute-start.5 = (bf16[8,192,256]{2,1,0:T(8,128)(2,1)}, bf16[8,192,256]{2,1,0:T(8,128)(2,1)}, u32[]{:S(2)}, u32[]{:S(2)}) collective-permute-start(bf16[8,192,256]{2,1,0:T(8,128)(2,1)} %collective-permute-done.4.rest_1_), channel_id=1, source_target_pairs={{8,0},{12,4},{9,1},{13,5},{10,2},{14,6},{11,3},{15,7}} | collective-permute-start | bytes 2359304 | tf_op jit(solution)/shard_map/ppermute | solution.py:232
  198.7 31.2 %collective-permute-start.2 = (bf16[8,192,256]{2,1,0:T(8,128)(2,1)}, bf16[8,192,256]{2,1,0:T(8,128)(2,1)}, u32[]{:S(2)}, u32[]{:S(2)}) collective-permute-start(bf16[8,192,256]{2,1,0:T(8,128)(2,1)} %collective-permute-done.1.rest_0_), channel_id=1, source_target_pairs={{16,24},{20,28},{17,25},{21,29},{18,26},{22,30},{19,27},{23,31}} | collective-permute-start | bytes 2359304 | tf_op jit(solution)/shard_map/ppermute | solution.py:231
  200.3 11.0 %collective-permute-start.21 = (bf16[3,192,256]{2,1,0:T(8,128)(2,1)}, bf16[3,192,256]{2,1,0:T(8,128)(2,1)}, u32[]{:S(2)}, u32[]{:S(2)}) collective-permute-start(bf16[3,192,256]{2,1,0:T(8,128)(2,1)} %get-tuple-element.55), channel_id=1, source_target_pairs={{0,2},{1,3},{2,0},{3,1},{4,6},{5,7},{6,4},{7,5},{8,10},{9,11},{10,... | collective-permute-start | bytes 884744 | tf_op jit(solution)/shard_map/ppermute | solution.py:304
  203.1 11.8 %collective-permute-start.22 = (bf16[3,192,256]{2,1,0:T(8,128)(2,1)}, bf16[3,192,256]{2,1,0:T(8,128)(2,1)}, u32[]{:S(2)}, u32[]{:S(2)}) collective-permute-start(bf16[3,192,256]{2,1,0:T(8,128)(2,1)} %get-tuple-element.56), channel_id=1, source_target_pairs={{0,3},{1,2},{2,1},{3,0},{4,7},{5,6},{6,5},{7,4},{8,11},{9,10},{10,... | collective-permute-start | bytes 884744 | tf_op jit(solution)/shard_map/ppermute | solution.py:304
  203.1 12.4 %collective-permute-start.23 = (bf16[3,192,256]{2,1,0:T(8,128)(2,1)}, bf16[3,192,256]{2,1,0:T(8,128)(2,1)}, u32[]{:S(2)}, u32[]{:S(2)}) collective-permute-start(bf16[3,192,256]{2,1,0:T(8,128)(2,1)} %get-tuple-element.57), channel_id=1, source_target_pairs={{0,4},{1,5},{2,6},{3,7},{4,0},{5,1},{6,2},{7,3},{8,12},{9,13},{10,... | collective-permute-start | bytes 884744 | tf_op jit(solution)/shard_map/ppermute | solution.py:304
  211.3 9.6 %collective-permute-start.24 = (bf16[3,192,256]{2,1,0:T(8,128)(2,1)}, bf16[3,192,256]{2,1,0:T(8,128)(2,1)}, u32[]{:S(2)}, u32[]{:S(2)}) collective-permute-start(bf16[3,192,256]{2,1,0:T(8,128)(2,1)} %get-tuple-element.58), channel_id=1, source_target_pairs={{0,5},{1,4},{2,7},{3,6},{4,1},{5,0},{6,3},{7,2},{8,13},{9,12},{10,... | collective-permute-start | bytes 884744 | tf_op jit(solution)/shard_map/ppermute | solution.py:304
  214.9 12.8 %collective-permute-start.25 = (bf16[3,192,256]{2,1,0:T(8,128)(2,1)}, bf16[3,192,256]{2,1,0:T(8,128)(2,1)}, u32[]{:S(2)}, u32[]{:S(2)}) collective-permute-start(bf16[3,192,256]{2,1,0:T(8,128)(2,1)} %get-tuple-element.59), channel_id=1, source_target_pairs={{0,6},{1,7},{2,4},{3,5},{4,2},{5,3},{6,0},{7,1},{8,14},{9,15},{10,... | collective-permute-start | bytes 884744 | tf_op jit(solution)/shard_map/ppermute | solution.py:304
  215.6 23.8 %copy-start.5 = (s32[3]{0:T(128)S(1)}, s32[3]{0:T(128)}, u32[]{:S(2)}) copy-start(s32[3]{0:T(128)} %constant.67.clone.1) | copy-start | bytes 40
  215.6 19.5 %collective-permute-start.26 = (bf16[3,192,256]{2,1,0:T(8,128)(2,1)}, bf16[3,192,256]{2,1,0:T(8,128)(2,1)}, u32[]{:S(2)}, u32[]{:S(2)}) collective-permute-start(bf16[3,192,256]{2,1,0:T(8,128)(2,1)} %get-tuple-element.60), channel_id=1, source_target_pairs={{0,7},{1,6},{2,5},{3,4},{4,3},{5,2},{6,1},{7,0},{8,15},{9,14},{10,... | collective-permute-start | bytes 884744 | tf_op jit(solution)/shard_map/ppermute | solution.py:304
  220.9 14.1 %collective-permute-start.13 = (bf16[1,192,256]{2,1,0:T(8,128)(2,1)}, bf16[1,192,256]{2,1,0:T(8,128)(2,1)}, u32[]{:S(2)}, u32[]{:S(2)}) collective-permute-start(bf16[1,192,256]{2,1,0:T(8,128)(2,1)} %get-tuple-element.46), channel_id=1, source_target_pairs={{0,1},{1,0},{2,3},{3,2},{4,5},{5,4},{6,7},{7,6},{8,9},{9,8},{10,11... | collective-permute-start | bytes 294920 | tf_op jit(solution)/shard_map/ppermute | solution.py:304
  227.7 8.9 %collective-permute-start.14 = (bf16[1,192,256]{2,1,0:T(8,128)(2,1)}, bf16[1,192,256]{2,1,0:T(8,128)(2,1)}, u32[]{:S(2)}, u32[]{:S(2)}) collective-permute-start(bf16[1,192,256]{2,1,0:T(8,128)(2,1)} %get-tuple-element.47), channel_id=1, source_target_pairs={{0,2},{1,3},{2,0},{3,1},{4,6},{5,7},{6,4},{7,5},{8,10},{9,11},{10,... | collective-permute-start | bytes 294920 | tf_op jit(solution)/shard_map/ppermute | solution.py:304
  227.7 11.0 %collective-permute-start.15 = (bf16[1,192,256]{2,1,0:T(8,128)(2,1)}, bf16[1,192,256]{2,1,0:T(8,128)(2,1)}, u32[]{:S(2)}, u32[]{:S(2)}) collective-permute-start(bf16[1,192,256]{2,1,0:T(8,128)(2,1)} %get-tuple-element.48), channel_id=1, source_target_pairs={{0,3},{1,2},{2,1},{3,0},{4,7},{5,6},{6,5},{7,4},{8,11},{9,10},{10,... | collective-permute-start | bytes 294920 | tf_op jit(solution)/shard_map/ppermute | solution.py:304
  229.9 9.0 %collective-permute-start.16 = (bf16[1,192,256]{2,1,0:T(8,128)(2,1)}, bf16[1,192,256]{2,1,0:T(8,128)(2,1)}, u32[]{:S(2)}, u32[]{:S(2)}) collective-permute-start(bf16[1,192,256]{2,1,0:T(8,128)(2,1)} %get-tuple-element.49), channel_id=1, source_target_pairs={{0,4},{1,5},{2,6},{3,7},{4,0},{5,1},{6,2},{7,3},{8,12},{9,13},{10,... | collective-permute-start | bytes 294920 | tf_op jit(solution)/shard_map/ppermute | solution.py:304
  235.1 5.4 %collective-permute-start.17 = (bf16[1,192,256]{2,1,0:T(8,128)(2,1)}, bf16[1,192,256]{2,1,0:T(8,128)(2,1)}, u32[]{:S(2)}, u32[]{:S(2)}) collective-permute-start(bf16[1,192,256]{2,1,0:T(8,128)(2,1)} %get-tuple-element.50), channel_id=1, source_target_pairs={{0,5},{1,4},{2,7},{3,6},{4,1},{5,0},{6,3},{7,2},{8,13},{9,12},{10,... | collective-permute-start | bytes 294920 | tf_op jit(solution)/shard_map/ppermute | solution.py:304
  235.1 6.8 %collective-permute-start.18 = (bf16[1,192,256]{2,1,0:T(8,128)(2,1)}, bf16[1,192,256]{2,1,0:T(8,128)(2,1)}, u32[]{:S(2)}, u32[]{:S(2)}) collective-permute-start(bf16[1,192,256]{2,1,0:T(8,128)(2,1)} %get-tuple-element.51), channel_id=1, source_target_pairs={{0,6},{1,7},{2,4},{3,5},{4,2},{5,3},{6,0},{7,1},{8,14},{9,15},{10,... | collective-permute-start | bytes 294920 | tf_op jit(solution)/shard_map/ppermute | solution.py:304
  236.7 7.5 %collective-permute-start.19 = (bf16[1,192,256]{2,1,0:T(8,128)(2,1)}, bf16[1,192,256]{2,1,0:T(8,128)(2,1)}, u32[]{:S(2)}, u32[]{:S(2)}) collective-permute-start(bf16[1,192,256]{2,1,0:T(8,128)(2,1)} %get-tuple-element.52), channel_id=1, source_target_pairs={{0,7},{1,6},{2,5},{3,4},{4,3},{5,2},{6,1},{7,0},{8,15},{9,14},{10,... | collective-permute-start | bytes 294920 | tf_op jit(solution)/shard_map/ppermute | solution.py:304
  238.7 5.8 %collective-permute-start.6 = (bf16[1,192,256]{2,1,0:T(8,128)(2,1)}, bf16[1,192,256]{2,1,0:T(8,128)(2,1)}, u32[]{:S(2)}, u32[]{:S(2)}) collective-permute-start(bf16[1,192,256]{2,1,0:T(8,128)(2,1)} %get-tuple-element.38), channel_id=1, source_target_pairs={{0,1},{1,0},{2,3},{3,2},{4,5},{5,4},{6,7},{7,6},{8,9},{9,8},{10,11... | collective-permute-start | bytes 294920 | tf_op jit(solution)/shard_map/ppermute | solution.py:304
  238.9 7.5 %collective-permute-start.7 = (bf16[1,192,256]{2,1,0:T(8,128)(2,1)}, bf16[1,192,256]{2,1,0:T(8,128)(2,1)}, u32[]{:S(2)}, u32[]{:S(2)}) collective-permute-start(bf16[1,192,256]{2,1,0:T(8,128)(2,1)} %get-tuple-element.39), channel_id=1, source_target_pairs={{0,2},{1,3},{2,0},{3,1},{4,6},{5,7},{6,4},{7,5},{8,10},{9,11},{10,... | collective-permute-start | bytes 294920 | tf_op jit(solution)/shard_map/ppermute | solution.py:304
  240.5 20.6 %collective-permute-start.8 = (bf16[1,192,256]{2,1,0:T(8,128)(2,1)}, bf16[1,192,256]{2,1,0:T(8,128)(2,1)}, u32[]{:S(2)}, u32[]{:S(2)}) collective-permute-start(bf16[1,192,256]{2,1,0:T(8,128)(2,1)} %get-tuple-element.40), channel_id=1, source_target_pairs={{0,3},{1,2},{2,1},{3,0},{4,7},{5,6},{6,5},{7,4},{8,11},{9,10},{10,... | collective-permute-start | bytes 294920 | tf_op jit(solution)/shard_map/ppermute | solution.py:304
  241.9 19.2 %collective-permute-start.9 = (bf16[1,192,256]{2,1,0:T(8,128)(2,1)}, bf16[1,192,256]{2,1,0:T(8,128)(2,1)}, u32[]{:S(2)}, u32[]{:S(2)}) collective-permute-start(bf16[1,192,256]{2,1,0:T(8,128)(2,1)} %get-tuple-element.41), channel_id=1, source_target_pairs={{0,4},{1,5},{2,6},{3,7},{4,0},{5,1},{6,2},{7,3},{8,12},{9,13},{10,... | collective-permute-start | bytes 294920 | tf_op jit(solution)/shard_map/ppermute | solution.py:304
  244.2 17.0 %collective-permute-start.10 = (bf16[1,192,256]{2,1,0:T(8,128)(2,1)}, bf16[1,192,256]{2,1,0:T(8,128)(2,1)}, u32[]{:S(2)}, u32[]{:S(2)}) collective-permute-start(bf16[1,192,256]{2,1,0:T(8,128)(2,1)} %get-tuple-element.42), channel_id=1, source_target_pairs={{0,5},{1,4},{2,7},{3,6},{4,1},{5,0},{6,3},{7,2},{8,13},{9,12},{10,... | collective-permute-start | bytes 294920 | tf_op jit(solution)/shard_map/ppermute | solution.py:304
  244.5 16.6 %collective-permute-start.11 = (bf16[1,192,256]{2,1,0:T(8,128)(2,1)}, bf16[1,192,256]{2,1,0:T(8,128)(2,1)}, u32[]{:S(2)}, u32[]{:S(2)}) collective-permute-start(bf16[1,192,256]{2,1,0:T(8,128)(2,1)} %get-tuple-element.43), channel_id=1, source_target_pairs={{0,6},{1,7},{2,4},{3,5},{4,2},{5,3},{6,0},{7,1},{8,14},{9,15},{10,... | collective-permute-start | bytes 294920 | tf_op jit(solution)/shard_map/ppermute | solution.py:304
  246.4 14.8 %collective-permute-start.12 = (bf16[1,192,256]{2,1,0:T(8,128)(2,1)}, bf16[1,192,256]{2,1,0:T(8,128)(2,1)}, u32[]{:S(2)}, u32[]{:S(2)}) collective-permute-start(bf16[1,192,256]{2,1,0:T(8,128)(2,1)} %get-tuple-element.44), channel_id=1, source_target_pairs={{0,7},{1,6},{2,5},{3,4},{4,3},{5,2},{6,1},{7,0},{8,15},{9,14},{10,... | collective-permute-start | bytes 294920 | tf_op jit(solution)/shard_map/ppermute | solution.py:304
